TPU v7x, 8 devices: a whole 2x2x1 slice. The times are simulated.
8 devices in a mesh: data: 2 (over z, y), dap: 4 (over x, core).
Axes of the slice: x: 2, y: 2, z: 1, core: 2. Of those that a mesh axis runs over, the one named last changes fastest.
Arguments:
- pair_z: float32 [24, 256, 256, 64], P('data', 'dap'), parts along dimension 0
- pair_mask: int32 [24, 256, 256], P('data', 'dap'), parts along dimension 0
- out_norm_gain: float32 [64], replicated
- out_norm_bias: float32 [64], replicated
- out_w_a: bfloat16 [64, 64], replicated
- out_w_agate: bfloat16 [64, 64], replicated
- out_w_b: bfloat16 [64, 64], replicated
- out_w_bgate: bfloat16 [64, 64], replicated
- out_w_gate: bfloat16 [64, 64], replicated
- out_x_gain: float32 [64], replicated
- out_x_bias: float32 [64], replicated
- out_w_proj: bfloat16 [64, 64], replicated
- in_norm_gain: float32 [64], replicated
- in_norm_bias: float32 [64], replicated
- in_w_a: bfloat16 [64, 64], replicated
- in_w_agate: bfloat16 [64, 64], replicated
- in_w_b: bfloat16 [64, 64], replicated
- in_w_bgate: bfloat16 [64, 64], replicated
- in_w_gate: bfloat16 [64, 64], replicated
- in_x_gain: float32 [64], replicated
- in_x_bias: float32 [64], replicated
- in_w_proj: bfloat16 [64, 64], replicated
- att_norm_gain: float32 [64], replicated
- att_norm_bias: float32 [64], replicated
- att_w_q: bfloat16 [64, 64], replicated
- att_w_k: bfloat16 [64, 64], replicated
- att_w_v: bfloat16 [64, 64], replicated
- att_w_bias: bfloat16 [64, 4], replicated
- att_w_gate: bfloat16 [64, 64], replicated
- att_w_proj: bfloat16 [64, 64], replicated
Outputs:
- output: float32 [24, 256, 256, 64], P('data', 'dap'), parts along dimension 0
There are 2 independent parts. A program takes and returns all parts, laid end to end along the dimension named above; an argument that names none is the same for every part.
All inputs are finite; a program needn't handle non-finite values.
Results may differ from a plain program's by a relative error of at most 0.00913572.
Values are sent between devices in bfloat16 or wider.
A program may use at most 1 GiB of HBM per device.

v0:
```python
import jax
import jax.numpy as jnp
from jax import lax
from jax.experimental import pallas as pl
from jax.experimental.pallas import tpu as pltpu
from jax.sharding import PartitionSpec as P


LN_EPS = 1e-5
F32, BF16 = jnp.float32, jnp.bfloat16
ROWS, CH, COLS = 64, 64, 256
TILE = 16


def channel_norm(vals, gain, shift, axis_id):
    ch_mean = jnp.mean(vals, axis=axis_id, keepdims=True)
    ch_var = jnp.mean(jnp.square(vals - ch_mean), axis=axis_id, keepdims=True)
    return (vals - ch_mean) * lax.rsqrt(ch_var + LN_EPS) * gain + shift


def sigmoid(vals):
    return 0.5 * jnp.tanh(0.5 * vals) + 0.5


def mm(lhs, rhs):
    return jnp.dot(lhs, rhs, preferred_element_type=F32)


def masked_norm(z_row, m_row, norm):
    return (m_row * channel_norm(z_row, norm[0], norm[1], 0)).astype(BF16)


def ab_row(proj, tile_a, tile_b, slot):
    tile_a[slot] = ((jnp.tanh(proj[CH:2 * CH]) + 1.0) * proj[:CH]).astype(BF16)
    tile_b[slot] = ((jnp.tanh(proj[3 * CH:]) + 1.0) * proj[2 * CH:3 * CH]).astype(BF16)


def x_norm_tile(x_s, tile_x, base, xg, xb):
    parts = [(sub, half) for sub in range(2) for half in range(2)]

    def load(c, part):
        return x_s[c, pl.ds(pl.multiple_of(base + 8 * part[0], 8), 8), 128 * part[1]:128 * part[1] + 128]

    means = [sum(load(c, p) for c in range(CH)) * (1.0 / CH) for p in parts]
    scales = [lax.rsqrt(sum(jnp.square(load(c, p) - means[n]) for c in range(CH)) * (1.0 / CH) + LN_EPS)
              for n, p in enumerate(parts)]
    for c in range(CH):
        rows = []
        for sub in range(2):
            rows.append(jnp.concatenate(
                [(load(c, (sub, half)) - means[2 * sub + half]) * scales[2 * sub + half] * xg[c] + xb[c]
                 for half in range(2)], axis=1))
        tile_x[c] = jnp.concatenate(rows, axis=0).astype(BF16)


LAG = 3


def staggered(count, *stages):
    held = [{} for _ in stages]
    for tick in range(count + LAG * (len(stages) - 1)):
        for k, stage in enumerate(stages):
            i = tick - LAG * k
            if 0 <= i < count:
                held[k][i] = stage(i, held[k - 1].pop(i) if k else None)


def u_kernel(sc, zt, zr1, zr2, zr3, mask0, mask1, mask2, mask3, norms, xgs, w_ab, w_sq, w_bias,
             z2_own, z2_par, bias_out, xo2, xo3, xi2, xi3,
             z_s, a_s, b_s, x_s, mask, tile_a, tile_b, tile_x, tile_c, tile_d, tile_z, in_sem, z_sem, x_sem):
    me, sample = sc[0], sc[1]
    srcs = (zt.at[sample], zr1, zr2, zr3)
    lanes = pl.ds(pl.multiple_of(128 * (me // 2), 128), 128)
    out_norm = (norms[0], norms[1])
    in_norm = (norms[2], norms[3])
    att_norm = (norms[4], norms[5])
    n_tiles = COLS // TILE

    def z_copy(r):
        start = pl.multiple_of(ROWS * (me ^ r), ROWS)
        return pltpu.make_async_copy(srcs[r], z_s.at[pl.ds(start, ROWS)], in_sem.at[r])

    for r in range(4):
        z_copy(r).start()
    for r, part in enumerate((mask0, mask1, mask2, mask3)):
        mask[pl.ds(pl.multiple_of(ROWS * (me ^ r), ROWS), ROWS), :] = part[...].astype(F32)

    def flush(base):
        a_s[:, pl.ds(base, TILE), :] = jnp.swapaxes(tile_a[...], 0, 1)
        b_s[:, pl.ds(base, TILE), :] = jnp.swapaxes(tile_b[...], 0, 1)

    def part_of(t):
        return (t * TILE // ROWS) ^ me, pl.ds(pl.multiple_of(t * TILE % ROWS, TILE), TILE)

    def export(t, start, own, par, far2, far3, sem):
        r, rows = part_of(t)
        act = (lambda cp: cp.start()) if start else (lambda cp: cp.wait())
        src = tile_c.at[t % 2] if far2.shape[-1] == COLS else tile_c.at[t % 2, :, :, lanes]
        for k, dst in ((0, own), (1, par), (2, far2), (3, far3)):
            if dst is not None:
                @pl.when(r == k)
                def _():
                    act(pltpu.make_async_copy(tile_z.at[t % 2] if k < 2 else src, dst.at[rows], sem.at[t % 2]))

    @pl.loop(0, n_tiles)
    def _(v):
        r = v * TILE // ROWS

        @pl.when(v * TILE % ROWS == 0)
        def _():
            pltpu.make_async_copy(zr1, z_s.at[pl.ds(0, ROWS)], in_sem.at[r]).wait()

        base = pl.multiple_of(ROWS * (me ^ r) + v * TILE % ROWS, TILE)
        staggered(
            TILE,
            lambda i, _: mm(w_ab[0], masked_norm(z_s[base + i], mask[pl.ds(base + i, 1), :], out_norm)),
            lambda i, proj: ab_row(proj, tile_a, tile_b, i))
        flush(base)

    @pl.loop(0, CH, unroll=4)
    def _(c):
        x_s[c] = lax.dot_general(a_s[c], b_s[c], (((1,), (1,)), ((), ())), preferred_element_type=F32)

    @pl.loop(0, n_tiles)
    def _(t):
        base = pl.multiple_of(TILE * t, TILE)

        @pl.when(t >= 2)
        def _():
            export(t - 2, False, None, None, xo2, xo3, x_sem)

        x_norm_tile(x_s, tile_x, base, xgs.at[0], xgs.at[1])
        tile_c[t % 2] = jnp.swapaxes(tile_x[...], 0, 1)

        def gate_and_update(i, _):
            normed = channel_norm(z_s[base + i], out_norm[0], out_norm[1], 0).astype(BF16)
            return mm(w_sq[0], normed), mm(w_sq[1], tile_c[t % 2, i])

        def next_norm(i, parts):
            z_one = z_s[base + i] + (jnp.tanh(parts[0]) + 1.0) * parts[1]
            tile_z[0, i] = z_one
            return masked_norm(z_one, mask[pl.ds(base + i, 1), :], in_norm)

        staggered(TILE, gate_and_update, next_norm, lambda i, normed: mm(w_ab[1], normed),
                  lambda i, proj: ab_row(proj, tile_a, tile_b, i))
        flush(base)
        z_s[pl.ds(base, TILE)] = tile_z[0]
        export(t, True, None, None, xo2, xo3, x_sem)

    for t in (n_tiles - 2, n_tiles - 1):
        export(t, False, None, None, xo2, xo3, x_sem)

    @pl.loop(0, CH, unroll=4)
    def _(c):
        x_s[c] = lax.dot_general(a_s[c], b_s[c], (((0,), (0,)), ((), ())), preferred_element_type=F32)

    @pl.loop(0, n_tiles)
    def _(t):
        base = pl.multiple_of(TILE * t, TILE)

        @pl.when(t >= 2)
        def _():
            export(t - 2, False, z2_own, z2_par, xi2, xi3, z_sem)

        x_norm_tile(x_s, tile_x, base, xgs.at[2], xgs.at[3])
        tile_c[t % 2] = jnp.swapaxes(tile_x[...], 0, 1)

        def gate_and_update(i, _):
            normed = channel_norm(z_s[base + i], in_norm[0], in_norm[1], 0).astype(BF16)
            return mm(w_sq[2], normed), mm(w_sq[3], tile_c[t % 2, i])

        def next_norm(i, parts):
            z_two = z_s[base + i] + (jnp.tanh(parts[0]) + 1.0) * parts[1]
            tile_z[t % 2, i] = z_two
            return channel_norm(z_two, att_norm[0], att_norm[1], 0).astype(BF16)

        def bias_row(i, normed):
            tile_d[i] = mm(w_bias[...], normed)

        staggered(TILE, gate_and_update, next_norm, bias_row)
        rows = pl.ds(pl.multiple_of(t * TILE % ROWS, TILE), TILE)
        bias_out[t * TILE // ROWS, :, rows, :] = jnp.swapaxes(tile_d[...], 0, 1)[:4].astype(BF16)
        export(t, True, z2_own, z2_par, xi2, xi3, z_sem)

    for t in (n_tiles - 2, n_tiles - 1):
        export(t, False, z2_own, z2_par, xi2, xi3, z_sem)


LANES = 128
VM = pl.BlockSpec(memory_space=pltpu.VMEM)
HB = pl.BlockSpec(memory_space=pl.ANY)
SM = pl.BlockSpec(memory_space=pltpu.SMEM)
PARAMS = pltpu.CompilerParams(vmem_limit_bytes=40 << 20, dimension_semantics=("arbitrary",))
AB_TILE = pltpu.VMEM((TILE, CH, COLS), BF16)
DMA2 = pltpu.SemaphoreType.DMA((2,))
ROW_HALF = jax.ShapeDtypeStruct((ROWS, CH, LANES), BF16)
ROW_FULL = jax.ShapeDtypeStruct((ROWS, CH, COLS), BF16)
ROW_WIDE = jax.ShapeDtypeStruct((ROWS, CH, COLS), F32)
SAMPLE_BF = pltpu.VMEM((CH, COLS, COLS), BF16)


def u_call(sc, zt, zr, masks, norms, xgs, w_ab, w_sq, w_bias):
    return pl.pallas_call(
        u_kernel,
        out_shape=(ROW_WIDE, ROW_WIDE, jax.ShapeDtypeStruct((4, 4, ROWS, COLS), BF16), ROW_HALF, ROW_HALF, ROW_FULL, ROW_FULL),
        in_specs=[SM] + [HB] * 4 + [VM] * 9,
        out_specs=(HB, HB, VM, HB, HB, HB, HB),
        scratch_shapes=[
            pltpu.VMEM((COLS, CH, COLS), F32), SAMPLE_BF, SAMPLE_BF,
            pltpu.VMEM((CH, COLS, COLS), F32), pltpu.VMEM((COLS, COLS), F32), AB_TILE, AB_TILE, pltpu.VMEM((CH, TILE, COLS), BF16), pltpu.VMEM((2, TILE, CH, COLS), BF16),
            pltpu.VMEM((TILE, 8, COLS), F32), pltpu.VMEM((2, TILE, CH, COLS), F32),
            pltpu.SemaphoreType.DMA((4,)), DMA2, DMA2,
        ],
        compiler_params=pltpu.CompilerParams(vmem_limit_bytes=62 << 20),
        name="pair_updates",
    )(sc, zt, *zr, *masks, norms, xgs, w_ab, w_sq, w_bias)


def l1_kernel(ids, z_in, mask_in, norms, w_ab, a_out, b_out, mask, tile_a, tile_b):
    out_norm = (norms[0], norms[1])
    mask[...] = mask_in[0].astype(F32)

    @pl.loop(0, ROWS // TILE)
    def _(t):
        base = pl.multiple_of(TILE * t, TILE)
        staggered(
            TILE,
            lambda i, _: mm(w_ab[0], masked_norm(z_in[0, base + i], mask[pl.ds(base + i, 1), :], out_norm)),
            lambda i, proj: ab_row(proj, tile_a, tile_b, i))
        a_out[0, :, pl.ds(base, TILE), :] = jnp.swapaxes(tile_a[...], 0, 1)
        b_out[0, :, pl.ds(base, TILE), :] = jnp.swapaxes(tile_b[...], 0, 1)


def l1_call(ids, zt, mask, norms, w_ab):
    n = ids.shape[0]
    ab = jax.ShapeDtypeStruct((n, CH, ROWS, COLS), BF16)
    ab_spec = pl.BlockSpec((1, CH, ROWS, COLS), lambda i, ids: (i, 0, 0, 0))
    return pl.pallas_call(
        l1_kernel,
        out_shape=(ab, ab),
        grid_spec=pltpu.PrefetchScalarGridSpec(
            num_scalar_prefetch=1, grid=(n,),
            in_specs=[pl.BlockSpec((1, ROWS, CH, COLS), lambda i, ids: (ids[i], 0, 0, 0)),
                      pl.BlockSpec((1, ROWS, COLS), lambda i, ids: (ids[i], 0, 0)), VM, VM],
            out_specs=(ab_spec, ab_spec),
            scratch_shapes=[pltpu.VMEM((ROWS, COLS), F32), AB_TILE, AB_TILE]),
        compiler_params=PARAMS,
        name="near_projections",
    )(ids, zt, mask, norms, w_ab)


def l2_kernel(sc, a_in, b_own, b_par, xgs, x_out, x_s, tile_x):
    odd = sc[0] % 2 == 1

    @pl.loop(0, CH, unroll=2)
    def _(c):
        for n in range(2):
            own, par = b_own[n, c].astype(F32), b_par[1 - n, c].astype(F32)
            pair = jnp.concatenate([jnp.where(odd, par, own), jnp.where(odd, own, par)], axis=0).astype(BF16)
            x_s[c, :, LANES * n:LANES * n + LANES] = lax.dot_general(
                a_in[n, c], pair, (((1,), (1,)), ((), ())), preferred_element_type=F32)

    @pl.loop(0, ROWS // TILE)
    def _(t):
        base = pl.multiple_of(TILE * t, TILE)
        x_norm_tile(x_s, tile_x, base, xgs.at[0], xgs.at[1])
        both = jnp.swapaxes(tile_x[...], 0, 1)
        for n in range(2):
            x_out[n, pl.ds(base, TILE)] = both[:, :, LANES * n:LANES * n + LANES]


def l2_call(sc, a_all, b_own, b_par, xgs):
    n = a_all.shape[0]
    ab_spec = pl.BlockSpec((2, CH, ROWS, COLS), lambda i: (i, 0, 0, 0))
    return pl.pallas_call(
        l2_kernel,
        grid=(n // 2,),
        out_shape=jax.ShapeDtypeStruct((n, ROWS, CH, LANES), BF16),
        in_specs=[SM, ab_spec, ab_spec, ab_spec, VM],
        out_specs=pl.BlockSpec((2, ROWS, CH, LANES), lambda i: (i, 0, 0, 0)),
        scratch_shapes=[pltpu.VMEM((CH, ROWS, COLS), F32), pltpu.VMEM((CH, TILE, COLS), BF16)],
        compiler_params=PARAMS,
        name="near_product",
    )(sc, a_all, b_own, b_par, xgs)


def r_kernel(sc, z_in, x_near, x_far, xi, norms, w_sq, w_bias, z_out, bias_out, tile_d):
    first = sc[0] < 2
    out_norm = (norms[0], norms[1])
    in_norm = (norms[2], norms[3])
    att_norm = (norms[4], norms[5])

    def outgoing(i, _):
        near, far = x_near[0, i].astype(F32), x_far[i].astype(F32)
        xn = jnp.concatenate([jnp.where(first, near, far), jnp.where(first, far, near)], axis=1).astype(BF16)
        normed = channel_norm(z_in[0, i], out_norm[0], out_norm[1], 0).astype(BF16)
        return mm(w_sq[0], normed), mm(w_sq[1], xn)

    def norm_one(i, parts):
        z_one = z_in[0, i] + (jnp.tanh(parts[0]) + 1.0) * parts[1]
        z_out[i] = z_one
        return channel_norm(z_one, in_norm[0], in_norm[1], 0).astype(BF16)

    def incoming(i, normed):
        return mm(w_sq[2], normed), mm(w_sq[3], xi[i])

    def norm_two(i, parts):
        z_two = z_out[i] + (jnp.tanh(parts[0]) + 1.0) * parts[1]
        z_out[i] = z_two
        return channel_norm(z_two, att_norm[0], att_norm[1], 0).astype(BF16)

    def bias_row(i, normed):
        tile_d[i] = mm(w_bias[...], normed)

    staggered(TILE, outgoing, norm_one, incoming, norm_two, bias_row)
    bias_out[...] = jnp.swapaxes(tile_d[...], 0, 1)[:4].astype(BF16)


def r_call(sc, zt, x_near, x_far, xi, norms, w_sq, w_bias):
    return pl.pallas_call(
        r_kernel,
        out_shape=(ROW_WIDE, jax.ShapeDtypeStruct((4, ROWS, COLS), BF16)),
        grid_spec=pltpu.PrefetchScalarGridSpec(
            num_scalar_prefetch=1, grid=(ROWS // TILE,),
            in_specs=[pl.BlockSpec((1, TILE, CH, COLS), lambda i, sc: (sc[1], i, 0, 0)),
                      pl.BlockSpec((1, TILE, CH, 128), lambda i, sc: (sc[2], i, 0, 0)),
                      pl.BlockSpec((TILE, CH, 128), lambda i, sc: (i, 0, 0)),
                      pl.BlockSpec((TILE, CH, COLS), lambda i, sc: (i, 0, 0)), VM, VM, VM],
            out_specs=(pl.BlockSpec((TILE, CH, COLS), lambda i, sc: (i, 0, 0)),
                       pl.BlockSpec((4, TILE, COLS), lambda i, sc: (0, i, 0))),
            scratch_shapes=[pltpu.VMEM((TILE, 8, COLS), F32)]),
        compiler_params=PARAMS,
        name="row_updates",
    )(sc, zt, x_near, x_far, xi, norms, w_sq, w_bias)


HEADS, HEAD = 4, 16
MASK_FILL = -1e9
CHUNK = 32
SLOTS = 2


def a_kernel(sc, z_in, mask_in, bias, norms, w_all, w_proj, out_in, out_ref, mask, bias_rows, bias_t, q_s, k_s, v_s, g_s, vn_s, gn_s, keep_s, s_buf, e_buf, p_s, top_s, inv_s, o_s):
    z_out = out_ref.at[0]
    mask[...] = mask_in[0].astype(F32)
    for r in range(4):
        bias_rows[:, pl.ds(pl.multiple_of(ROWS * (sc[1] ^ r), ROWS), ROWS), :] = bias[r].astype(F32)
    for h in range(HEADS):
        bias_t[h] = bias_rows[h].T
    n_rows = z_in.shape[0]

    def project(row, slot):
        row = jnp.clip(row, 0, n_rows - 1)
        normed = channel_norm(z_in[row], norms[0], norms[1], 0).astype(BF16)
        proj = mm(w_all[...], normed)
        k_s[slot] = proj[CH:2 * CH].T.astype(BF16)
        q = proj[:CH].astype(BF16)
        for h in range(HEADS):
            q_s[slot, h, HEAD * h:HEAD * h + HEAD] = q[HEAD * h:HEAD * h + HEAD]
        vn_s[slot] = proj[2 * CH:3 * CH].astype(BF16)
        gn_s[slot] = sigmoid(proj[3 * CH:])

    def keep_mask(row, slot):
        row = jnp.clip(row, 0, n_rows - 1)
        keep_s[slot] = jnp.broadcast_to(mask[pl.ds(row, 1), :], (128, COLS)).T

    def fold(part, op):
        out = part[:8]
        for n in range(1, part.shape[0] // 8):
            out = op(out, part[8 * n:8 * n + 8])
        return out

    def scores(slot, h):
        return mm(k_s[slot], q_s[slot, h])

    def weigh(slot, h, probs):
        heads = slice(HEAD * h, HEAD * h + HEAD)
        o_s[slot, heads] = mm(v_s[slot, heads], probs)

    def step(slot, h, logits, defer=False):
        buf, prev = h % 2, (h + 1) % 2
        top, total, probs = None, None, []
        for c in range(COLS // CHUNK):
            rows = slice(CHUNK * c, CHUNK * c + CHUNK)
            scale = (e_buf[buf, rows] * jnp.concatenate([inv_s[buf]] * (CHUNK // 8), axis=0)).astype(BF16)
            probs.append(scale)
            exps = jnp.exp(s_buf[prev, rows] - jnp.concatenate([top_s[prev]] * (CHUNK // 8), axis=0))
            e_buf[prev, rows] = exps
            part = fold(exps, jnp.add)
            total = part if total is None else total + part
            keep = keep_s[slot, rows]
            keep = jnp.concatenate([keep, keep], axis=1) > 0
            vals = jnp.where(keep, logits[rows] + bias_t[h, rows], MASK_FILL)
            s_buf[buf, rows] = vals
            part = fold(vals, jnp.maximum)
            top = part if top is None else jnp.maximum(top, part)
        top_s[buf] = jnp.broadcast_to(jnp.max(top, axis=0, keepdims=True), (8, COLS))
        inv_s[prev] = jnp.broadcast_to(1.0 / jnp.sum(total, axis=0, keepdims=True), (8, COLS))
        if defer:
            p_s[...] = jnp.concatenate(probs, axis=0)
        else:
            weigh(1 - slot if h < 2 else slot, (h - 2) % HEADS, jnp.concatenate(probs, axis=0))

    def finish(row, slot):
        row = jnp.clip(row, 0, n_rows - 1)
        gated = (g_s[slot] * o_s[slot]).astype(BF16)
        z_out[row] = z_in[row] + mm(w_proj[...], gated)

    q_s[...] = jnp.zeros_like(q_s)
    project(0, 0)
    keep_mask(0, 0)

    @pl.loop(0, n_rows // 2 + 1)
    def _(pair):
        first = 2 * pair - 1
        lg = scores(1, 0)
        weigh(0, 1, p_s[...])
        for slot in (1, 0):
            row = first + 1 - slot
            for h in range(HEADS):
                nxt = scores(slot, h + 1) if h < HEADS - 1 else (scores(0, 0) if slot else None)
                if h == 2:
                    project(row + 2, slot)
                step(slot, h, lg, defer=slot == 0 and h == 3)
                lg = nxt
                if h == 2:
                    finish(row - 1, 1 - slot)
                    v_s[1 - slot] = vn_s[1 - slot]
                    g_s[1 - slot] = gn_s[1 - slot]
            keep_mask(row + 2, slot)


def a_call(sc, z_in, mask, bias, norms, w_all, w_proj, out):
    full = lambda a: pl.BlockSpec(a.shape, lambda i, sc: (0,) * a.ndim)
    fresh = out is None
    call = pl.pallas_call(
        a_first if fresh else a_kernel,
        out_shape=jax.ShapeDtypeStruct((mask.shape[0], ROWS, CH, COLS), F32),
        grid_spec=pltpu.PrefetchScalarGridSpec(
            num_scalar_prefetch=1, grid=(1,),
            in_specs=[full(z_in), pl.BlockSpec((1, ROWS, COLS), lambda i, sc: (sc[0], 0, 0)),
                      full(bias), full(norms), full(w_all), full(w_proj)] + ([] if fresh else [HB]),
            out_specs=pl.BlockSpec((1, ROWS, CH, COLS), lambda i, sc: (sc[0], 0, 0, 0)),
            scratch_shapes=[
                pltpu.VMEM((ROWS, COLS), F32), pltpu.VMEM((HEADS, COLS, COLS), F32), pltpu.VMEM((HEADS, COLS, COLS), F32),
                pltpu.VMEM((SLOTS, HEADS, CH, COLS), BF16), pltpu.VMEM((SLOTS, COLS, CH), BF16),
                pltpu.VMEM((SLOTS, CH, COLS), BF16), pltpu.VMEM((SLOTS, CH, COLS), F32), pltpu.VMEM((SLOTS, CH, COLS), BF16),
                pltpu.VMEM((SLOTS, CH, COLS), F32), pltpu.VMEM((SLOTS, COLS, 128), F32), pltpu.VMEM((2, COLS, COLS), F32),
                pltpu.VMEM((2, COLS, COLS), F32), pltpu.VMEM((COLS, COLS), BF16), pltpu.VMEM((2, 8, COLS), F32),
                pltpu.VMEM((2, 8, COLS), F32), pltpu.VMEM((SLOTS, CH, COLS), F32),
            ]),
        compiler_params=pltpu.CompilerParams(vmem_limit_bytes=48 << 20, dimension_semantics=("arbitrary",)),
        input_output_aliases={} if fresh else {7: 0},
        name="triangle_attention",
    )
    args = (sc, z_in, mask, bias, norms, w_all, w_proj)
    return call(*args) if fresh else call(*args, out)


def a_first(sc, z_in, mask_in, bias, norms, w_all, w_proj, out_ref, *scratch):
    a_kernel(sc, z_in, mask_in, bias, norms, w_all, w_proj, None, out_ref, *scratch)


def exchange(values, r):
    return lax.ppermute(values, 'dap', [(i, i ^ r) for i in range(4)])


def update_weights(params):
    norm_gain, norm_bias, w_a, w_agate, w_b, w_bgate, w_gate, x_gain, x_bias, w_proj = params
    half = jnp.bfloat16(0.5)
    wide = lambda v: jnp.broadcast_to(v[:, None], (CH, COLS))
    deep = lambda v: jnp.broadcast_to(v[:, None, None], (CH, 8, 128))
    return ([wide(norm_gain), wide(norm_bias)], [deep(x_gain), deep(x_bias)],
            half * jnp.concatenate([w_a.T, w_agate.T, w_b.T, w_bgate.T], axis=0), [half * w_gate.T, half * w_proj.T])


def solution(mesh):
    def local_block(pair_z, pair_mask, *weights):
        me = lax.axis_index('dap')
        zt = jnp.transpose(pair_z, (0, 1, 3, 2))
        n_own = zt.shape[0] // 4
        mask_bf = pair_mask.astype(BF16)
        masks = [lax.dynamic_slice_in_dim(mask_bf, n_own * (me ^ r), n_own, axis=0) for r in range(4)]
        arrived, zt_t = [], zt
        for t in range(n_own):
            sends = [lax.dynamic_index_in_dim(zt_t, n_own * (me ^ r) + t, 0, keepdims=False) for r in (2, 3, 1)]
            *sends, zt_t = lax.optimization_barrier((*sends, zt))
            if t == 0:
                weights, masks = lax.optimization_barrier((weights, masks, sends[0]))[:2]
            got = [exchange(v, r) for v, r in zip(sends, (2, 3, 1))]
            arrived.append((got[2], got[0], got[1]))
        masks = [exchange(m, r) if r else m for r, m in enumerate(masks)]

        out_n, out_x, out_ab, out_sq = update_weights(weights[:10])
        in_n, in_x, in_ab, in_sq = update_weights(weights[10:20])
        att_gain, att_shift, w_q, w_k, w_v, w_bias, w_gate, w_proj = weights[20:]
        att_n = [jnp.broadcast_to(v[:, None], (CH, COLS)) for v in (att_gain, att_shift)]
        norms = jnp.stack(out_n + in_n + att_n)
        xgs = jnp.stack(out_x + in_x)
        w_ab = jnp.stack([out_ab, in_ab])
        w_sq = jnp.stack(out_sq + in_sq)
        w_bias8 = jnp.concatenate([w_bias.T, jnp.zeros((4, CH), BF16)], axis=0)
        w_all = jnp.concatenate([w_q.T * jnp.bfloat16(HEAD ** -0.5), w_k.T, w_v.T, w_gate.T], axis=0)
        w_out = w_proj.T
        att_norms = norms[4:]

        token = [None]

        def ordered(call, sc, *args):
            sc = jnp.stack([jnp.asarray(v, jnp.int32) for v in sc])
            if token[0] is not None:
                sc = lax.optimization_barrier((sc, token[0]))[0]
            res = call(sc, *args)
            token[0] = jax.tree.leaves(res)[-1]
            return res

        far = [(t, r) for t in range(n_own) for r in (2, 3)]
        a_far, b_far = ordered(l1_call, [n_own * (me ^ r) + t for t, r in far], zt, pair_mask, norms, w_ab)
        b_par = exchange(b_far, 1)
        x_near = ordered(l2_call, [me], a_far, b_far, b_par, xgs)

        out = None
        held = []
        for t in range(n_own):
            z_own, z_par, bias, *far_x = ordered(u_call, [me, n_own * me + t], zt, arrived[t], [m[t] for m in masks],
                                                 norms, xgs, w_ab, w_sq, w_bias8)
            got = {}
            bias_blk = {2: lax.dynamic_index_in_dim(bias, me, 0, keepdims=False),
                        3: lax.dynamic_index_in_dim(bias, me ^ 1, 0, keepdims=False)}
            z_near, bias_near = exchange(z_par, 1), exchange(bias, 1)
            for r in (2, 3):
                got[r] = [exchange(v, r) for v in (bias_blk[r], far_x[r - 2], far_x[r])]
            held.append(got)
            out = ordered(a_call, [n_own * me + t, 0], z_own, pair_mask, bias, att_norms, w_all, w_out, out)
            out = ordered(a_call, [n_own * (me ^ 1) + t, 0], z_near, pair_mask, bias_near, att_norms, w_all, w_out, out)
        for t in range(n_own):
            mine, z_two = {}, {}
            for r in (2, 3):
                bias_far, x_far, xi = held[t][r]
                z_two[r], bias_own = ordered(r_call, [me, n_own * (me ^ r) + t, far.index((t, r))], zt, x_near, x_far, xi,
                                             norms, w_sq, w_bias8)
                mine[r] = (bias_own, bias_far)
            both = jnp.stack([*mine[3], *mine[2]])
            par = exchange(both, 1)
            for r in (2, 3):
                bias = jnp.stack([mine[r][0], par[2 * r - 4], mine[r][1], par[2 * r - 3]])
                out = ordered(a_call, [n_own * (me ^ r) + t, me], z_two[r], pair_mask, bias, att_norms, w_all, w_out, out)
        return jnp.transpose(out, (0, 1, 3, 2))

    pair_spec = P('data', 'dap')
    return jax.shard_map(local_block, mesh=mesh, in_specs=(pair_spec, pair_spec) + (P(),) * 28,
                         out_specs=pair_spec, check_vma=False)
```

profile of v0, /device:TPU:0, one launch (start us, length us, event | category | flops | bytes accessed | tf_op | source)
XLA Modules:
  0.0 1495.6 jit_solution(3009527960890176995)
XLA Ops:
  0.1 9.8 dynamic-slice_bitcast_fusion.6
  11.6 28.7 %near_projections.1 = (bf16[6,64,64,256]{3,2,1,0:T(8,128)(2,1)S(1)}, bf16[6,64,64,256]{3,2,1,0:T(8,128)(2,1)}) custom-call(s32[6]{0:T(128)S(1)} %stack.272.ids, f32[12,64,64,256]{3,2,1,0:T(8,128)} %bitcast.160, s32[12,64,256]{2,1,0:T(8,128)S(1)} %copy-done.1, f32[6,64,256]{2,1,0:T(8,128)S(1)} %broadcast_dynamic-update-slice_fusion.norms, ...), custom_call_target="tpu_custom_call" | custom-call | tf_op jit(solution)/shard_map/near_projections/pallas_call | solution.py:238
  40.3 4.6 copy-done.5
  45.7 2.5 collective-permute-start.2
  48.4 1.7 collective-permute-start.6
  51.2 9.7 dynamic-slice_bitcast_fusion.3
  63.5 168.0 %collective-permute-done.6 = bf16[3,64,256]{2,1,0:T(8,128)(2,1)S(1)} collective-permute-done((bf16[3,64,256]{2,1,0:T(8,128)(2,1)S(1)}, bf16[3,64,256]{2,1,0:T(8,128)(2,1)S(1)}, u32[]{:S(2)}, u32[]{:S(2)}) %collective-permute-start.6) | collective-permute-done | bytes 98336 | tf_op jit(solution)/shard_map/ppermute | solution.py:465
  231.5 1.5 collective-permute-start.5
  233.6 2.7 collective-permute-done.5
  238.2 32.9 %near_product.1.x_near = bf16[6,64,64,128]{3,2,1,0:T(8,128)(2,1)S(1)} custom-call(s32[1]{0:T(128)} %bitcast.1.sc, bf16[6,64,64,256]{3,2,1,0:T(8,128)(2,1)} %copy-done.5, bf16[6,64,64,256]{3,2,1,0:T(8,128)(2,1)} %get-tuple-element.120.b_own, bf16[6,64,64,256]{3,2,1,0:T(8,128)(2,1)} %collective-permute-done.b_par, f32[4,64,8,128]{3,2,1,0:T(8,128)S(1)} %pad_maximum_fusion.xgs), custom_call_target="tpu_custom_call" | custom-call | tf_op jit(solution)/shard_map/near_product/pallas_call | solution.py:275
  271.1 2.6 copy-done
  273.8 94.9 %pair_updates.3 = (f32[64,64,256]{2,1,0:T(8,128)}, f32[64,64,256]{2,1,0:T(8,128)}, bf16[4,4,64,256]{3,2,1,0:T(8,128)(2,1)}, bf16[64,64,128]{2,1,0:T(8,128)(2,1)}...) custom-call(s32[2]{0:T(128)} %pad_add_fusion.20.sc, ...), custom_call_target="tpu_custom_call" | custom-call | tf_op jit(solution)/shard_map/pair_updates/pallas_call | solution.py:203
  371.5 9.8 dynamic-slice_bitcast_fusion
  382.3 34.1 %triangle_attention.12.out_in = f32[12,64,64,256]{3,2,1,0:T(8,128)} custom-call(s32[2]{0:T(128)S(1)} %pad_add_fusion.sc, f32[64,64,256]{2,1,0:T(8,128)S(1)} %copy-done.21, s32[12,64,256]{2,1,0:T(8,128)S(1)} %copy-done.1, bf16[4,4,64,256]{3,2,1,0:T(8,128)(2,1)S(1)} %copy-done.29, f32[2,64,256]{2,1,0:T(8,128)S(1)} %pad_maximum_fusion.11.norms, ...), custom_call_target="tpu_custom_call" | custom-call | tf_op jit(solution)/shard_map/triangle_attention/pallas_call | solution.py:457
  416.4 36.1 %triangle_attention.13.out_in = f32[12,64,64,256]{3,2,1,0:T(8,128)} custom-call(s32[2]{0:T(128)S(1)} %pad_add_fusion.1.sc, f32[64,64,256]{2,1,0:T(8,128)} %collective-permute-done.7.z_in, s32[12,64,256]{2,1,0:T(8,128)S(1)} %copy-done.1, bf16[4,4,64,256]{3,2,1,0:T(8,128)(2,1)S(1)} %collective-permute-done.8.bias, ...), custom_call_target="tpu_custom_call", output_to_operand_aliasing={{}: (7, {})} | custom-call | tf_op jit(solution)/shard_map/triangle_attention/pallas_call | solution.py:457
  452.6 10.0 collective-permute-done.10.zr2
  462.6 88.6 %collective-permute-done.11.zr3 = f32[64,64,256]{2,1,0:T(8,128)} collective-permute-done((f32[64,64,256]{2,1,0:T(8,128)}, f32[64,64,256]{2,1,0:T(8,128)}, u32[]{:S(2)}, u32[]{:S(2)}) %collective-permute-start.11) | collective-permute-done | bytes 4194336 | tf_op jit(solution)/shard_map/ppermute | solution.py:465
  551.2 94.8 %pair_updates.4 = (f32[64,64,256]{2,1,0:T(8,128)}, f32[64,64,256]{2,1,0:T(8,128)}, bf16[4,4,64,256]{3,2,1,0:T(8,128)(2,1)}, bf16[64,64,128]{2,1,0:T(8,128)(2,1)}...) custom-call(s32[2]{0:T(128)} %pad_add_fusion.19.sc, ...), custom_call_target="tpu_custom_call" | custom-call | tf_op jit(solution)/shard_map/pair_updates/pallas_call | solution.py:203
  649.5 2.2 copy-done.20
  652.7 34.0 %triangle_attention.14.out_in = f32[12,64,64,256]{3,2,1,0:T(8,128)} custom-call(s32[2]{0:T(128)S(1)} %pad_add_fusion.2.sc, f32[64,64,256]{2,1,0:T(8,128)S(1)} %copy-done.20, s32[12,64,256]{2,1,0:T(8,128)S(1)} %copy-done.1, bf16[4,4,64,256]{3,2,1,0:T(8,128)(2,1)S(1)} %copy-done.30, ...), custom_call_target="tpu_custom_call", output_to_operand_aliasing={{}: (7, {})} | custom-call | tf_op jit(solution)/shard_map/triangle_attention/pallas_call | solution.py:457
  686.7 36.1 %triangle_attention.15.out_in = f32[12,64,64,256]{3,2,1,0:T(8,128)} custom-call(s32[2]{0:T(128)S(1)} %pad_add_fusion.3.sc, f32[64,64,256]{2,1,0:T(8,128)} %collective-permute-done.12.z_in, s32[12,64,256]{2,1,0:T(8,128)S(1)} %copy-done.1, bf16[4,4,64,256]{3,2,1,0:T(8,128)(2,1)S(1)} %collective-permute-done.13.bias, ...), custom_call_target="tpu_custom_call", output_to_operand_aliasing={{}: (7, {})} | custom-call | tf_op jit(solution)/shard_map/triangle_attention/pallas_call | solution.py:457
  722.8 17.5 %collective-permute-done.15.zr2 = f32[64,64,256]{2,1,0:T(8,128)} collective-permute-done((f32[64,64,256]{2,1,0:T(8,128)}, f32[64,64,256]{2,1,0:T(8,128)}, u32[]{:S(2)}, u32[]{:S(2)}) %collective-permute-start.15) | collective-permute-done | bytes 4194336 | tf_op jit(solution)/shard_map/ppermute | solution.py:465
  740.4 88.9 %collective-permute-done.16.zr3 = f32[64,64,256]{2,1,0:T(8,128)} collective-permute-done((f32[64,64,256]{2,1,0:T(8,128)}, f32[64,64,256]{2,1,0:T(8,128)}, u32[]{:S(2)}, u32[]{:S(2)}) %collective-permute-start.16) | collective-permute-done | bytes 4194336 | tf_op jit(solution)/shard_map/ppermute | solution.py:465
  829.2 95.1 %pair_updates.5 = (f32[64,64,256]{2,1,0:T(8,128)}, f32[64,64,256]{2,1,0:T(8,128)}, bf16[4,4,64,256]{3,2,1,0:T(8,128)(2,1)}, bf16[64,64,128]{2,1,0:T(8,128)(2,1)}...) custom-call(s32[2]{0:T(128)} %pad_add_fusion.18.sc, ...), custom_call_target="tpu_custom_call" | custom-call | tf_op jit(solution)/shard_map/pair_updates/pallas_call | solution.py:203
  926.7 1.5 collective-permute-start.21
  928.1 112.6 %collective-permute-done.19.x_far = bf16[64,64,128]{2,1,0:T(8,128)(2,1)S(1)} collective-permute-done((bf16[64,64,128]{2,1,0:T(8,128)(2,1)}, bf16[64,64,128]{2,1,0:T(8,128)(2,1)S(1)}, u32[]{:S(2)}, u32[]{:S(2)}) %collective-permute-start.19) | collective-permute-done | bytes 1048608 | tf_op jit(solution)/shard_map/ppermute | solution.py:465
  1041.7 19.9 %collective-permute-done.21.x_far = bf16[64,64,128]{2,1,0:T(8,128)(2,1)S(1)} collective-permute-done((bf16[64,64,128]{2,1,0:T(8,128)(2,1)}, bf16[64,64,128]{2,1,0:T(8,128)(2,1)S(1)}, u32[]{:S(2)}, u32[]{:S(2)}) %collective-permute-start.21) | collective-permute-done | bytes 1048608 | tf_op jit(solution)/shard_map/ppermute | solution.py:465
  1063.1 1.4 copy-done.25
  1064.4 1.5 collective-permute-start.29
  1069.7 2.2 copy-done.7
  1072.9 34.0 %triangle_attention.16.out_in = f32[12,64,64,256]{3,2,1,0:T(8,128)} custom-call(s32[2]{0:T(128)S(1)} %pad_add_fusion.4.sc, f32[64,64,256]{2,1,0:T(8,128)S(1)} %copy-done.7, s32[12,64,256]{2,1,0:T(8,128)S(1)} %copy-done.1, bf16[4,4,64,256]{3,2,1,0:T(8,128)(2,1)S(1)} %copy-done.27, ...), custom_call_target="tpu_custom_call", output_to_operand_aliasing={{}: (7, {})} | custom-call | tf_op jit(solution)/shard_map/triangle_attention/pallas_call | solution.py:457
  1106.9 36.4 %triangle_attention.17.out_in = f32[12,64,64,256]{3,2,1,0:T(8,128)} custom-call(s32[2]{0:T(128)S(1)} %pad_add_fusion.5.sc, f32[64,64,256]{2,1,0:T(8,128)} %collective-permute-done.17.z_in, s32[12,64,256]{2,1,0:T(8,128)S(1)} %copy-done.1, bf16[4,4,64,256]{3,2,1,0:T(8,128)(2,1)S(1)} %collective-permute-done.18.bias, ...), custom_call_target="tpu_custom_call", output_to_operand_aliasing={{}: (7, {})} | custom-call | tf_op jit(solution)/shard_map/triangle_attention/pallas_call | solution.py:457
  1143.4 1.6 copy-done.26
  1145.0 8.9 row_updates.6
  1153.9 2.0 copy-done.10
  1155.9 8.6 row_updates.7
  1164.6 2.0 copy-done.8
  1166.6 14.2 collective-permute-done.23
  1180.8 3.2 collective-permute-done.24
  1186.8 22.2 %collective-permute-done.28.x_far = bf16[64,64,128]{2,1,0:T(8,128)(2,1)S(1)} collective-permute-done((bf16[64,64,128]{2,1,0:T(8,128)(2,1)S(1)}, bf16[64,64,128]{2,1,0:T(8,128)(2,1)S(1)}, u32[]{:S(2)}, u32[]{:S(2)}) %collective-permute-start.28) | collective-permute-done | bytes 1048608 | tf_op jit(solution)/shard_map/ppermute | solution.py:465
  1209.0 1.5 collective-permute-start.30
  1210.5 1.6 collective-permute-start.31
  1212.6 2.2 copy-done.11
  1214.8 34.4 %triangle_attention.18.out_in = f32[12,64,64,256]{3,2,1,0:T(8,128)} custom-call(s32[2]{0:T(128)S(1)} %pad_add_fusion.15.sc, f32[64,64,256]{2,1,0:T(8,128)S(1)} %copy-done.11, s32[12,64,256]{2,1,0:T(8,128)S(1)} %copy-done.1, bf16[4,4,64,256]{3,2,1,0:T(8,128)(2,1)S(1)} %pad_maximum_fusion.7.bias, ...), custom_call_target="tpu_custom_call", output_to_operand_aliasing={{}: (7, {})} | custom-call | tf_op jit(solution)/shard_map/triangle_attention/pallas_call | solution.py:457
  1249.2 2.2 copy-done.9
  1251.4 34.0 %triangle_attention.19.out_in = f32[12,64,64,256]{3,2,1,0:T(8,128)} custom-call(s32[2]{0:T(128)S(1)} %pad_add_fusion.14.sc, f32[64,64,256]{2,1,0:T(8,128)S(1)} %copy-done.9, s32[12,64,256]{2,1,0:T(8,128)S(1)} %copy-done.1, bf16[4,4,64,256]{3,2,1,0:T(8,128)(2,1)S(1)} %fusion.11.bias, ...), custom_call_target="tpu_custom_call", output_to_operand_aliasing={{}: (7, {})} | custom-call | tf_op jit(solution)/shard_map/triangle_attention/pallas_call | solution.py:457
  1285.3 8.9 row_updates.8
  1294.2 2.0 copy-done.14
  1296.2 8.8 row_updates.9
  1305.0 2.0 copy-done.12
  1307.1 1.8 collective-permute-start.32
  1310.9 17.5 %collective-permute-done.33.x_far = bf16[64,64,128]{2,1,0:T(8,128)(2,1)} collective-permute-done((bf16[64,64,128]{2,1,0:T(8,128)(2,1)}, bf16[64,64,128]{2,1,0:T(8,128)(2,1)}, u32[]{:S(2)}, u32[]{:S(2)}) %collective-permute-start.33) | collective-permute-done | bytes 1048608 | tf_op jit(solution)/shard_map/ppermute | solution.py:465
  1328.8 2.2 copy-done.15
  1331.0 34.0 %triangle_attention.20.out_in = f32[12,64,64,256]{3,2,1,0:T(8,128)} custom-call(s32[2]{0:T(128)S(1)} %pad_add_fusion.11.sc, f32[64,64,256]{2,1,0:T(8,128)S(1)} %copy-done.15, s32[12,64,256]{2,1,0:T(8,128)S(1)} %copy-done.1, bf16[4,4,64,256]{3,2,1,0:T(8,128)(2,1)S(1)} %pad_maximum_fusion.8.bias, ...), custom_call_target="tpu_custom_call", output_to_operand_aliasing={{}: (7, {})} | custom-call | tf_op jit(solution)/shard_map/triangle_attention/pallas_call | solution.py:457
  1365.0 2.2 copy-done.13
  1367.2 34.0 %triangle_attention.21.out_in = f32[12,64,64,256]{3,2,1,0:T(8,128)} custom-call(s32[2]{0:T(128)S(1)} %get-tuple-element.192.sc, f32[64,64,256]{2,1,0:T(8,128)S(1)} %copy-done.13, s32[12,64,256]{2,1,0:T(8,128)S(1)} %copy-done.1, bf16[4,4,64,256]{3,2,1,0:T(8,128)(2,1)S(1)} %fusion.7.bias, ...), custom_call_target="tpu_custom_call", output_to_operand_aliasing={{}: (7, {})} | custom-call | tf_op jit(solution)/shard_map/triangle_attention/pallas_call | solution.py:457
  1401.1 8.9 row_updates.10
  1410.0 2.0 copy-done.18
  1412.0 9.0 row_updates.11
  1421.1 2.0 copy-done.16
  1423.3 1.8 collective-permute-done.39
  1425.2 2.2 copy-done.19
  1427.4 34.0 %triangle_attention.22.out_in = f32[12,64,64,256]{3,2,1,0:T(8,128)} custom-call(s32[2]{0:T(128)S(1)} %pad_add_fusion.7.sc, f32[64,64,256]{2,1,0:T(8,128)S(1)} %copy-done.19, s32[12,64,256]{2,1,0:T(8,128)S(1)} %copy-done.1, bf16[4,4,64,256]{3,2,1,0:T(8,128)(2,1)S(1)} %pad_maximum_fusion.9.bias, ...), custom_call_target="tpu_custom_call", output_to_operand_aliasing={{}: (7, {})} | custom-call | tf_op jit(solution)/shard_map/triangle_attention/pallas_call | solution.py:457
  1461.5 34.0 %triangle_attention.23 = f32[12,64,64,256]{3,2,1,0:T(8,128)} custom-call(s32[2]{0:T(128)S(1)} %get-tuple-element.203.sc, f32[64,64,256]{2,1,0:T(8,128)S(1)} %copy-done.17, s32[12,64,256]{2,1,0:T(8,128)S(1)} %copy-done.1, bf16[4,4,64,256]{3,2,1,0:T(8,128)(2,1)S(1)} %fusion.3.bias, ...), custom_call_target="tpu_custom_call", output_to_operand_aliasing={{}: (7, {})} | custom-call | tf_op jit(solution)/shard_map/triangle_attention/pallas_call | solution.py:457
  (263 shorter events, 32.6 us)
Async XLA Ops:
  0.1 11.3 copy-start.57
  11.1 29.2 %copy-start.22 = (bf16[2,256,64]{2,1,0:T(8,128)(2,1)}, bf16[2,256,64]{2,1,0:T(8,128)(2,1)S(1)}, u32[]{:S(2)}) copy-start(bf16[2,256,64]{2,1,0:T(8,128)(2,1)S(1)} %pad_maximum_fusion.10.w_ab) | copy-start | bytes 196612
  11.5 28.8 %copy-start.2 = (f32[6,64,256]{2,1,0:T(8,128)}, f32[6,64,256]{2,1,0:T(8,128)S(1)}, u32[]{:S(2)}) copy-start(f32[6,64,256]{2,1,0:T(8,128)S(1)} %broadcast_dynamic-update-slice_fusion.norms) | copy-start | bytes 1179652
  11.6 38.6 %copy-start.47 = (bf16[64,64]{1,0:T(8,128)(2,1)S(1)}, bf16[64,64]{1,0:T(8,128)(2,1)}, u32[]{:S(2)}) copy-start(bf16[64,64]{1,0:T(8,128)(2,1)} %param.48) | copy-start | bytes 24580
  11.6 38.7 %copy-start.48 = (bf16[64,64]{1,0:T(8,128)(2,1)S(1)}, bf16[64,64]{1,0:T(8,128)(2,1)}, u32[]{:S(2)}) copy-start(bf16[64,64]{1,0:T(8,128)(2,1)} %param.51) | copy-start | bytes 24580
  11.6 38.8 %copy-start.49 = (bf16[64,64]{1,0:T(8,128)(2,1)S(1)}, bf16[64,64]{1,0:T(8,128)(2,1)}, u32[]{:S(2)}) copy-start(bf16[64,64]{1,0:T(8,128)(2,1)} %param.38) | copy-start | bytes 24580
  11.6 38.9 %copy-start.50 = (bf16[64,64]{1,0:T(8,128)(2,1)S(1)}, bf16[64,64]{1,0:T(8,128)(2,1)}, u32[]{:S(2)}) copy-start(bf16[64,64]{1,0:T(8,128)(2,1)} %param.41) | copy-start | bytes 24580
  11.6 39.0 %copy-start.58 = (bf16[64,4]{0,1:T(4,128)(2,1)S(1)}, bf16[64,4]{0,1:T(4,128)(2,1)}, u32[]{:S(2)}) copy-start(bf16[64,4]{0,1:T(4,128)(2,1)} %param.57) | copy-start | bytes 1540
  44.9 193.4 %collective-permute-start = (bf16[6,64,64,256]{3,2,1,0:T(8,128)(2,1)}, bf16[6,64,64,256]{3,2,1,0:T(8,128)(2,1)}, u32[]{:S(2)}, u32[]{:S(2)}) collective-permute-start(bf16[6,64,64,256]{3,2,1,0:T(8,128)(2,1)} %get-tuple-element.120.b_own), channel_id=1, source_target_pairs={{0,1},{1,0},{2,3},{3,2},{4,5},{5,4},{6,7},{7,6}} | collective-permute-start | bytes 37748744 | tf_op jit(solution)/shard_map/ppermute | solution.py:465
  45.7 228.0 %collective-permute-start.2 = (f32[64,64,256]{2,1,0:T(8,128)}, f32[64,64,256]{2,1,0:T(8,128)}, u32[]{:S(2)}, u32[]{:S(2)}) collective-permute-start(f32[64,64,256]{2,1,0:T(8,128)} %get-tuple-element.105), channel_id=1, source_target_pairs={{0,2},{1,3},{2,0},{3,1},{4,6},{5,7},{6,4},{7,5}} | collective-permute-start | bytes 12582920 | tf_op jit(solution)/shard_map/ppermute | solution.py:465
  48.2 225.5 %collective-permute-start.1 = (f32[64,64,256]{2,1,0:T(8,128)}, f32[64,64,256]{2,1,0:T(8,128)}, u32[]{:S(2)}, u32[]{:S(2)}) collective-permute-start(f32[64,64,256]{2,1,0:T(8,128)} %get-tuple-element.128), channel_id=1, source_target_pairs={{0,1},{1,0},{2,3},{3,2},{4,5},{5,4},{6,7},{7,6}} | collective-permute-start | bytes 12582920 | tf_op jit(solution)/shard_map/ppermute | solution.py:465
  48.4 225.3 %collective-permute-start.3 = (f32[64,64,256]{2,1,0:T(8,128)}, f32[64,64,256]{2,1,0:T(8,128)}, u32[]{:S(2)}, u32[]{:S(2)}) collective-permute-start(f32[64,64,256]{2,1,0:T(8,128)} %get-tuple-element.129), channel_id=1, source_target_pairs={{0,3},{1,2},{2,1},{3,0},{4,7},{5,6},{6,5},{7,4}} | collective-permute-start | bytes 12582920 | tf_op jit(solution)/shard_map/ppermute | solution.py:465
  48.4 183.0 %collective-permute-start.6 = (bf16[3,64,256]{2,1,0:T(8,128)(2,1)S(1)}, bf16[3,64,256]{2,1,0:T(8,128)(2,1)S(1)}, u32[]{:S(2)}, u32[]{:S(2)}) collective-permute-start(bf16[3,64,256]{2,1,0:T(8,128)(2,1)S(1)} %get-tuple-element.133), channel_id=1, source_target_pairs={{0,3},{1,2},{2,1},{3,0},{4,7},{5,6},{6,5},{7,4}} | collective-permute-start | bytes 294920 | tf_op jit(solution)/shard_map/ppermute | solution.py:465
  62.2 208.9 %copy-start.4 = (f32[4,64,8,128]{3,2,1,0:T(8,128)}, f32[4,64,8,128]{3,2,1,0:T(8,128)S(1)}, u32[]{:S(2)}) copy-start(f32[4,64,8,128]{3,2,1,0:T(8,128)S(1)} %pad_maximum_fusion.xgs) | copy-start | bytes 3145732
  231.5 4.8 collective-permute-start.5
  236.3 1.3 collective-permute-start.4
  273.7 97.3 %copy-start.51 = (bf16[64,64]{1,0:T(8,128)(2,1)S(1)}, bf16[64,64]{1,0:T(8,128)(2,1)}, u32[]{:S(2)}) copy-start(bf16[64,64]{1,0:T(8,128)(2,1)} %param.54) | copy-start | bytes 24580
  273.7 97.3 %copy-start.52 = (bf16[64,64]{1,0:T(8,128)(2,1)S(1)}, bf16[64,64]{1,0:T(8,128)(2,1)}, u32[]{:S(2)}) copy-start(bf16[64,64]{1,0:T(8,128)(2,1)} %param.55) | copy-start | bytes 24580
  273.7 97.4 %copy-start.53 = (bf16[64,64]{1,0:T(8,128)(2,1)S(1)}, bf16[64,64]{1,0:T(8,128)(2,1)}, u32[]{:S(2)}) copy-start(bf16[64,64]{1,0:T(8,128)(2,1)} %param.56) | copy-start | bytes 24580
  273.8 97.5 %copy-start.54 = (bf16[64,64]{1,0:T(8,128)(2,1)S(1)}, bf16[64,64]{1,0:T(8,128)(2,1)}, u32[]{:S(2)}) copy-start(bf16[64,64]{1,0:T(8,128)(2,1)} %param.58) | copy-start | bytes 24580
  273.8 97.6 %copy-start.55 = (bf16[64,64]{1,0:T(8,128)(2,1)S(1)}, bf16[64,64]{1,0:T(8,128)(2,1)}, u32[]{:S(2)}) copy-start(bf16[64,64]{1,0:T(8,128)(2,1)} %param.59) | copy-start | bytes 24580
  368.6 47.8 %collective-permute-start.7 = (f32[64,64,256]{2,1,0:T(8,128)}, f32[64,64,256]{2,1,0:T(8,128)}, u32[]{:S(2)}, u32[]{:S(2)}) collective-permute-start(f32[64,64,256]{2,1,0:T(8,128)} %get-tuple-element.149), channel_id=1, source_target_pairs={{0,1},{1,0},{2,3},{3,2},{4,5},{5,4},{6,7},{7,6}} | collective-permute-start | bytes 12582920 | tf_op jit(solution)/shard_map/ppermute | solution.py:465
  368.8 93.8 %collective-permute-start.10 = (f32[64,64,256]{2,1,0:T(8,128)}, f32[64,64,256]{2,1,0:T(8,128)}, u32[]{:S(2)}, u32[]{:S(2)}) collective-permute-start(f32[64,64,256]{2,1,0:T(8,128)} %get-tuple-element.153), channel_id=1, source_target_pairs={{0,2},{1,3},{2,0},{3,1},{4,6},{5,7},{6,4},{7,5}} | collective-permute-start | bytes 12582920 | tf_op jit(solution)/shard_map/ppermute | solution.py:465
  370.0 181.2 %collective-permute-start.11 = (f32[64,64,256]{2,1,0:T(8,128)}, f32[64,64,256]{2,1,0:T(8,128)}, u32[]{:S(2)}, u32[]{:S(2)}) collective-permute-start(f32[64,64,256]{2,1,0:T(8,128)} %get-tuple-element.154), channel_id=1, source_target_pairs={{0,3},{1,2},{2,1},{3,0},{4,7},{5,6},{6,5},{7,4}} | collective-permute-start | bytes 12582920 | tf_op jit(solution)/shard_map/ppermute | solution.py:465
  370.5 180.7 %collective-permute-start.9 = (f32[64,64,256]{2,1,0:T(8,128)}, f32[64,64,256]{2,1,0:T(8,128)}, u32[]{:S(2)}, u32[]{:S(2)}) collective-permute-start(f32[64,64,256]{2,1,0:T(8,128)} %get-tuple-element.152), channel_id=1, source_target_pairs={{0,1},{1,0},{2,3},{3,2},{4,5},{5,4},{6,7},{7,6}} | collective-permute-start | bytes 12582920 | tf_op jit(solution)/shard_map/ppermute | solution.py:465
  381.5 35.0 %collective-permute-start.8 = (bf16[4,4,64,256]{3,2,1,0:T(8,128)(2,1)S(1)}, bf16[4,4,64,256]{3,2,1,0:T(8,128)(2,1)S(1)}, u32[]{:S(2)}, u32[]{:S(2)}) collective-permute-start(bf16[4,4,64,256]{3,2,1,0:T(8,128)(2,1)S(1)} %copy-done.29), channel_id=1, source_target_pairs={{0,1},{1,0},{2,3},{3,2},{4,5},{5,4},{6,7},{7,6}} | collective-permute-start | bytes 1572872 | tf_op jit(solution)/shard_map/ppermute | solution.py:465
  646.1 40.6 %collective-permute-start.12 = (f32[64,64,256]{2,1,0:T(8,128)}, f32[64,64,256]{2,1,0:T(8,128)}, u32[]{:S(2)}, u32[]{:S(2)}) collective-permute-start(f32[64,64,256]{2,1,0:T(8,128)} %get-tuple-element.160), channel_id=1, source_target_pairs={{0,1},{1,0},{2,3},{3,2},{4,5},{5,4},{6,7},{7,6}} | collective-permute-start | bytes 12582920 | tf_op jit(solution)/shard_map/ppermute | solution.py:465
  646.6 76.3 %collective-permute-start.14 = (f32[64,64,256]{2,1,0:T(8,128)}, f32[64,64,256]{2,1,0:T(8,128)}, u32[]{:S(2)}, u32[]{:S(2)}) collective-permute-start(f32[64,64,256]{2,1,0:T(8,128)} %get-tuple-element.163), channel_id=1, source_target_pairs={{0,1},{1,0},{2,3},{3,2},{4,5},{5,4},{6,7},{7,6}} | collective-permute-start | bytes 12582920 | tf_op jit(solution)/shard_map/ppermute | solution.py:465
  646.6 93.8 %collective-permute-start.15 = (f32[64,64,256]{2,1,0:T(8,128)}, f32[64,64,256]{2,1,0:T(8,128)}, u32[]{:S(2)}, u32[]{:S(2)}) collective-permute-start(f32[64,64,256]{2,1,0:T(8,128)} %get-tuple-element.164), channel_id=1, source_target_pairs={{0,2},{1,3},{2,0},{3,1},{4,6},{5,7},{6,4},{7,5}} | collective-permute-start | bytes 12582920 | tf_op jit(solution)/shard_map/ppermute | solution.py:465
  647.4 181.9 %collective-permute-start.16 = (f32[64,64,256]{2,1,0:T(8,128)}, f32[64,64,256]{2,1,0:T(8,128)}, u32[]{:S(2)}, u32[]{:S(2)}) collective-permute-start(f32[64,64,256]{2,1,0:T(8,128)} %get-tuple-element.165), channel_id=1, source_target_pairs={{0,3},{1,2},{2,1},{3,0},{4,7},{5,6},{6,5},{7,4}} | collective-permute-start | bytes 12582920 | tf_op jit(solution)/shard_map/ppermute | solution.py:465
  648.4 38.3 %collective-permute-start.13 = (bf16[4,4,64,256]{3,2,1,0:T(8,128)(2,1)}, bf16[4,4,64,256]{3,2,1,0:T(8,128)(2,1)S(1)}, u32[]{:S(2)}, u32[]{:S(2)}) collective-permute-start(bf16[4,4,64,256]{3,2,1,0:T(8,128)(2,1)} %get-tuple-element.158.bias), channel_id=1, source_target_pairs={{0,1},{1,0},{2,3},{3,2},{4,5},{5,4},{6,7},{7,6}} | collective-permute-start | bytes 1572872 | tf_op jit(solution)/shard_map/ppermute | solution.py:465
  924.3 144.7 %collective-permute-start.17 = (f32[64,64,256]{2,1,0:T(8,128)}, f32[64,64,256]{2,1,0:T(8,128)}, u32[]{:S(2)}, u32[]{:S(2)}) collective-permute-start(f32[64,64,256]{2,1,0:T(8,128)} %get-tuple-element.171), channel_id=1, source_target_pairs={{0,1},{1,0},{2,3},{3,2},{4,5},{5,4},{6,7},{7,6}} | collective-permute-start | bytes 12582920 | tf_op jit(solution)/shard_map/ppermute | solution.py:465
  924.6 138.4 %collective-permute-start.20 = (bf16[64,64,256]{2,1,0:T(8,128)(2,1)}, bf16[64,64,256]{2,1,0:T(8,128)(2,1)S(1)}, u32[]{:S(2)}, u32[]{:S(2)}) collective-permute-start(bf16[64,64,256]{2,1,0:T(8,128)(2,1)} %get-tuple-element.174), channel_id=1, source_target_pairs={{0,2},{1,3},{2,0},{3,1},{4,6},{5,7},{6,4},{7,5}} | collective-permute-start | bytes 6291464 | tf_op jit(solution)/shard_map/ppermute | solution.py:465
  925.0 141.0 %collective-permute-start.22 = (bf16[64,64,256]{2,1,0:T(8,128)(2,1)}, bf16[64,64,256]{2,1,0:T(8,128)(2,1)S(1)}, u32[]{:S(2)}, u32[]{:S(2)}) collective-permute-start(bf16[64,64,256]{2,1,0:T(8,128)(2,1)} %get-tuple-element.139), channel_id=1, source_target_pairs={{0,3},{1,2},{2,1},{3,0},{4,7},{5,6},{6,5},{7,4}} | collective-permute-start | bytes 6291464 | tf_op jit(solution)/shard_map/ppermute | solution.py:465
  926.2 114.6 %collective-permute-start.19 = (bf16[64,64,128]{2,1,0:T(8,128)(2,1)}, bf16[64,64,128]{2,1,0:T(8,128)(2,1)S(1)}, u32[]{:S(2)}, u32[]{:S(2)}) collective-permute-start(bf16[64,64,128]{2,1,0:T(8,128)(2,1)} %get-tuple-element.173), channel_id=1, source_target_pairs={{0,2},{1,3},{2,0},{3,1},{4,6},{5,7},{6,4},{7,5}} | collective-permute-start | bytes 3145736 | tf_op jit(solution)/shard_map/ppermute | solution.py:465
  926.7 135.0 %collective-permute-start.21 = (bf16[64,64,128]{2,1,0:T(8,128)(2,1)}, bf16[64,64,128]{2,1,0:T(8,128)(2,1)S(1)}, u32[]{:S(2)}, u32[]{:S(2)}) collective-permute-start(bf16[64,64,128]{2,1,0:T(8,128)(2,1)} %get-tuple-element.177), channel_id=1, source_target_pairs={{0,3},{1,2},{2,1},{3,0},{4,7},{5,6},{6,5},{7,4}} | collective-permute-start | bytes 3145736 | tf_op jit(solution)/shard_map/ppermute | solution.py:465
  1041.7 26.1 %collective-permute-start.18 = (bf16[4,4,64,256]{3,2,1,0:T(8,128)(2,1)}, bf16[4,4,64,256]{3,2,1,0:T(8,128)(2,1)S(1)}, u32[]{:S(2)}, u32[]{:S(2)}) collective-permute-start(bf16[4,4,64,256]{3,2,1,0:T(8,128)(2,1)} %get-tuple-element.169.bias), channel_id=1, source_target_pairs={{0,1},{1,0},{2,3},{3,2},{4,5},{5,4},{6,7},{7,6}} | collective-permute-start | bytes 1572872 | tf_op jit(solution)/shard_map/ppermute | solution.py:465
  1062.6 147.8 %collective-permute-start.27 = (bf16[64,64,256]{2,1,0:T(8,128)(2,1)}, bf16[64,64,256]{2,1,0:T(8,128)(2,1)}, u32[]{:S(2)}, u32[]{:S(2)}) collective-permute-start(bf16[64,64,256]{2,1,0:T(8,128)(2,1)} %get-tuple-element.185), channel_id=1, source_target_pairs={{0,2},{1,3},{2,0},{3,1},{4,6},{5,7},{6,4},{7,5}} | collective-permute-start | bytes 6291464 | tf_op jit(solution)/shard_map/ppermute | solution.py:465
  1064.4 147.7 %collective-permute-start.29 = (bf16[64,64,256]{2,1,0:T(8,128)(2,1)}, bf16[64,64,256]{2,1,0:T(8,128)(2,1)}, u32[]{:S(2)}, u32[]{:S(2)}) collective-permute-start(bf16[64,64,256]{2,1,0:T(8,128)(2,1)} %get-tuple-element.155), channel_id=1, source_target_pairs={{0,3},{1,2},{2,1},{3,0},{4,7},{5,6},{6,5},{7,4}} | collective-permute-start | bytes 6291464 | tf_op jit(solution)/shard_map/ppermute | solution.py:465
  1067.4 117.2 %collective-permute-start.26 = (bf16[64,64,128]{2,1,0:T(8,128)(2,1)}, bf16[64,64,128]{2,1,0:T(8,128)(2,1)}, u32[]{:S(2)}, u32[]{:S(2)}) collective-permute-start(bf16[64,64,128]{2,1,0:T(8,128)(2,1)} %get-tuple-element.184), channel_id=1, source_target_pairs={{0,2},{1,3},{2,0},{3,1},{4,6},{5,7},{6,4},{7,5}} | collective-permute-start | bytes 3145736 | tf_op jit(solution)/shard_map/ppermute | solution.py:465
  1067.8 113.0 %collective-permute-start.23 = (bf16[4,64,256]{2,1,0:T(8,128)(2,1)S(1)}, bf16[4,64,256]{2,1,0:T(8,128)(2,1)S(1)}, u32[]{:S(2)}, u32[]{:S(2)}) collective-permute-start(bf16[4,64,256]{2,1,0:T(8,128)(2,1)S(1)} %get-tuple-element.230), channel_id=1, source_target_pairs={{0,3},{1,2},{2,1},{3,0},{4,7},{5,6},{6,5},{7,4}} | collective-permute-start | bytes 393224 | tf_op jit(solution)/shard_map/ppermute | solution.py:465
  1069.0 115.0 %collective-permute-start.24 = (bf16[4,64,256]{2,1,0:T(8,128)(2,1)S(1)}, bf16[4,64,256]{2,1,0:T(8,128)(2,1)S(1)}, u32[]{:S(2)}, u32[]{:S(2)}) collective-permute-start(bf16[4,64,256]{2,1,0:T(8,128)(2,1)S(1)} %get-tuple-element.231), channel_id=1, source_target_pairs={{0,2},{1,3},{2,0},{3,1},{4,6},{5,7},{6,4},{7,5}} | collective-permute-start | bytes 393224 | tf_op jit(solution)/shard_map/ppermute | solution.py:465
  1072.9 70.4 %slice-start = ((s8[6291456]{0:T(1024)(128)(4,1)}), s8[4194304]{0:T(1024)(128)(4,1)S(1)}, s32[]{:S(2)}) async-start(s8[6291456]{0:T(1024)(128)(4,1)} %bitcast.134), calls=%async_computation | async-start | bytes 8388608
  1106.9 36.5 %slice-start.1 = ((s8[6291456]{0:T(1024)(128)(4,1)}), s8[2097152]{0:T(1024)(128)(4,1)S(1)}, s32[]{:S(2)}) async-start(s8[6291456]{0:T(1024)(128)(4,1)} %bitcast.134), calls=%async_computation.1 | async-start | bytes 4194304
  1106.9 36.5 %copy-start.3 = (f32[6,64,256]{2,1,0:T(8,128)S(1)}, f32[6,64,256]{2,1,0:T(8,128)}, u32[]{:S(2)}) copy-start(f32[6,64,256]{2,1,0:T(8,128)} %copy-done.2) | copy-start | bytes 1179652
  1106.9 36.5 %copy-start.6 = (bf16[4,64,64]{2,1,0:T(8,128)(2,1)S(1)}, bf16[4,64,64]{2,1,0:T(8,128)(2,1)}, u32[]{:S(2)}) copy-start(bf16[4,64,64]{2,1,0:T(8,128)(2,1)} %pad_maximum_fusion.12.w_sq) | copy-start | bytes 98308
  1106.9 36.5 %copy-start.37 = (bf16[64,64,128]{2,1,0:T(8,128)(2,1)S(1)}, bf16[64,64,128]{2,1,0:T(8,128)(2,1)}, u32[]{:S(2)}) copy-start(bf16[64,64,128]{2,1,0:T(8,128)(2,1)} %copy-done.36) | copy-start | bytes 3145732
  1106.9 36.5 %copy-start.38 = (bf16[8,64]{1,0:T(8,128)(2,1)S(1)}, bf16[8,64]{1,0:T(8,128)(2,1)}, u32[]{:S(2)}) copy-start(bf16[8,64]{1,0:T(8,128)(2,1)} %concatenate.53.w_bias) | copy-start | bytes 3076
  1155.9 28.2 %copy-start.67 = (bf16[64,64,128]{2,1,0:T(8,128)(2,1)S(1)}, bf16[64,64,128]{2,1,0:T(8,128)(2,1)}, u32[]{:S(2)}) copy-start(bf16[64,64,128]{2,1,0:T(8,128)(2,1)} %get-tuple-element.188) | copy-start | bytes 3145732
  1155.9 30.8 %copy-start.31 = (bf16[4,4,64,256]{3,2,1,0:T(8,128)(2,1)S(1)}, bf16[4,4,64,256]{3,2,1,0:T(8,128)(2,1)}, u32[]{:S(2)}) copy-start(bf16[4,4,64,256]{3,2,1,0:T(8,128)(2,1)} %get-tuple-element.158.bias) | copy-start | bytes 1572868
  1184.1 1.9 collective-permute-start.25
  1184.1 24.8 %collective-permute-start.28 = (bf16[64,64,128]{2,1,0:T(8,128)(2,1)S(1)}, bf16[64,64,128]{2,1,0:T(8,128)(2,1)S(1)}, u32[]{:S(2)}, u32[]{:S(2)}) collective-permute-start(bf16[64,64,128]{2,1,0:T(8,128)(2,1)S(1)} %copy-done.67), channel_id=1, source_target_pairs={{0,3},{1,2},{2,1},{3,0},{4,7},{5,6},{6,5},{7,4}} | collective-permute-start | bytes 3145736 | tf_op jit(solution)/shard_map/ppermute | solution.py:465
  1184.6 227.4 %collective-permute-start.36 = (bf16[64,64,256]{2,1,0:T(8,128)(2,1)}, bf16[64,64,256]{2,1,0:T(8,128)(2,1)}, u32[]{:S(2)}, u32[]{:S(2)}) collective-permute-start(bf16[64,64,256]{2,1,0:T(8,128)(2,1)} %get-tuple-element.166), channel_id=1, source_target_pairs={{0,3},{1,2},{2,1},{3,0},{4,7},{5,6},{6,5},{7,4}} | collective-permute-start | bytes 6291464 | tf_op jit(solution)/shard_map/ppermute | solution.py:465
  1186.0 215.1 %collective-permute-start.34 = (bf16[64,64,256]{2,1,0:T(8,128)(2,1)}, bf16[64,64,256]{2,1,0:T(8,128)(2,1)}, u32[]{:S(2)}, u32[]{:S(2)}) collective-permute-start(bf16[64,64,256]{2,1,0:T(8,128)(2,1)} %get-tuple-element.196), channel_id=1, source_target_pairs={{0,2},{1,3},{2,0},{3,1},{4,6},{5,7},{6,4},{7,5}} | collective-permute-start | bytes 6291464 | tf_op jit(solution)/shard_map/ppermute | solution.py:465
  1209.0 98.1 %collective-permute-start.30 = (bf16[4,64,256]{2,1,0:T(8,128)(2,1)S(1)}, bf16[4,64,256]{2,1,0:T(8,128)(2,1)S(1)}, u32[]{:S(2)}, u32[]{:S(2)}) collective-permute-start(bf16[4,64,256]{2,1,0:T(8,128)(2,1)S(1)} %get-tuple-element.224), channel_id=1, source_target_pairs={{0,3},{1,2},{2,1},{3,0},{4,7},{5,6},{6,5},{7,4}} | collective-permute-start | bytes 393224 | tf_op jit(solution)/shard_map/ppermute | solution.py:465
  1210.5 96.6 %collective-permute-start.31 = (bf16[4,64,256]{2,1,0:T(8,128)(2,1)S(1)}, bf16[4,64,256]{2,1,0:T(8,128)(2,1)S(1)}, u32[]{:S(2)}, u32[]{:S(2)}) collective-permute-start(bf16[4,64,256]{2,1,0:T(8,128)(2,1)S(1)} %get-tuple-element.225), channel_id=1, source_target_pairs={{0,2},{1,3},{2,0},{3,1},{4,6},{5,7},{6,4},{7,5}} | collective-permute-start | bytes 393224 | tf_op jit(solution)/shard_map/ppermute | solution.py:465
  1212.1 116.2 %collective-permute-start.33 = (bf16[64,64,128]{2,1,0:T(8,128)(2,1)}, bf16[64,64,128]{2,1,0:T(8,128)(2,1)}, u32[]{:S(2)}, u32[]{:S(2)}) collective-permute-start(bf16[64,64,128]{2,1,0:T(8,128)(2,1)} %get-tuple-element.195), channel_id=1, source_target_pairs={{0,2},{1,3},{2,0},{3,1},{4,6},{5,7},{6,4},{7,5}} | collective-permute-start | bytes 3145736 | tf_op jit(solution)/shard_map/ppermute | solution.py:465
  1296.2 12.9 copy-start.28
  1307.1 105.0 %collective-permute-start.35 = (bf16[64,64,128]{2,1,0:T(8,128)(2,1)}, bf16[64,64,128]{2,1,0:T(8,128)(2,1)}, u32[]{:S(2)}, u32[]{:S(2)}) collective-permute-start(bf16[64,64,128]{2,1,0:T(8,128)(2,1)} %get-tuple-element.199), channel_id=1, source_target_pairs={{0,3},{1,2},{2,1},{3,0},{4,7},{5,6},{6,5},{7,4}} | collective-permute-start | bytes 3145736 | tf_op jit(solution)/shard_map/ppermute | solution.py:465
  1307.1 3.3 collective-permute-start.32
  1310.5 112.7 %collective-permute-start.37 = (bf16[4,64,256]{2,1,0:T(8,128)(2,1)S(1)}, bf16[4,64,256]{2,1,0:T(8,128)(2,1)S(1)}, u32[]{:S(2)}, u32[]{:S(2)}) collective-permute-start(bf16[4,64,256]{2,1,0:T(8,128)(2,1)S(1)} %get-tuple-element.218), channel_id=1, source_target_pairs={{0,3},{1,2},{2,1},{3,0},{4,7},{5,6},{6,5},{7,4}} | collective-permute-start | bytes 393224 | tf_op jit(solution)/shard_map/ppermute | solution.py:465
  1328.3 94.8 %collective-permute-start.38 = (bf16[4,64,256]{2,1,0:T(8,128)(2,1)S(1)}, bf16[4,64,256]{2,1,0:T(8,128)(2,1)S(1)}, u32[]{:S(2)}, u32[]{:S(2)}) collective-permute-start(bf16[4,64,256]{2,1,0:T(8,128)(2,1)S(1)} %get-tuple-element.219), channel_id=1, source_target_pairs={{0,2},{1,3},{2,0},{3,1},{4,6},{5,7},{6,4},{7,5}} | collective-permute-start | bytes 393224 | tf_op jit(solution)/shard_map/ppermute | solution.py:465
  1423.2 1.9 collective-permute-start.39
  1427.4 34.0 %copy-start.17 = (f32[64,64,256]{2,1,0:T(8,128)S(1)}, f32[64,64,256]{2,1,0:T(8,128)}, u32[]{:S(2)}) copy-start(f32[64,64,256]{2,1,0:T(8,128)} %copy-done.16) | copy-start | bytes 12582916
  (46 other events, 290.9 us)
where the time goes:
time: 1510 us; the launch traced here: 1500 us
  Pallas kernels  814 us (54%)
  waiting for transfers between devices  569 us (38%)
  local copies, waits for them, and re-layouts  78.4 us (5%)
  starting transfers between devices  28 us (2%)
    ppermute x40, waiting for transfers between devices, exchange(): return lax.ppermute(values, 'dap', [(i, i ^ r) for i in range(4)])  569 us
    pallas_call x12, Pallas kernels, a_call(): return call(*args) if fresh else call(*args, out)  415 us
    pallas_call x3, Pallas kernels, u_call(): pl.pallas_call(u_kernel, out_shape=(ROW_WIDE, ROW_WIDE, jax.ShapeDtypeStr...  285 us
    pallas_call x6, Pallas kernels, r_call(): pl.pallas_call(r_kernel, out_shape=(ROW_WIDE, jax.ShapeDtypeStruct((4, RO...  53.1 us
    unnamed x145, local copies, waits for them, and re-layouts  43.4 us
    pallas_call x1, Pallas kernels, l2_call(): pl.pallas_call(l2_kernel, grid=(n // 2,), out_shape=jax.ShapeDtypeStruct(...  32.9 us
  transfers between devices with their start and end apart: 40, of which 16 were waited for; matrix products, arithmetic and copies ran while one was open for 2% of the time, Pallas kernels for 29%

commit v1 on v0

--- a/solution.py
+++ b/solution.py
@@ -1,3 +1,5 @@
+import functools
+
 import jax
 import jax.numpy as jnp
 from jax import lax
@@ -12,10 +14,15 @@
 TILE = 16
 
 
-def channel_norm(vals, gain, shift, axis_id):
+def channel_stats(vals, axis_id):
     ch_mean = jnp.mean(vals, axis=axis_id, keepdims=True)
     ch_var = jnp.mean(jnp.square(vals - ch_mean), axis=axis_id, keepdims=True)
-    return (vals - ch_mean) * lax.rsqrt(ch_var + LN_EPS) * gain + shift
+    return ch_mean, lax.rsqrt(ch_var + LN_EPS)
+
+
+def channel_norm(vals, norm, stats=None):
+    ch_mean, scale = channel_stats(vals, 0) if stats is None else stats
+    return (vals - ch_mean) * scale * norm[0] + norm[1]
 
 
 def sigmoid(vals):
@@ -24,10 +31,6 @@
 
 def mm(lhs, rhs):
     return jnp.dot(lhs, rhs, preferred_element_type=F32)
-
-
-def masked_norm(z_row, m_row, norm):
-    return (m_row * channel_norm(z_row, norm[0], norm[1], 0)).astype(BF16)
 
 
 def ab_row(proj, tile_a, tile_b, slot):
@@ -66,11 +69,11 @@
 
 
 def u_kernel(sc, zt, zr1, zr2, zr3, mask0, mask1, mask2, mask3, norms, xgs, w_ab, w_sq, w_bias,
-             z2_own, z2_par, bias_out, xo2, xo3, xi2, xi3,
-             z_s, a_s, b_s, x_s, mask, tile_a, tile_b, tile_x, tile_c, tile_d, tile_z, in_sem, z_sem, x_sem):
+             z2_own, z2_par, bias_out, far2, far3,
+             z_s, a_s, b_s, x_s, mask, stats, tile_a, tile_b, tile_x, tile_c, tile_d, tile_z, in_sem, z_sem, x_sem):
     me, sample = sc[0], sc[1]
     srcs = (zt.at[sample], zr1, zr2, zr3)
-    lanes = pl.ds(pl.multiple_of(128 * (me // 2), 128), 128)
+    lanes = pl.ds(pl.multiple_of(LANES * (me // 2), LANES), LANES)
     out_norm = (norms[0], norms[1])
     in_norm = (norms[2], norms[3])
     att_norm = (norms[4], norms[5])
@@ -85,22 +88,40 @@
     for r, part in enumerate((mask0, mask1, mask2, mask3)):
         mask[pl.ds(pl.multiple_of(ROWS * (me ^ r), ROWS), ROWS), :] = part[...].astype(F32)
 
+    def mask_row(base, i):
+        return mask[pl.ds(base + i, 1), :]
+
+    def measure(base, i, vals=None):
+        found = channel_stats(z_s[base + i] if vals is None else vals, 0)
+        for n in range(2):
+            stats[n if vals is None else n + 2, pl.ds(base + i, 1), :] = found[n]
+        return found
+
+    def recall(base, i, first):
+        return [stats[first + n, pl.ds(base + i, 1), :] for n in range(2)]
+
     def flush(base):
         a_s[:, pl.ds(base, TILE), :] = jnp.swapaxes(tile_a[...], 0, 1)
         b_s[:, pl.ds(base, TILE), :] = jnp.swapaxes(tile_b[...], 0, 1)
 
-    def part_of(t):
-        return (t * TILE // ROWS) ^ me, pl.ds(pl.multiple_of(t * TILE % ROWS, TILE), TILE)
-
-    def export(t, start, own, par, far2, far3, sem):
-        r, rows = part_of(t)
+    def export(t, start, outgoing, sem):
+        r = (t * TILE // ROWS) ^ me
+        q = t % (ROWS // TILE)
+        rows = pl.ds(pl.multiple_of(TILE * q, TILE), TILE)
+        half = pl.ds(pl.multiple_of(ROWS + TILE * (q % 2), TILE), TILE)
+        side = pl.ds(pl.multiple_of(LANES * (q // 2), LANES), LANES)
         act = (lambda cp: cp.start()) if start else (lambda cp: cp.wait())
-        src = tile_c.at[t % 2] if far2.shape[-1] == COLS else tile_c.at[t % 2, :, :, lanes]
-        for k, dst in ((0, own), (1, par), (2, far2), (3, far3)):
-            if dst is not None:
+        for k, dst in ((0, z2_own), (1, z2_par), (2, far2), (3, far3)):
+            if k > 1 or not outgoing:
                 @pl.when(r == k)
                 def _():
-                    act(pltpu.make_async_copy(tile_z.at[t % 2] if k < 2 else src, dst.at[rows], sem.at[t % 2]))
+                    if k < 2:
+                        src, to = tile_z.at[t % 2], dst.at[rows]
+                    elif outgoing:
+                        src, to = tile_c.at[t % 2, :, :, lanes], dst.at[half, :, side]
+                    else:
+                        src, to = tile_c.at[t % 2], dst.at[rows]
+                    act(pltpu.make_async_copy(src, to, sem.at[t % 2]))
 
     @pl.loop(0, n_tiles)
     def _(v):
@@ -113,7 +134,7 @@
         base = pl.multiple_of(ROWS * (me ^ r) + v * TILE % ROWS, TILE)
         staggered(
             TILE,
-            lambda i, _: mm(w_ab[0], masked_norm(z_s[base + i], mask[pl.ds(base + i, 1), :], out_norm)),
+            lambda i, _: mm(w_ab[0], (mask_row(base, i) * channel_norm(z_s[base + i], out_norm, measure(base, i))).astype(BF16)),
             lambda i, proj: ab_row(proj, tile_a, tile_b, i))
         flush(base)
 
@@ -127,28 +148,28 @@
 
         @pl.when(t >= 2)
         def _():
-            export(t - 2, False, None, None, xo2, xo3, x_sem)
+            export(t - 2, False, True, x_sem)
 
         x_norm_tile(x_s, tile_x, base, xgs.at[0], xgs.at[1])
         tile_c[t % 2] = jnp.swapaxes(tile_x[...], 0, 1)
 
         def gate_and_update(i, _):
-            normed = channel_norm(z_s[base + i], out_norm[0], out_norm[1], 0).astype(BF16)
+            normed = channel_norm(z_s[base + i], out_norm, recall(base, i, 0)).astype(BF16)
             return mm(w_sq[0], normed), mm(w_sq[1], tile_c[t % 2, i])
 
         def next_norm(i, parts):
             z_one = z_s[base + i] + (jnp.tanh(parts[0]) + 1.0) * parts[1]
             tile_z[0, i] = z_one
-            return masked_norm(z_one, mask[pl.ds(base + i, 1), :], in_norm)
+            return (mask_row(base, i) * channel_norm(z_one, in_norm, measure(base, i, z_one))).astype(BF16)
 
         staggered(TILE, gate_and_update, next_norm, lambda i, normed: mm(w_ab[1], normed),
                   lambda i, proj: ab_row(proj, tile_a, tile_b, i))
         flush(base)
         z_s[pl.ds(base, TILE)] = tile_z[0]
-        export(t, True, None, None, xo2, xo3, x_sem)
+        export(t, True, True, x_sem)
 
     for t in (n_tiles - 2, n_tiles - 1):
-        export(t, False, None, None, xo2, xo3, x_sem)
+        export(t, False, True, x_sem)
 
     @pl.loop(0, CH, unroll=4)
     def _(c):
@@ -160,19 +181,19 @@
 
         @pl.when(t >= 2)
         def _():
-            export(t - 2, False, z2_own, z2_par, xi2, xi3, z_sem)
+            export(t - 2, False, False, z_sem)
 
         x_norm_tile(x_s, tile_x, base, xgs.at[2], xgs.at[3])
         tile_c[t % 2] = jnp.swapaxes(tile_x[...], 0, 1)
 
         def gate_and_update(i, _):
-            normed = channel_norm(z_s[base + i], in_norm[0], in_norm[1], 0).astype(BF16)
+            normed = channel_norm(z_s[base + i], in_norm, recall(base, i, 2)).astype(BF16)
             return mm(w_sq[2], normed), mm(w_sq[3], tile_c[t % 2, i])
 
         def next_norm(i, parts):
             z_two = z_s[base + i] + (jnp.tanh(parts[0]) + 1.0) * parts[1]
             tile_z[t % 2, i] = z_two
-            return channel_norm(z_two, att_norm[0], att_norm[1], 0).astype(BF16)
+            return channel_norm(z_two, att_norm).astype(BF16)
 
         def bias_row(i, normed):
             tile_d[i] = mm(w_bias[...], normed)
@@ -180,10 +201,17 @@
         staggered(TILE, gate_and_update, next_norm, bias_row)
         rows = pl.ds(pl.multiple_of(t * TILE % ROWS, TILE), TILE)
         bias_out[t * TILE // ROWS, :, rows, :] = jnp.swapaxes(tile_d[...], 0, 1)[:4].astype(BF16)
-        export(t, True, z2_own, z2_par, xi2, xi3, z_sem)
-
+        export(t, True, False, z_sem)
+
+    def bias_copy(n):
+        return pltpu.make_async_copy(bias_out.at[me ^ n], (far2, far3)[n].at[pl.ds(FAR_BIAS, 4)], x_sem.at[n])
+
+    for n in range(2):
+        bias_copy(n).start()
     for t in (n_tiles - 2, n_tiles - 1):
-        export(t, False, z2_own, z2_par, xi2, xi3, z_sem)
+        export(t, False, False, z_sem)
+    for n in range(2):
+        bias_copy(n).wait()
 
 
 LANES = 128
@@ -193,8 +221,8 @@
 PARAMS = pltpu.CompilerParams(vmem_limit_bytes=40 << 20, dimension_semantics=("arbitrary",))
 AB_TILE = pltpu.VMEM((TILE, CH, COLS), BF16)
 DMA2 = pltpu.SemaphoreType.DMA((2,))
-ROW_HALF = jax.ShapeDtypeStruct((ROWS, CH, LANES), BF16)
-ROW_FULL = jax.ShapeDtypeStruct((ROWS, CH, COLS), BF16)
+FAR_BIAS = ROWS + ROWS // 2
+FAR = jax.ShapeDtypeStruct((FAR_BIAS + 4, CH, COLS), BF16)
 ROW_WIDE = jax.ShapeDtypeStruct((ROWS, CH, COLS), F32)
 SAMPLE_BF = pltpu.VMEM((CH, COLS, COLS), BF16)
 
@@ -202,12 +230,12 @@
 def u_call(sc, zt, zr, masks, norms, xgs, w_ab, w_sq, w_bias):
     return pl.pallas_call(
         u_kernel,
-        out_shape=(ROW_WIDE, ROW_WIDE, jax.ShapeDtypeStruct((4, 4, ROWS, COLS), BF16), ROW_HALF, ROW_HALF, ROW_FULL, ROW_FULL),
+        out_shape=(ROW_WIDE, ROW_WIDE, jax.ShapeDtypeStruct((4, 4, ROWS, COLS), BF16), FAR, FAR),
         in_specs=[SM] + [HB] * 4 + [VM] * 9,
-        out_specs=(HB, HB, VM, HB, HB, HB, HB),
+        out_specs=(HB, HB, VM, HB, HB),
         scratch_shapes=[
             pltpu.VMEM((COLS, CH, COLS), F32), SAMPLE_BF, SAMPLE_BF,
-            pltpu.VMEM((CH, COLS, COLS), F32), pltpu.VMEM((COLS, COLS), F32), AB_TILE, AB_TILE, pltpu.VMEM((CH, TILE, COLS), BF16), pltpu.VMEM((2, TILE, CH, COLS), BF16),
+            pltpu.VMEM((CH, COLS, COLS), F32), pltpu.VMEM((COLS, COLS), F32), pltpu.VMEM((4, COLS, COLS), F32), AB_TILE, AB_TILE, pltpu.VMEM((CH, TILE, COLS), BF16), pltpu.VMEM((2, TILE, CH, COLS), BF16),
             pltpu.VMEM((TILE, 8, COLS), F32), pltpu.VMEM((2, TILE, CH, COLS), F32),
             pltpu.SemaphoreType.DMA((4,)), DMA2, DMA2,
         ],
@@ -225,7 +253,7 @@
         base = pl.multiple_of(TILE * t, TILE)
         staggered(
             TILE,
-            lambda i, _: mm(w_ab[0], masked_norm(z_in[0, base + i], mask[pl.ds(base + i, 1), :], out_norm)),
+            lambda i, _: mm(w_ab[0], (mask[pl.ds(base + i, 1), :] * channel_norm(z_in[0, base + i], out_norm)).astype(BF16)),
             lambda i, proj: ab_row(proj, tile_a, tile_b, i))
         a_out[0, :, pl.ds(base, TILE), :] = jnp.swapaxes(tile_a[...], 0, 1)
         b_out[0, :, pl.ds(base, TILE), :] = jnp.swapaxes(tile_b[...], 0, 1)
@@ -293,13 +321,13 @@
     def outgoing(i, _):
         near, far = x_near[0, i].astype(F32), x_far[i].astype(F32)
         xn = jnp.concatenate([jnp.where(first, near, far), jnp.where(first, far, near)], axis=1).astype(BF16)
-        normed = channel_norm(z_in[0, i], out_norm[0], out_norm[1], 0).astype(BF16)
+        normed = channel_norm(z_in[0, i], out_norm).astype(BF16)
         return mm(w_sq[0], normed), mm(w_sq[1], xn)
 
     def norm_one(i, parts):
         z_one = z_in[0, i] + (jnp.tanh(parts[0]) + 1.0) * parts[1]
         z_out[i] = z_one
-        return channel_norm(z_one, in_norm[0], in_norm[1], 0).astype(BF16)
+        return channel_norm(z_one, in_norm).astype(BF16)
 
     def incoming(i, normed):
         return mm(w_sq[2], normed), mm(w_sq[3], xi[i])
@@ -307,7 +335,7 @@
     def norm_two(i, parts):
         z_two = z_out[i] + (jnp.tanh(parts[0]) + 1.0) * parts[1]
         z_out[i] = z_two
-        return channel_norm(z_two, att_norm[0], att_norm[1], 0).astype(BF16)
+        return channel_norm(z_two, att_norm).astype(BF16)
 
     def bias_row(i, normed):
         tile_d[i] = mm(w_bias[...], normed)
@@ -316,42 +344,67 @@
     bias_out[...] = jnp.swapaxes(tile_d[...], 0, 1)[:4].astype(BF16)
 
 
-def r_call(sc, zt, x_near, x_far, xi, norms, w_sq, w_bias):
+def r_call(sc, zt, x_near, far, norms, w_sq, w_bias):
     return pl.pallas_call(
         r_kernel,
         out_shape=(ROW_WIDE, jax.ShapeDtypeStruct((4, ROWS, COLS), BF16)),
         grid_spec=pltpu.PrefetchScalarGridSpec(
             num_scalar_prefetch=1, grid=(ROWS // TILE,),
             in_specs=[pl.BlockSpec((1, TILE, CH, COLS), lambda i, sc: (sc[1], i, 0, 0)),
-                      pl.BlockSpec((1, TILE, CH, 128), lambda i, sc: (sc[2], i, 0, 0)),
-                      pl.BlockSpec((TILE, CH, 128), lambda i, sc: (i, 0, 0)),
+                      pl.BlockSpec((1, TILE, CH, LANES), lambda i, sc: (sc[2], i, 0, 0)),
+                      pl.BlockSpec((TILE, CH, LANES), lambda i, sc: (ROWS // TILE + i % 2, 0, i // 2)),
                       pl.BlockSpec((TILE, CH, COLS), lambda i, sc: (i, 0, 0)), VM, VM, VM],
             out_specs=(pl.BlockSpec((TILE, CH, COLS), lambda i, sc: (i, 0, 0)),
                        pl.BlockSpec((4, TILE, COLS), lambda i, sc: (0, i, 0))),
             scratch_shapes=[pltpu.VMEM((TILE, 8, COLS), F32)]),
         compiler_params=PARAMS,
         name="row_updates",
-    )(sc, zt, x_near, x_far, xi, norms, w_sq, w_bias)
+    )(sc, zt, x_near, far, far, norms, w_sq, w_bias)
 
 
 HEADS, HEAD = 4, 16
 MASK_FILL = -1e9
 CHUNK = 32
 SLOTS = 2
-
-
-def a_kernel(sc, z_in, mask_in, bias, norms, w_all, w_proj, out_in, out_ref, mask, bias_rows, bias_t, q_s, k_s, v_s, g_s, vn_s, gn_s, keep_s, s_buf, e_buf, p_s, top_s, inv_s, o_s):
-    z_out = out_ref.at[0]
-    mask[...] = mask_in[0].astype(F32)
-    for r in range(4):
-        bias_rows[:, pl.ds(pl.multiple_of(ROWS * (sc[1] ^ r), ROWS), ROWS), :] = bias[r].astype(F32)
-    for h in range(HEADS):
-        bias_t[h] = bias_rows[h].T
-    n_rows = z_in.shape[0]
+STEPS = 6
+
+
+def attention_kernel(n, fresh, sc, *refs):
+    z_refs, bias_refs = refs[:n], refs[n:2 * n]
+    mask_in, norms, w_all, w_proj = refs[2 * n:2 * n + 4]
+    rest = refs[2 * n + (4 if fresh else 5):]
+    (out, z_in, z_out, mask_i, mask, bias_rows, bias_t, q_s, k_s, v_s, g_s, vn_s, gn_s, keep_s, s_buf, e_buf, p_s,
+     top_s, inv_s, o_s, m_sem, z_sem, o_sem) = rest
+    n_rows = n * ROWS
+
+    def z_copy(j):
+        return pltpu.make_async_copy(z_refs[j], z_in.at[pl.ds(ROWS * j, ROWS)], z_sem.at[j])
+
+    def m_copy(j):
+        return pltpu.make_async_copy(mask_in.at[sc[j]], mask_i.at[pl.ds(ROWS * j, ROWS)], m_sem.at[j])
+
+    def o_copy(j):
+        return pltpu.make_async_copy(z_out.at[pl.ds(ROWS * j, ROWS)], out.at[sc[j]], o_sem.at[j])
+
+    for j in range(n):
+        m_copy(j).start()
+        z_copy(j).start()
+    for j in range(n):
+        for r in range(4):
+            bias_rows[j, :, pl.ds(pl.multiple_of(ROWS * (sc[n + j] ^ r), ROWS), ROWS), :] = bias_refs[j][r].astype(F32)
+    for j in range(n):
+        m_copy(j).wait()
+    z_copy(0).wait()
+    mask[...] = mask_i[...].astype(F32)
+    q_s[...] = jnp.zeros_like(q_s)
+
+    @pl.loop(0, n * HEADS)
+    def _(h):
+        bias_t[h // HEADS, h % HEADS] = bias_rows[h // HEADS, h % HEADS].T
 
     def project(row, slot):
-        row = jnp.clip(row, 0, n_rows - 1)
-        normed = channel_norm(z_in[row], norms[0], norms[1], 0).astype(BF16)
+        row = jnp.minimum(row, n_rows - 1)
+        normed = channel_norm(z_in[row], (norms[0], norms[1])).astype(BF16)
         proj = mm(w_all[...], normed)
         k_s[slot] = proj[CH:2 * CH].T.astype(BF16)
         q = proj[:CH].astype(BF16)
@@ -361,8 +414,8 @@
         gn_s[slot] = sigmoid(proj[3 * CH:])
 
     def keep_mask(row, slot):
-        row = jnp.clip(row, 0, n_rows - 1)
-        keep_s[slot] = jnp.broadcast_to(mask[pl.ds(row, 1), :], (128, COLS)).T
+        row = jnp.minimum(row, n_rows - 1)
+        keep_s[slot] = jnp.broadcast_to(mask[pl.ds(row, 1), :], (LANES, COLS)).T
 
     def fold(part, op):
         out = part[:8]
@@ -377,20 +430,20 @@
         heads = slice(HEAD * h, HEAD * h + HEAD)
         o_s[slot, heads] = mm(v_s[slot, heads], probs)
 
-    def step(slot, h, logits, defer=False):
+    def step(row, slot, h, logits, defer):
         buf, prev = h % 2, (h + 1) % 2
+        sample = jnp.clip(row, 0, n_rows - 1) // ROWS
         top, total, probs = None, None, []
         for c in range(COLS // CHUNK):
             rows = slice(CHUNK * c, CHUNK * c + CHUNK)
-            scale = (e_buf[buf, rows] * jnp.concatenate([inv_s[buf]] * (CHUNK // 8), axis=0)).astype(BF16)
-            probs.append(scale)
+            probs.append((e_buf[buf, rows] * jnp.concatenate([inv_s[buf]] * (CHUNK // 8), axis=0)).astype(BF16))
             exps = jnp.exp(s_buf[prev, rows] - jnp.concatenate([top_s[prev]] * (CHUNK // 8), axis=0))
             e_buf[prev, rows] = exps
             part = fold(exps, jnp.add)
             total = part if total is None else total + part
             keep = keep_s[slot, rows]
             keep = jnp.concatenate([keep, keep], axis=1) > 0
-            vals = jnp.where(keep, logits[rows] + bias_t[h, rows], MASK_FILL)
+            vals = jnp.where(keep, logits[rows] + bias_t[sample, h, rows], MASK_FILL)
             s_buf[buf, rows] = vals
             part = fold(vals, jnp.maximum)
             top = part if top is None else jnp.maximum(top, part)
@@ -402,63 +455,70 @@
             weigh(1 - slot if h < 2 else slot, (h - 2) % HEADS, jnp.concatenate(probs, axis=0))
 
     def finish(row, slot):
-        row = jnp.clip(row, 0, n_rows - 1)
         gated = (g_s[slot] * o_s[slot]).astype(BF16)
-        z_out[row] = z_in[row] + mm(w_proj[...], gated)
-
-    q_s[...] = jnp.zeros_like(q_s)
+        z_out[jnp.maximum(row, 0)] = z_in[jnp.clip(row, 0, n_rows - 1)] + mm(w_proj[...], gated)
+
     project(0, 0)
     keep_mask(0, 0)
-
-    @pl.loop(0, n_rows // 2 + 1)
-    def _(pair):
-        first = 2 * pair - 1
+    n_steps = (n_rows + 2 + STEPS - 1) // STEPS
+
+    @pl.loop(0, n_steps)
+    def _(it):
+        first = STEPS * it - 1
         lg = scores(1, 0)
         weigh(0, 1, p_s[...])
-        for slot in (1, 0):
-            row = first + 1 - slot
+        for k in range(STEPS):
+            row, slot, last = first + k, 1 - k % 2, k == STEPS - 1
             for h in range(HEADS):
-                nxt = scores(slot, h + 1) if h < HEADS - 1 else (scores(0, 0) if slot else None)
+                nxt = scores(slot, h + 1) if h < HEADS - 1 else (None if last else scores(1 - slot, 0))
                 if h == 2:
                     project(row + 2, slot)
-                step(slot, h, lg, defer=slot == 0 and h == 3)
+                step(row, slot, h, lg, last and h == HEADS - 1)
                 lg = nxt
-                if h == 2:
+                if h == 3:
                     finish(row - 1, 1 - slot)
                     v_s[1 - slot] = vn_s[1 - slot]
                     g_s[1 - slot] = gn_s[1 - slot]
             keep_mask(row + 2, slot)
-
-
-def a_call(sc, z_in, mask, bias, norms, w_all, w_proj, out):
-    full = lambda a: pl.BlockSpec(a.shape, lambda i, sc: (0,) * a.ndim)
-    fresh = out is None
-    call = pl.pallas_call(
-        a_first if fresh else a_kernel,
+        for j in range(1, n):
+            @pl.when(it == (ROWS * j - 1) // STEPS - 1)
+            def _():
+                z_copy(j).wait()
+
+            @pl.when(it == (ROWS * j + 1) // STEPS)
+            def _():
+                o_copy(j - 1).start()
+
+    o_copy(n - 1).start()
+    for j in range(n):
+        o_copy(j).wait()
+
+
+def attend(sc, z_parts, biases, mask, norms, w_all, w_proj, out):
+    n, fresh = len(z_parts), out is None
+    args = (sc, *z_parts, *biases, mask, norms, w_all, w_proj) + (() if fresh else (out,))
+    rows = n * ROWS
+    pair = pltpu.VMEM((SLOTS, CH, COLS), BF16)
+    wide = pltpu.VMEM((SLOTS, CH, COLS), F32)
+    square = pltpu.VMEM((SLOTS, COLS, COLS), F32)
+    each = pltpu.VMEM((n, HEADS, COLS, COLS), F32)
+    line = pltpu.VMEM((SLOTS, 8, COLS), F32)
+    sems = pltpu.SemaphoreType.DMA((n,))
+    return pl.pallas_call(
+        functools.partial(attention_kernel, n, fresh),
         out_shape=jax.ShapeDtypeStruct((mask.shape[0], ROWS, CH, COLS), F32),
-        grid_spec=pltpu.PrefetchScalarGridSpec(
-            num_scalar_prefetch=1, grid=(1,),
-            in_specs=[full(z_in), pl.BlockSpec((1, ROWS, COLS), lambda i, sc: (sc[0], 0, 0)),
-                      full(bias), full(norms), full(w_all), full(w_proj)] + ([] if fresh else [HB]),
-            out_specs=pl.BlockSpec((1, ROWS, CH, COLS), lambda i, sc: (sc[0], 0, 0, 0)),
-            scratch_shapes=[
-                pltpu.VMEM((ROWS, COLS), F32), pltpu.VMEM((HEADS, COLS, COLS), F32), pltpu.VMEM((HEADS, COLS, COLS), F32),
-                pltpu.VMEM((SLOTS, HEADS, CH, COLS), BF16), pltpu.VMEM((SLOTS, COLS, CH), BF16),
-                pltpu.VMEM((SLOTS, CH, COLS), BF16), pltpu.VMEM((SLOTS, CH, COLS), F32), pltpu.VMEM((SLOTS, CH, COLS), BF16),
-                pltpu.VMEM((SLOTS, CH, COLS), F32), pltpu.VMEM((SLOTS, COLS, 128), F32), pltpu.VMEM((2, COLS, COLS), F32),
-                pltpu.VMEM((2, COLS, COLS), F32), pltpu.VMEM((COLS, COLS), BF16), pltpu.VMEM((2, 8, COLS), F32),
-                pltpu.VMEM((2, 8, COLS), F32), pltpu.VMEM((SLOTS, CH, COLS), F32),
-            ]),
-        compiler_params=pltpu.CompilerParams(vmem_limit_bytes=48 << 20, dimension_semantics=("arbitrary",)),
-        input_output_aliases={} if fresh else {7: 0},
+        in_specs=[SM] + [HB] * n + [VM] * n + [HB] + [VM] * 3 + ([] if fresh else [HB]),
+        out_specs=HB,
+        scratch_shapes=[
+            pltpu.VMEM((rows, CH, COLS), F32), pltpu.VMEM((rows + STEPS, CH, COLS), F32), pltpu.VMEM((rows, COLS), jnp.int32),
+            pltpu.VMEM((rows, COLS), F32), each, each, pltpu.VMEM((SLOTS, HEADS, CH, COLS), BF16),
+            pltpu.VMEM((SLOTS, COLS, CH), BF16), pair, wide, pair, wide, pltpu.VMEM((SLOTS, COLS, LANES), F32),
+            square, square, pltpu.VMEM((COLS, COLS), BF16), line, line, wide, sems, sems, sems,
+        ],
+        compiler_params=pltpu.CompilerParams(vmem_limit_bytes=48 << 20),
+        input_output_aliases={} if fresh else {len(args) - 1: 0},
         name="triangle_attention",
-    )
-    args = (sc, z_in, mask, bias, norms, w_all, w_proj)
-    return call(*args) if fresh else call(*args, out)
-
-
-def a_first(sc, z_in, mask_in, bias, norms, w_all, w_proj, out_ref, *scratch):
-    a_kernel(sc, z_in, mask_in, bias, norms, w_all, w_proj, None, out_ref, *scratch)
+    )(*args)
 
 
 def exchange(values, r):
@@ -514,37 +574,35 @@
             token[0] = jax.tree.leaves(res)[-1]
             return res
 
+        def attention(jobs, out):
+            samples, orders, z_parts, biases = zip(*jobs)
+            return ordered(attend, samples + orders, z_parts, biases, pair_mask, att_norms, w_all, w_out, out)
+
         far = [(t, r) for t in range(n_own) for r in (2, 3)]
         a_far, b_far = ordered(l1_call, [n_own * (me ^ r) + t for t, r in far], zt, pair_mask, norms, w_ab)
         b_par = exchange(b_far, 1)
         x_near = ordered(l2_call, [me], a_far, b_far, b_par, xgs)
 
         out = None
-        held = []
+        held, waiting = [], []
         for t in range(n_own):
-            z_own, z_par, bias, *far_x = ordered(u_call, [me, n_own * me + t], zt, arrived[t], [m[t] for m in masks],
-                                                 norms, xgs, w_ab, w_sq, w_bias8)
-            got = {}
-            bias_blk = {2: lax.dynamic_index_in_dim(bias, me, 0, keepdims=False),
-                        3: lax.dynamic_index_in_dim(bias, me ^ 1, 0, keepdims=False)}
-            z_near, bias_near = exchange(z_par, 1), exchange(bias, 1)
-            for r in (2, 3):
-                got[r] = [exchange(v, r) for v in (bias_blk[r], far_x[r - 2], far_x[r])]
-            held.append(got)
-            out = ordered(a_call, [n_own * me + t, 0], z_own, pair_mask, bias, att_norms, w_all, w_out, out)
-            out = ordered(a_call, [n_own * (me ^ 1) + t, 0], z_near, pair_mask, bias_near, att_norms, w_all, w_out, out)
+            z_own, z_par, bias, far2, far3 = ordered(u_call, [me, n_own * me + t], zt, arrived[t],
+                                                     [m[t] for m in masks], norms, xgs, w_ab, w_sq, w_bias8)
+            held.append({2: exchange(far2, 2), 3: exchange(far3, 3)})
+            near = (n_own * (me ^ 1) + t, 0, exchange(z_par, 1), exchange(bias, 1))
+            out = attention(waiting + [(n_own * me + t, 0, z_own, bias)], out)
+            waiting = [near]
         for t in range(n_own):
             mine, z_two = {}, {}
             for r in (2, 3):
-                bias_far, x_far, xi = held[t][r]
-                z_two[r], bias_own = ordered(r_call, [me, n_own * (me ^ r) + t, far.index((t, r))], zt, x_near, x_far, xi,
-                                             norms, w_sq, w_bias8)
-                mine[r] = (bias_own, bias_far)
-            both = jnp.stack([*mine[3], *mine[2]])
-            par = exchange(both, 1)
-            for r in (2, 3):
-                bias = jnp.stack([mine[r][0], par[2 * r - 4], mine[r][1], par[2 * r - 3]])
-                out = ordered(a_call, [n_own * (me ^ r) + t, me], z_two[r], pair_mask, bias, att_norms, w_all, w_out, out)
+                z_two[r], bias_own = ordered(r_call, [me, n_own * (me ^ r) + t, far.index((t, r))], zt, x_near,
+                                             held[t][r], norms, w_sq, w_bias8)
+                mine[r] = (bias_own, held[t][r][FAR_BIAS:])
+            par = exchange(jnp.stack([*mine[3], *mine[2]]), 1)
+            out = attention(waiting + [
+                (n_own * (me ^ r) + t, me, z_two[r], jnp.stack([mine[r][0], par[2 * r - 4], mine[r][1], par[2 * r - 3]]))
+                for r in (2, 3)], out)
+            waiting = []
         return jnp.transpose(out, (0, 1, 3, 2))
 
     pair_spec = P('data', 'dap')

time: 1510 us -> 1190 us (0.79)
  waiting for transfers between devices: 569 us -> 299 us
  Pallas kernels: 814 us -> 787 us
    ppermute x40 -> x28, waiting for transfers between devices: 569 us -> 299 us  [exchange(): return lax.ppermute(values, 'dap', [(i, i ^ r) for i in range(4)])]
    pallas_call x12 -> x6, Pallas kernels: 415 us -> 390 us  [attend(): pl.pallas_call(functools.partial(attention_kernel, n, fresh), out_shape=j...]
    unnamed x145 -> x109, local copies, waits for them, and re-layouts: 43.4 us -> 27.7 us
  transfers between devices with their start and end apart: 40 -> 28, of which waited for: 16 -> 9; matrix products, arithmetic and copies ran while one was open for 2% -> 3% of each run, Pallas kernels for 29% -> 51%
where the time goes in v1:
time: 1190 us; the launch traced here: 1180 us
  Pallas kernels  787 us (66%)
  waiting for transfers between devices  299 us (25%)
  local copies, waits for them, and re-layouts  68.3 us (6%)
  starting transfers between devices  24.4 us (2%)
    pallas_call x6, Pallas kernels, attend(): pl.pallas_call(functools.partial(attention_kernel, n, fresh), out_shape=j...  390 us
    ppermute x28, waiting for transfers between devices, exchange(): return lax.ppermute(values, 'dap', [(i, i ^ r) for i in range(4)])  299 us
    pallas_call x3, Pallas kernels, u_call(): pl.pallas_call(u_kernel, out_shape=(ROW_WIDE, ROW_WIDE, jax.ShapeDtypeStr...  278 us
    pallas_call x6, Pallas kernels, r_call(): pl.pallas_call(r_kernel, out_shape=(ROW_WIDE, jax.ShapeDtypeStruct((4, RO...  57.5 us
    pallas_call x1, Pallas kernels, l2_call(): pl.pallas_call(l2_kernel, grid=(n // 2,), out_shape=jax.ShapeDtypeStruct(...  32.9 us
    squeeze x3, local copies, waits for them, and re-layouts, local_block(): lax.dynamic_index_in_dim(zt_t, n_own * (me ^ r) + t, 0, keepdims=False)  29.2 us
    pallas_call x1, Pallas kernels, l1_call(): pl.pallas_call(l1_kernel, out_shape=(ab, ab), grid_spec=pltpu.PrefetchSca...  28.7 us
    unnamed x109, local copies, waits for them, and re-layouts  27.7 us
  transfers between devices with their start and end apart: 28, of which 9 were waited for; matrix products, arithmetic and copies ran while one was open for 3% of the time, Pallas kernels for 51%

profile of v1, /device:TPU:0, one launch (start us, length us, event | category | flops | bytes accessed | tf_op | source)
XLA Modules:
  0.0 1184.8 jit_solution(2480670849152289308)
XLA Ops:
  0.0 1.2 convert_element_type.3
  1.4 9.8 dynamic-slice_bitcast_fusion.6
  12.7 28.7 %near_projections.1 = (bf16[6,64,64,256]{3,2,1,0:T(8,128)(2,1)S(1)}, bf16[6,64,64,256]{3,2,1,0:T(8,128)(2,1)}) custom-call(s32[6]{0:T(128)S(1)} %stack.248.ids, f32[12,64,64,256]{3,2,1,0:T(8,128)} %bitcast.148, s32[12,64,256]{2,1,0:T(8,128)S(1)} %copy-done.2, f32[6,64,256]{2,1,0:T(8,128)S(1)} %broadcast_dynamic-update-slice_fusion.norms, ...), custom_call_target="tpu_custom_call" | custom-call | tf_op jit(solution)/shard_map/near_projections/pallas_call | solution.py:266
  41.5 4.6 copy-done.6
  46.0 0.8 collective-permute-start
  46.9 3.0 collective-permute-start.2
  50.0 22.0 %collective-permute-done.4 = bf16[3,64,256]{2,1,0:T(8,128)(2,1)S(1)} collective-permute-done((bf16[3,64,256]{2,1,0:T(8,128)(2,1)S(1)}, bf16[3,64,256]{2,1,0:T(8,128)(2,1)S(1)}, u32[]{:S(2)}, u32[]{:S(2)}) %collective-permute-start.4) | collective-permute-done | bytes 98336 | tf_op jit(solution)/shard_map/ppermute | solution.py:525
  72.0 2.9 collective-permute-start.5
  74.8 157.9 %collective-permute-done.5 = bf16[3,64,256]{2,1,0:T(8,128)(2,1)S(1)} collective-permute-done((bf16[3,64,256]{2,1,0:T(8,128)(2,1)S(1)}, bf16[3,64,256]{2,1,0:T(8,128)(2,1)S(1)}, u32[]{:S(2)}, u32[]{:S(2)}) %collective-permute-start.5) | collective-permute-done | bytes 98336 | tf_op jit(solution)/shard_map/ppermute | solution.py:525
  233.3 9.7 dynamic-slice_bitcast_fusion.3
  243.0 1.4 collective-permute-start.7
  244.7 1.1 collective-permute-start.9
  245.8 9.7 dynamic-slice_bitcast_fusion
  255.5 0.8 collective-permute-start.12
  258.3 1.1 collective-permute-start.14
  263.3 32.9 %near_product.1.x_near = bf16[6,64,64,128]{3,2,1,0:T(8,128)(2,1)S(1)} custom-call(s32[1]{0:T(128)} %bitcast.2.sc, bf16[6,64,64,256]{3,2,1,0:T(8,128)(2,1)} %copy-done.6, bf16[6,64,64,256]{3,2,1,0:T(8,128)(2,1)} %get-tuple-element.108.b_own, bf16[6,64,64,256]{3,2,1,0:T(8,128)(2,1)} %collective-permute-done.b_par, f32[4,64,8,128]{3,2,1,0:T(8,128)S(1)} %pad_maximum_fusion.xgs), custom_call_target="tpu_custom_call" | custom-call | tf_op jit(solution)/shard_map/near_product/pallas_call | solution.py:303
  296.2 2.6 copy-done
  298.8 92.5 %pair_updates.3 = (f32[64,64,256]{2,1,0:T(8,128)}, f32[64,64,256]{2,1,0:T(8,128)}, bf16[4,4,64,256]{3,2,1,0:T(8,128)(2,1)}, bf16[100,64,256]{2,1,0:T(8,128)(2,1)}, bf16[100,64,256]{2,1,0:T(8,128)(2,1)}) custom-call(s32[2]{0:T(128)} %pad_add_fusion.11.sc, f32[12,64,64,256]{3,2,1,0:T(8,128)} %bitcast.151, f32[64,64,256]{2,1,0:T(8,128)} %collective-permute-done.1.zr1, ...), custom_call_target="tpu_custom_call" | custom-call | tf_op jit(solution)/shard_map/pair_updates/pallas_call | solution.py:231
  391.4 0.8 collective-permute-start.10
  392.9 33.2 %collective-permute-done.9.zr3 = f32[64,64,256]{2,1,0:T(8,128)} collective-permute-done((f32[64,64,256]{2,1,0:T(8,128)}, f32[64,64,256]{2,1,0:T(8,128)}, u32[]{:S(2)}, u32[]{:S(2)}) %collective-permute-start.9) | collective-permute-done | bytes 4194336 | tf_op jit(solution)/shard_map/ppermute | solution.py:525
  426.1 1.4 collective-permute-start.17
  428.2 2.2 copy-done.14
  430.4 1.0 copy-done.19
  431.5 33.6 %triangle_attention.6.refs_8_ = f32[12,64,64,256]{3,2,1,0:T(8,128)} custom-call(s32[2]{0:T(128)S(1)} %pad_add_fusion.10.sc, f32[64,64,256]{2,1,0:T(8,128)S(1)} %copy-done.14, bf16[4,4,64,256]{3,2,1,0:T(8,128)(2,1)S(1)} %copy-done.19, s32[12,64,256]{2,1,0:T(8,128)S(1)} %copy-done.2, f32[2,64,256]{2,1,0:T(8,128)S(1)} %pad_maximum_fusion.11.refs_3_.refs_5_.refs_7_, ...), custom_call_target="tpu_custom_call" | custom-call | tf_op jit(solution)/shard_map/triangle_attention/pallas_call | solution.py:507
  465.0 92.6 %pair_updates.4 = (f32[64,64,256]{2,1,0:T(8,128)}, f32[64,64,256]{2,1,0:T(8,128)}, bf16[4,4,64,256]{3,2,1,0:T(8,128)(2,1)}, bf16[100,64,256]{2,1,0:T(8,128)(2,1)}, bf16[100,64,256]{2,1,0:T(8,128)(2,1)}) custom-call(s32[2]{0:T(128)} %pad_add_fusion.9.sc, f32[12,64,64,256]{3,2,1,0:T(8,128)} %bitcast.152, f32[64,64,256]{2,1,0:T(8,128)} %collective-permute-done.7.zr1, ...), custom_call_target="tpu_custom_call" | custom-call | tf_op jit(solution)/shard_map/pair_updates/pallas_call | solution.py:231
  557.9 0.9 collective-permute-start.18
  558.8 47.0 %collective-permute-done.14.zr3 = f32[64,64,256]{2,1,0:T(8,128)} collective-permute-done((f32[64,64,256]{2,1,0:T(8,128)}, f32[64,64,256]{2,1,0:T(8,128)}, u32[]{:S(2)}, u32[]{:S(2)}) %collective-permute-start.14) | collective-permute-done | bytes 4194336 | tf_op jit(solution)/shard_map/ppermute | solution.py:525
  605.9 1.7 collective-permute-start.11
  607.6 1.5 collective-permute-done.11.refs_2_
  610.5 1.0 copy-done.18
  611.5 65.3 %triangle_attention.7.refs_8_ = f32[12,64,64,256]{3,2,1,0:T(8,128)} custom-call(s32[4]{0:T(128)S(1)} %get-tuple-element.142.sc, f32[64,64,256]{2,1,0:T(8,128)} %collective-permute-done.10.refs_0_, f32[64,64,256]{2,1,0:T(8,128)} %get-tuple-element.144.refs_1_, ...), custom_call_target="tpu_custom_call", output_to_operand_aliasing={{}: (9, {})} | custom-call | tf_op jit(solution)/shard_map/triangle_attention/pallas_call | solution.py:507
  676.8 92.4 %pair_updates.5 = (f32[64,64,256]{2,1,0:T(8,128)}, f32[64,64,256]{2,1,0:T(8,128)}, bf16[4,4,64,256]{3,2,1,0:T(8,128)(2,1)}, bf16[100,64,256]{2,1,0:T(8,128)(2,1)}, bf16[100,64,256]{2,1,0:T(8,128)(2,1)}) custom-call(s32[2]{0:T(128)} %pad_add_fusion.8.sc, f32[12,64,64,256]{3,2,1,0:T(8,128)} %bitcast.153, f32[64,64,256]{2,1,0:T(8,128)} %collective-permute-done.12.zr1, ...), custom_call_target="tpu_custom_call" | custom-call | tf_op jit(solution)/shard_map/pair_updates/pallas_call | solution.py:231
  769.3 1.4 collective-permute-start.23
  770.7 0.7 collective-permute-start.25
  772.6 0.9 slice_bitcast_fusion.4
  773.5 0.9 slice_bitcast_fusion.5
  774.4 1.0 copy-done.16
  775.5 65.3 %triangle_attention.8.refs_10_ = f32[12,64,64,256]{3,2,1,0:T(8,128)} custom-call(s32[4]{0:T(128)S(1)} %get-tuple-element.152.sc, f32[64,64,256]{2,1,0:T(8,128)} %collective-permute-done.15.refs_0_, f32[64,64,256]{2,1,0:T(8,128)} %get-tuple-element.154.refs_1_, ...), custom_call_target="tpu_custom_call", output_to_operand_aliasing={{}: (9, {})} | custom-call | tf_op jit(solution)/shard_map/triangle_attention/pallas_call | solution.py:507
  840.8 2.8 copy-done.1
  843.6 9.4 row_updates.6
  853.0 2.0 copy-done.8
  855.0 10.1 row_updates.7
  865.1 2.0 copy-done.9
  867.2 0.8 collective-permute-start.21
  868.0 0.9 slice_bitcast_fusion.2
  868.9 17.8 %collective-permute-done.23.x_far.xi = bf16[100,64,256]{2,1,0:T(8,128)(2,1)} collective-permute-done((bf16[100,64,256]{2,1,0:T(8,128)(2,1)}, bf16[100,64,256]{2,1,0:T(8,128)(2,1)}, u32[]{:S(2)}, u32[]{:S(2)}) %collective-permute-start.23) | collective-permute-done | bytes 3276832 | tf_op jit(solution)/shard_map/ppermute | solution.py:525
  886.7 1.7 collective-permute-start.20
  888.5 0.9 slice_bitcast_fusion.3
  890.0 95.5 %triangle_attention.9.refs_8_ = f32[12,64,64,256]{3,2,1,0:T(8,128)} custom-call(s32[6]{0:T(128)S(1)} %stack.234.sc, f32[64,64,256]{2,1,0:T(8,128)} %collective-permute-done.19.refs_0_, f32[64,64,256]{2,1,0:T(8,128)} %copy-done.8, f32[64,64,256]{2,1,0:T(8,128)} %copy-done.9, ...), custom_call_target="tpu_custom_call", output_to_operand_aliasing={{}: (11, {})} | custom-call | tf_op jit(solution)/shard_map/triangle_attention/pallas_call | solution.py:507
  985.6 9.5 row_updates.8
  995.0 2.0 copy-done.10
  997.1 9.5 row_updates.9
  1006.5 2.0 copy-done.12
  1009.1 0.9 slice_bitcast_fusion
  1010.0 17.2 %collective-permute-done.26.x_far.xi = bf16[100,64,256]{2,1,0:T(8,128)(2,1)} collective-permute-done((bf16[100,64,256]{2,1,0:T(8,128)(2,1)}, bf16[100,64,256]{2,1,0:T(8,128)(2,1)}, u32[]{:S(2)}, u32[]{:S(2)}) %collective-permute-start.26) | collective-permute-done | bytes 3276832 | tf_op jit(solution)/shard_map/ppermute | solution.py:525
  1027.2 0.9 slice_bitcast_fusion.1
  1028.3 65.3 %triangle_attention.10.refs_8_ = f32[12,64,64,256]{3,2,1,0:T(8,128)} custom-call(s32[4]{0:T(128)S(1)} %add_add_fusion.1.sc, f32[64,64,256]{2,1,0:T(8,128)} %copy-done.10, f32[64,64,256]{2,1,0:T(8,128)} %copy-done.12, bf16[4,4,64,256]{3,2,1,0:T(8,128)(2,1)S(1)} %pad_maximum_fusion.8.refs_2_, ...), custom_call_target="tpu_custom_call", output_to_operand_aliasing={{}: (9, {})} | custom-call | tf_op jit(solution)/shard_map/triangle_attention/pallas_call | solution.py:507
  1093.6 9.6 row_updates.10
  1103.3 2.0 copy-done.11
  1105.3 9.5 row_updates.11
  1114.7 2.0 copy-done.13
  1116.8 0.8 collective-permute-start.27
  1117.7 1.5 collective-permute-done.27
  1119.3 65.3 %triangle_attention.11 = f32[12,64,64,256]{3,2,1,0:T(8,128)} custom-call(s32[4]{0:T(128)S(1)} %add_add_fusion.sc, f32[64,64,256]{2,1,0:T(8,128)} %copy-done.11, f32[64,64,256]{2,1,0:T(8,128)} %copy-done.13, bf16[4,4,64,256]{3,2,1,0:T(8,128)(2,1)S(1)} %pad_maximum_fusion.9.refs_2_, ...), custom_call_target="tpu_custom_call", output_to_operand_aliasing={{}: (9, {})} | custom-call | tf_op jit(solution)/shard_map/triangle_attention/pallas_call | solution.py:507
  (196 shorter events, 14.1 us)
Async XLA Ops:
  1.3 10.3 copy-start.24
  1.3 10.4 copy-start.25
  1.3 10.5 copy-start.26
  1.3 10.5 copy-start.27
  1.3 10.6 copy-start.28
  1.3 10.7 copy-start.29
  1.3 10.8 copy-start.43
  1.3 10.9 copy-start.44
  1.4 11.0 copy-start.45
  1.4 11.0 copy-start.40
  1.4 11.1 copy-start.39
  1.4 11.4 copy-start.2
  12.6 28.9 %copy-start.3 = (f32[6,64,256]{2,1,0:T(8,128)}, f32[6,64,256]{2,1,0:T(8,128)S(1)}, u32[]{:S(2)}) copy-start(f32[6,64,256]{2,1,0:T(8,128)S(1)} %broadcast_dynamic-update-slice_fusion.norms) | copy-start | bytes 1179652
  12.6 28.8 %copy-start.15 = (bf16[2,256,64]{2,1,0:T(8,128)(2,1)}, bf16[2,256,64]{2,1,0:T(8,128)(2,1)S(1)}, u32[]{:S(2)}) copy-start(bf16[2,256,64]{2,1,0:T(8,128)(2,1)S(1)} %pad_maximum_fusion.10.w_ab) | copy-start | bytes 196612
  46.0 212.3 %collective-permute-start = (bf16[6,64,64,256]{3,2,1,0:T(8,128)(2,1)}, bf16[6,64,64,256]{3,2,1,0:T(8,128)(2,1)}, u32[]{:S(2)}, u32[]{:S(2)}) collective-permute-start(bf16[6,64,64,256]{3,2,1,0:T(8,128)(2,1)} %get-tuple-element.108.b_own), channel_id=1, source_target_pairs={{0,1},{1,0},{2,3},{3,2},{4,5},{5,4},{6,7},{7,6}} | collective-permute-start | bytes 37748744 | tf_op jit(solution)/shard_map/ppermute | solution.py:525
  46.9 197.5 %collective-permute-start.1 = (f32[64,64,256]{2,1,0:T(8,128)}, f32[64,64,256]{2,1,0:T(8,128)}, u32[]{:S(2)}, u32[]{:S(2)}) collective-permute-start(f32[64,64,256]{2,1,0:T(8,128)} %get-tuple-element.116), channel_id=1, source_target_pairs={{0,1},{1,0},{2,3},{3,2},{4,5},{5,4},{6,7},{7,6}} | collective-permute-start | bytes 12582920 | tf_op jit(solution)/shard_map/ppermute | solution.py:525
  46.9 197.8 %collective-permute-start.2 = (f32[64,64,256]{2,1,0:T(8,128)}, f32[64,64,256]{2,1,0:T(8,128)}, u32[]{:S(2)}, u32[]{:S(2)}) collective-permute-start(f32[64,64,256]{2,1,0:T(8,128)} %get-tuple-element.93), channel_id=1, source_target_pairs={{0,2},{1,3},{2,0},{3,1},{4,6},{5,7},{6,4},{7,5}} | collective-permute-start | bytes 12582920 | tf_op jit(solution)/shard_map/ppermute | solution.py:525
  49.8 205.7 %collective-permute-start.3 = (f32[64,64,256]{2,1,0:T(8,128)}, f32[64,64,256]{2,1,0:T(8,128)}, u32[]{:S(2)}, u32[]{:S(2)}) collective-permute-start(f32[64,64,256]{2,1,0:T(8,128)} %get-tuple-element.117), channel_id=1, source_target_pairs={{0,3},{1,2},{2,1},{3,0},{4,7},{5,6},{6,5},{7,4}} | collective-permute-start | bytes 12582920 | tf_op jit(solution)/shard_map/ppermute | solution.py:525
  49.8 22.1 %collective-permute-start.4 = (bf16[3,64,256]{2,1,0:T(8,128)(2,1)S(1)}, bf16[3,64,256]{2,1,0:T(8,128)(2,1)S(1)}, u32[]{:S(2)}, u32[]{:S(2)}) collective-permute-start(bf16[3,64,256]{2,1,0:T(8,128)(2,1)S(1)} %get-tuple-element.119), channel_id=1, source_target_pairs={{0,1},{1,0},{2,3},{3,2},{4,5},{5,4},{6,7},{7,6}} | collective-permute-start | bytes 294920 | tf_op jit(solution)/shard_map/ppermute | solution.py:525
  72.0 160.8 %collective-permute-start.5 = (bf16[3,64,256]{2,1,0:T(8,128)(2,1)S(1)}, bf16[3,64,256]{2,1,0:T(8,128)(2,1)S(1)}, u32[]{:S(2)}, u32[]{:S(2)}) collective-permute-start(bf16[3,64,256]{2,1,0:T(8,128)(2,1)S(1)} %get-tuple-element.120), channel_id=1, source_target_pairs={{0,2},{1,3},{2,0},{3,1},{4,6},{5,7},{6,4},{7,5}} | collective-permute-start | bytes 294920 | tf_op jit(solution)/shard_map/ppermute | solution.py:525
  232.8 10.2 collective-permute-start.6
  243.0 13.3 %collective-permute-start.7 = (f32[64,64,256]{2,1,0:T(8,128)}, f32[64,64,256]{2,1,0:T(8,128)}, u32[]{:S(2)}, u32[]{:S(2)}) collective-permute-start(f32[64,64,256]{2,1,0:T(8,128)} %get-tuple-element.138), channel_id=1, source_target_pairs={{0,1},{1,0},{2,3},{3,2},{4,5},{5,4},{6,7},{7,6}} | collective-permute-start | bytes 12582920 | tf_op jit(solution)/shard_map/ppermute | solution.py:525
  244.3 147.0 %collective-permute-start.8 = (f32[64,64,256]{2,1,0:T(8,128)}, f32[64,64,256]{2,1,0:T(8,128)}, u32[]{:S(2)}, u32[]{:S(2)}) collective-permute-start(f32[64,64,256]{2,1,0:T(8,128)} %get-tuple-element.139), channel_id=1, source_target_pairs={{0,2},{1,3},{2,0},{3,1},{4,6},{5,7},{6,4},{7,5}} | collective-permute-start | bytes 12582920 | tf_op jit(solution)/shard_map/ppermute | solution.py:525
  244.6 12.0 %copy-start.30 = (bf16[64,64]{1,0:T(8,128)(2,1)S(1)}, bf16[64,64]{1,0:T(8,128)(2,1)}, u32[]{:S(2)}) copy-start(bf16[64,64]{1,0:T(8,128)(2,1)} %param.51) | copy-start | bytes 24580
  244.6 12.1 %copy-start.31 = (bf16[64,64]{1,0:T(8,128)(2,1)S(1)}, bf16[64,64]{1,0:T(8,128)(2,1)}, u32[]{:S(2)}) copy-start(bf16[64,64]{1,0:T(8,128)(2,1)} %param.48) | copy-start | bytes 24580
  244.6 12.2 %copy-start.32 = (bf16[64,64]{1,0:T(8,128)(2,1)S(1)}, bf16[64,64]{1,0:T(8,128)(2,1)}, u32[]{:S(2)}) copy-start(bf16[64,64]{1,0:T(8,128)(2,1)} %param.41) | copy-start | bytes 24580
  244.6 12.3 %copy-start.33 = (bf16[64,64]{1,0:T(8,128)(2,1)S(1)}, bf16[64,64]{1,0:T(8,128)(2,1)}, u32[]{:S(2)}) copy-start(bf16[64,64]{1,0:T(8,128)(2,1)} %param.38) | copy-start | bytes 24580
  244.6 15.4 %copy-start.41 = (bf16[64,4]{0,1:T(4,128)(2,1)S(1)}, bf16[64,4]{0,1:T(4,128)(2,1)}, u32[]{:S(2)}) copy-start(bf16[64,4]{0,1:T(4,128)(2,1)} %param.57) | copy-start | bytes 1540
  244.7 16.0 %copy-start.46 = (f32[64]{0:T(128)S(1)}, f32[64]{0:T(128)}, u32[]{:S(2)}) copy-start(f32[64]{0:T(128)} %param.50) | copy-start | bytes 772
  244.7 16.1 %copy-start.47 = (f32[64]{0:T(128)S(1)}, f32[64]{0:T(128)}, u32[]{:S(2)}) copy-start(f32[64]{0:T(128)} %param.49) | copy-start | bytes 772
  244.7 16.2 %copy-start.48 = (f32[64]{0:T(128)S(1)}, f32[64]{0:T(128)}, u32[]{:S(2)}) copy-start(f32[64]{0:T(128)} %param.40) | copy-start | bytes 772
  244.7 16.4 %copy-start.49 = (f32[64]{0:T(128)S(1)}, f32[64]{0:T(128)}, u32[]{:S(2)}) copy-start(f32[64]{0:T(128)} %param.39) | copy-start | bytes 772
  244.7 181.4 %collective-permute-start.9 = (f32[64,64,256]{2,1,0:T(8,128)}, f32[64,64,256]{2,1,0:T(8,128)}, u32[]{:S(2)}, u32[]{:S(2)}) collective-permute-start(f32[64,64,256]{2,1,0:T(8,128)} %get-tuple-element.140), channel_id=1, source_target_pairs={{0,3},{1,2},{2,1},{3,0},{4,7},{5,6},{6,5},{7,4}} | collective-permute-start | bytes 12582920 | tf_op jit(solution)/shard_map/ppermute | solution.py:525
  255.5 302.1 %collective-permute-start.12 = (f32[64,64,256]{2,1,0:T(8,128)}, f32[64,64,256]{2,1,0:T(8,128)}, u32[]{:S(2)}, u32[]{:S(2)}) collective-permute-start(f32[64,64,256]{2,1,0:T(8,128)} %get-tuple-element.148), channel_id=1, source_target_pairs={{0,1},{1,0},{2,3},{3,2},{4,5},{5,4},{6,7},{7,6}} | collective-permute-start | bytes 12582920 | tf_op jit(solution)/shard_map/ppermute | solution.py:525
  256.3 301.6 %collective-permute-start.13 = (f32[64,64,256]{2,1,0:T(8,128)}, f32[64,64,256]{2,1,0:T(8,128)}, u32[]{:S(2)}, u32[]{:S(2)}) collective-permute-start(f32[64,64,256]{2,1,0:T(8,128)} %get-tuple-element.149), channel_id=1, source_target_pairs={{0,2},{1,3},{2,0},{3,1},{4,6},{5,7},{6,4},{7,5}} | collective-permute-start | bytes 12582920 | tf_op jit(solution)/shard_map/ppermute | solution.py:525
  258.3 347.5 %collective-permute-start.14 = (f32[64,64,256]{2,1,0:T(8,128)}, f32[64,64,256]{2,1,0:T(8,128)}, u32[]{:S(2)}, u32[]{:S(2)}) collective-permute-start(f32[64,64,256]{2,1,0:T(8,128)} %get-tuple-element.150), channel_id=1, source_target_pairs={{0,3},{1,2},{2,1},{3,0},{4,7},{5,6},{6,5},{7,4}} | collective-permute-start | bytes 12582920 | tf_op jit(solution)/shard_map/ppermute | solution.py:525
  261.3 34.9 %copy-start.5 = (f32[4,64,8,128]{3,2,1,0:T(8,128)}, f32[4,64,8,128]{3,2,1,0:T(8,128)S(1)}, u32[]{:S(2)}) copy-start(f32[4,64,8,128]{3,2,1,0:T(8,128)S(1)} %pad_maximum_fusion.xgs) | copy-start | bytes 3145732
  298.8 93.3 %copy-start.34 = (bf16[64,64]{1,0:T(8,128)(2,1)S(1)}, bf16[64,64]{1,0:T(8,128)(2,1)}, u32[]{:S(2)}) copy-start(bf16[64,64]{1,0:T(8,128)(2,1)} %param.54) | copy-start | bytes 24580
  298.8 128.8 %copy-start.35 = (bf16[64,64]{1,0:T(8,128)(2,1)S(1)}, bf16[64,64]{1,0:T(8,128)(2,1)}, u32[]{:S(2)}) copy-start(bf16[64,64]{1,0:T(8,128)(2,1)} %param.58) | copy-start | bytes 24580
  298.8 128.9 %copy-start.36 = (bf16[64,64]{1,0:T(8,128)(2,1)S(1)}, bf16[64,64]{1,0:T(8,128)(2,1)}, u32[]{:S(2)}) copy-start(bf16[64,64]{1,0:T(8,128)(2,1)} %param.56) | copy-start | bytes 24580
  298.8 129.0 %copy-start.37 = (bf16[64,64]{1,0:T(8,128)(2,1)S(1)}, bf16[64,64]{1,0:T(8,128)(2,1)}, u32[]{:S(2)}) copy-start(bf16[64,64]{1,0:T(8,128)(2,1)} %param.55) | copy-start | bytes 24580
  298.8 129.1 %copy-start.38 = (bf16[64,64]{1,0:T(8,128)(2,1)S(1)}, bf16[64,64]{1,0:T(8,128)(2,1)}, u32[]{:S(2)}) copy-start(bf16[64,64]{1,0:T(8,128)(2,1)} %param.59) | copy-start | bytes 24580
  391.4 218.1 %collective-permute-start.10 = (f32[64,64,256]{2,1,0:T(8,128)}, f32[64,64,256]{2,1,0:T(8,128)}, u32[]{:S(2)}, u32[]{:S(2)}) collective-permute-start(f32[64,64,256]{2,1,0:T(8,128)} %get-tuple-element.143), channel_id=1, source_target_pairs={{0,1},{1,0},{2,3},{3,2},{4,5},{5,4},{6,7},{7,6}} | collective-permute-start | bytes 12582920 | tf_op jit(solution)/shard_map/ppermute | solution.py:525
  426.1 343.2 %collective-permute-start.17 = (bf16[100,64,256]{2,1,0:T(8,128)(2,1)}, bf16[100,64,256]{2,1,0:T(8,128)(2,1)}, u32[]{:S(2)}, u32[]{:S(2)}) collective-permute-start(bf16[100,64,256]{2,1,0:T(8,128)(2,1)} %get-tuple-element.157), channel_id=1, source_target_pairs={{0,2},{1,3},{2,0},{3,1},{4,6},{5,7},{6,4},{7,5}} | collective-permute-start | bytes 9830408 | tf_op jit(solution)/shard_map/ppermute | solution.py:525
  465.0 140.8 %copy-start.20 = (bf16[4,4,64,256]{3,2,1,0:T(8,128)(2,1)S(1)}, bf16[4,4,64,256]{3,2,1,0:T(8,128)(2,1)}, u32[]{:S(2)}) copy-start(bf16[4,4,64,256]{3,2,1,0:T(8,128)(2,1)} %get-tuple-element.130.refs_1_) | copy-start | bytes 1572868
  557.6 213.8 %collective-permute-start.15 = (f32[64,64,256]{2,1,0:T(8,128)}, f32[64,64,256]{2,1,0:T(8,128)}, u32[]{:S(2)}, u32[]{:S(2)}) collective-permute-start(f32[64,64,256]{2,1,0:T(8,128)} %get-tuple-element.153), channel_id=1, source_target_pairs={{0,1},{1,0},{2,3},{3,2},{4,5},{5,4},{6,7},{7,6}} | collective-permute-start | bytes 12582920 | tf_op jit(solution)/shard_map/ppermute | solution.py:525
  557.9 212.8 %collective-permute-start.18 = (bf16[100,64,256]{2,1,0:T(8,128)(2,1)}, bf16[100,64,256]{2,1,0:T(8,128)(2,1)}, u32[]{:S(2)}, u32[]{:S(2)}) collective-permute-start(bf16[100,64,256]{2,1,0:T(8,128)(2,1)} %get-tuple-element.127), channel_id=1, source_target_pairs={{0,3},{1,2},{2,1},{3,0},{4,7},{5,6},{6,5},{7,4}} | collective-permute-start | bytes 9830408 | tf_op jit(solution)/shard_map/ppermute | solution.py:525
  605.9 3.3 collective-permute-start.11
  609.1 160.1 %collective-permute-start.16 = (bf16[4,4,64,256]{3,2,1,0:T(8,128)(2,1)}, bf16[4,4,64,256]{3,2,1,0:T(8,128)(2,1)S(1)}, u32[]{:S(2)}, u32[]{:S(2)}) collective-permute-start(bf16[4,4,64,256]{3,2,1,0:T(8,128)(2,1)} %get-tuple-element.145.refs_3_), channel_id=1, source_target_pairs={{0,1},{1,0},{2,3},{3,2},{4,5},{5,4},{6,7},{7,6}} | collective-permute-start | bytes 1572872 | tf_op jit(solution)/shard_map/ppermute | solution.py:525
  609.5 257.7 %collective-permute-start.22 = (bf16[100,64,256]{2,1,0:T(8,128)(2,1)}, bf16[100,64,256]{2,1,0:T(8,128)(2,1)}, u32[]{:S(2)}, u32[]{:S(2)}) collective-permute-start(bf16[100,64,256]{2,1,0:T(8,128)(2,1)} %get-tuple-element.166), channel_id=1, source_target_pairs={{0,2},{1,3},{2,0},{3,1},{4,6},{5,7},{6,4},{7,5}} | collective-permute-start | bytes 9830408 | tf_op jit(solution)/shard_map/ppermute | solution.py:525
  769.3 120.7 %collective-permute-start.19 = (f32[64,64,256]{2,1,0:T(8,128)}, f32[64,64,256]{2,1,0:T(8,128)}, u32[]{:S(2)}, u32[]{:S(2)}) collective-permute-start(f32[64,64,256]{2,1,0:T(8,128)} %get-tuple-element.162), channel_id=1, source_target_pairs={{0,1},{1,0},{2,3},{3,2},{4,5},{5,4},{6,7},{7,6}} | collective-permute-start | bytes 12582920 | tf_op jit(solution)/shard_map/ppermute | solution.py:525
  769.3 117.4 %collective-permute-start.23 = (bf16[100,64,256]{2,1,0:T(8,128)(2,1)}, bf16[100,64,256]{2,1,0:T(8,128)(2,1)}, u32[]{:S(2)}, u32[]{:S(2)}) collective-permute-start(bf16[100,64,256]{2,1,0:T(8,128)(2,1)} %get-tuple-element.141), channel_id=1, source_target_pairs={{0,3},{1,2},{2,1},{3,0},{4,7},{5,6},{6,5},{7,4}} | collective-permute-start | bytes 9830408 | tf_op jit(solution)/shard_map/ppermute | solution.py:525
  770.7 238.3 %collective-permute-start.25 = (bf16[100,64,256]{2,1,0:T(8,128)(2,1)}, bf16[100,64,256]{2,1,0:T(8,128)(2,1)}, u32[]{:S(2)}, u32[]{:S(2)}) collective-permute-start(bf16[100,64,256]{2,1,0:T(8,128)(2,1)} %get-tuple-element.174), channel_id=1, source_target_pairs={{0,2},{1,3},{2,0},{3,1},{4,6},{5,7},{6,4},{7,5}} | collective-permute-start | bytes 9830408 | tf_op jit(solution)/shard_map/ppermute | solution.py:525
  771.4 255.7 %collective-permute-start.26 = (bf16[100,64,256]{2,1,0:T(8,128)(2,1)}, bf16[100,64,256]{2,1,0:T(8,128)(2,1)}, u32[]{:S(2)}, u32[]{:S(2)}) collective-permute-start(bf16[100,64,256]{2,1,0:T(8,128)(2,1)} %get-tuple-element.151), channel_id=1, source_target_pairs={{0,3},{1,2},{2,1},{3,0},{4,7},{5,6},{6,5},{7,4}} | collective-permute-start | bytes 9830408 | tf_op jit(solution)/shard_map/ppermute | solution.py:525
  775.5 65.3 %copy-start.4 = (f32[6,64,256]{2,1,0:T(8,128)S(1)}, f32[6,64,256]{2,1,0:T(8,128)}, u32[]{:S(2)}) copy-start(f32[6,64,256]{2,1,0:T(8,128)} %copy-done.3) | copy-start | bytes 1179652
  775.5 65.3 %copy-start.7 = (bf16[4,64,64]{2,1,0:T(8,128)(2,1)S(1)}, bf16[4,64,64]{2,1,0:T(8,128)(2,1)}, u32[]{:S(2)}) copy-start(bf16[4,64,64]{2,1,0:T(8,128)(2,1)} %pad_maximum_fusion.12.w_sq) | copy-start | bytes 98308
  775.5 65.3 %copy-start.21 = (bf16[8,64]{1,0:T(8,128)(2,1)S(1)}, bf16[8,64]{1,0:T(8,128)(2,1)}, u32[]{:S(2)}) copy-start(bf16[8,64]{1,0:T(8,128)(2,1)} %concatenate.53.w_bias) | copy-start | bytes 3076
  855.0 31.8 %copy-start.17 = (bf16[4,4,64,256]{3,2,1,0:T(8,128)(2,1)S(1)}, bf16[4,4,64,256]{3,2,1,0:T(8,128)(2,1)}, u32[]{:S(2)}) copy-start(bf16[4,4,64,256]{3,2,1,0:T(8,128)(2,1)} %get-tuple-element.155.refs_3_) | copy-start | bytes 1572868
  855.0 130.6 %slice-start = ((s8[6291456]{0:T(1024)(128)(4,1)}), s8[4194304]{0:T(1024)(128)(4,1)S(1)}, s32[]{:S(2)}) async-start(s8[6291456]{0:T(1024)(128)(4,1)} %bitcast.128), calls=%async_computation | async-start | bytes 8388608
  867.2 22.2 %collective-permute-start.21 = (bf16[4,4,64,256]{3,2,1,0:T(8,128)(2,1)S(1)}, bf16[4,4,64,256]{3,2,1,0:T(8,128)(2,1)S(1)}, u32[]{:S(2)}, u32[]{:S(2)}) collective-permute-start(bf16[4,4,64,256]{3,2,1,0:T(8,128)(2,1)S(1)} %fusion.9), channel_id=1, source_target_pairs={{0,1},{1,0},{2,3},{3,2},{4,5},{5,4},{6,7},{7,6}} | collective-permute-start | bytes 1572872 | tf_op jit(solution)/shard_map/ppermute | solution.py:525
  886.7 3.3 collective-permute-start.20
  890.0 95.6 %slice-start.1 = ((s8[6291456]{0:T(1024)(128)(4,1)}), s8[2097152]{0:T(1024)(128)(4,1)S(1)}, s32[]{:S(2)}) async-start(s8[6291456]{0:T(1024)(128)(4,1)} %bitcast.128), calls=%async_computation.1 | async-start | bytes 4194304
  1008.6 19.5 %collective-permute-start.24 = (bf16[4,4,64,256]{3,2,1,0:T(8,128)(2,1)S(1)}, bf16[4,4,64,256]{3,2,1,0:T(8,128)(2,1)S(1)}, u32[]{:S(2)}, u32[]{:S(2)}) collective-permute-start(bf16[4,4,64,256]{3,2,1,0:T(8,128)(2,1)S(1)} %fusion.5), channel_id=1, source_target_pairs={{0,1},{1,0},{2,3},{3,2},{4,5},{5,4},{6,7},{7,6}} | collective-permute-start | bytes 1572872 | tf_op jit(solution)/shard_map/ppermute | solution.py:525
  1116.8 2.3 collective-permute-start.27
  (16 other events, 57.5 us)

commit v2 on v1

--- a/solution.py
+++ b/solution.py
@@ -68,7 +68,7 @@
                 held[k][i] = stage(i, held[k - 1].pop(i) if k else None)
 
 
-def u_kernel(sc, zt, zr1, zr2, zr3, mask0, mask1, mask2, mask3, norms, xgs, w_ab, w_sq, w_bias,
+def u_kernel(last, sc, zt, zr1, zr2, zr3, mask0, mask1, mask2, mask3, norms, xgs, w_ab, w_sq, w_bias,
              z2_own, z2_par, bias_out, far2, far3,
              z_s, a_s, b_s, x_s, mask, stats, tile_a, tile_b, tile_x, tile_c, tile_d, tile_z, in_sem, z_sem, x_sem):
     me, sample = sc[0], sc[1]
@@ -112,10 +112,11 @@
         side = pl.ds(pl.multiple_of(LANES * (q // 2), LANES), LANES)
         act = (lambda cp: cp.start()) if start else (lambda cp: cp.wait())
         for k, dst in ((0, z2_own), (1, z2_par), (2, far2), (3, far3)):
-            if k > 1 or not outgoing:
+            plain = k < 2 or (last and k == 3)
+            if not (outgoing and plain):
                 @pl.when(r == k)
                 def _():
-                    if k < 2:
+                    if plain:
                         src, to = tile_z.at[t % 2], dst.at[rows]
                     elif outgoing:
                         src, to = tile_c.at[t % 2, :, :, lanes], dst.at[half, :, side]
@@ -203,14 +204,17 @@
         bias_out[t * TILE // ROWS, :, rows, :] = jnp.swapaxes(tile_d[...], 0, 1)[:4].astype(BF16)
         export(t, True, False, z_sem)
 
+    bias_to = ((far2, 0, 0), (far2, 1, 1), (far2, 3, 2)) if last else ((far2, 0, 0), (far3, 1, 0))
+
     def bias_copy(n):
-        return pltpu.make_async_copy(bias_out.at[me ^ n], (far2, far3)[n].at[pl.ds(FAR_BIAS, 4)], x_sem.at[n])
-
-    for n in range(2):
+        dst, block, place = bias_to[n]
+        return pltpu.make_async_copy(bias_out.at[me ^ block], dst.at[pl.ds(FAR_BIAS + 4 * place, 4)], in_sem.at[n])
+
+    for n in range(len(bias_to)):
         bias_copy(n).start()
     for t in (n_tiles - 2, n_tiles - 1):
         export(t, False, False, z_sem)
-    for n in range(2):
+    for n in range(len(bias_to)):
         bias_copy(n).wait()
 
 
@@ -223,14 +227,15 @@
 DMA2 = pltpu.SemaphoreType.DMA((2,))
 FAR_BIAS = ROWS + ROWS // 2
 FAR = jax.ShapeDtypeStruct((FAR_BIAS + 4, CH, COLS), BF16)
+FAR_LAST = jax.ShapeDtypeStruct((FAR_BIAS + 12, CH, COLS), BF16)
 ROW_WIDE = jax.ShapeDtypeStruct((ROWS, CH, COLS), F32)
 SAMPLE_BF = pltpu.VMEM((CH, COLS, COLS), BF16)
 
 
-def u_call(sc, zt, zr, masks, norms, xgs, w_ab, w_sq, w_bias):
+def u_call(last, sc, zt, zr, masks, norms, xgs, w_ab, w_sq, w_bias):
     return pl.pallas_call(
-        u_kernel,
-        out_shape=(ROW_WIDE, ROW_WIDE, jax.ShapeDtypeStruct((4, 4, ROWS, COLS), BF16), FAR, FAR),
+        functools.partial(u_kernel, last),
+        out_shape=(ROW_WIDE, ROW_WIDE, jax.ShapeDtypeStruct((4, 4, ROWS, COLS), BF16), *((FAR_LAST, ROW_WIDE) if last else (FAR, FAR))),
         in_specs=[SM] + [HB] * 4 + [VM] * 9,
         out_specs=(HB, HB, VM, HB, HB),
         scratch_shapes=[
@@ -369,22 +374,25 @@
 STEPS = 6
 
 
-def attention_kernel(n, fresh, sc, *refs):
+def attention_kernel(n, fresh, away, sc, *refs):
     z_refs, bias_refs = refs[:n], refs[n:2 * n]
     mask_in, norms, w_all, w_proj = refs[2 * n:2 * n + 4]
-    rest = refs[2 * n + (4 if fresh else 5):]
+    rest = refs[2 * n + 4 + away + (not fresh):]
+    mask_away, out_away = refs[2 * n + 4], rest[1]
     (out, z_in, z_out, mask_i, mask, bias_rows, bias_t, q_s, k_s, v_s, g_s, vn_s, gn_s, keep_s, s_buf, e_buf, p_s,
-     top_s, inv_s, o_s, m_sem, z_sem, o_sem) = rest
+     top_s, inv_s, o_s, m_sem, z_sem, o_sem) = rest[:1] + rest[1 + away:]
     n_rows = n * ROWS
 
     def z_copy(j):
         return pltpu.make_async_copy(z_refs[j], z_in.at[pl.ds(ROWS * j, ROWS)], z_sem.at[j])
 
     def m_copy(j):
-        return pltpu.make_async_copy(mask_in.at[sc[j]], mask_i.at[pl.ds(ROWS * j, ROWS)], m_sem.at[j])
+        src = mask_away.at[0] if away and j == n - 1 else mask_in.at[sc[j]]
+        return pltpu.make_async_copy(src, mask_i.at[pl.ds(ROWS * j, ROWS)], m_sem.at[j])
 
     def o_copy(j):
-        return pltpu.make_async_copy(z_out.at[pl.ds(ROWS * j, ROWS)], out.at[sc[j]], o_sem.at[j])
+        dst = out_away if away and j == n - 1 else out.at[sc[j]]
+        return pltpu.make_async_copy(z_out.at[pl.ds(ROWS * j, ROWS)], dst, o_sem.at[j])
 
     for j in range(n):
         m_copy(j).start()
@@ -494,9 +502,10 @@
         o_copy(j).wait()
 
 
-def attend(sc, z_parts, biases, mask, norms, w_all, w_proj, out):
-    n, fresh = len(z_parts), out is None
-    args = (sc, *z_parts, *biases, mask, norms, w_all, w_proj) + (() if fresh else (out,))
+def attend(sc, z_parts, biases, mask, norms, w_all, w_proj, out, mask_away=None):
+    n, fresh, away = len(z_parts), out is None, mask_away is not None
+    args = (sc, *z_parts, *biases, mask, norms, w_all, w_proj) + ((mask_away,) if away else ()) + (() if fresh else (out,))
+    whole = jax.ShapeDtypeStruct((mask.shape[0], ROWS, CH, COLS), F32)
     rows = n * ROWS
     pair = pltpu.VMEM((SLOTS, CH, COLS), BF16)
     wide = pltpu.VMEM((SLOTS, CH, COLS), F32)
@@ -505,10 +514,10 @@
     line = pltpu.VMEM((SLOTS, 8, COLS), F32)
     sems = pltpu.SemaphoreType.DMA((n,))
     return pl.pallas_call(
-        functools.partial(attention_kernel, n, fresh),
-        out_shape=jax.ShapeDtypeStruct((mask.shape[0], ROWS, CH, COLS), F32),
-        in_specs=[SM] + [HB] * n + [VM] * n + [HB] + [VM] * 3 + ([] if fresh else [HB]),
-        out_specs=HB,
+        functools.partial(attention_kernel, n, fresh, away),
+        out_shape=(whole, ROW_WIDE) if away else whole,
+        in_specs=[SM] + [HB] * n + [VM] * n + [HB] + [VM] * 3 + [HB] * (away + (not fresh)),
+        out_specs=(HB, HB) if away else HB,
         scratch_shapes=[
             pltpu.VMEM((rows, CH, COLS), F32), pltpu.VMEM((rows + STEPS, CH, COLS), F32), pltpu.VMEM((rows, COLS), jnp.int32),
             pltpu.VMEM((rows, COLS), F32), each, each, pltpu.VMEM((SLOTS, HEADS, CH, COLS), BF16),
@@ -540,16 +549,20 @@
         zt = jnp.transpose(pair_z, (0, 1, 3, 2))
         n_own = zt.shape[0] // 4
         mask_bf = pair_mask.astype(BF16)
-        masks = [lax.dynamic_slice_in_dim(mask_bf, n_own * (me ^ r), n_own, axis=0) for r in range(4)]
-        arrived, zt_t = [], zt
+        arrived, before = [], ()
         for t in range(n_own):
-            sends = [lax.dynamic_index_in_dim(zt_t, n_own * (me ^ r) + t, 0, keepdims=False) for r in (2, 3, 1)]
-            *sends, zt_t = lax.optimization_barrier((*sends, zt))
-            if t == 0:
-                weights, masks = lax.optimization_barrier((weights, masks, sends[0]))[:2]
-            got = [exchange(v, r) for v, r in zip(sends, (2, 3, 1))]
-            arrived.append((got[2], got[0], got[1]))
-        masks = [exchange(m, r) if r else m for r, m in enumerate(masks)]
+            got = {}
+            for r in (2, 3, 1):
+                send = lax.dynamic_index_in_dim(lax.optimization_barrier((zt, *before))[0], n_own * (me ^ r) + t, 0, keepdims=False)
+                if t == 0 or r == 1:
+                    before = (send,)
+                got[r] = exchange(send, r)
+                if t == 0 and r == 2:
+                    mask_bf, weights = lax.optimization_barrier((mask_bf, weights, send))[:2]
+                    masks = [lax.dynamic_slice_in_dim(mask_bf, n_own * (me ^ k), n_own, axis=0) for k in range(4)]
+                    before = (*before, *masks)
+                    masks = [exchange(m, k) if k else m for k, m in enumerate(masks)]
+            arrived.append((got[1], got[2], got[3]))
 
         out_n, out_x, out_ab, out_sq = update_weights(weights[:10])
         in_n, in_x, in_ab, in_sq = update_weights(weights[10:20])
@@ -574,9 +587,9 @@
             token[0] = jax.tree.leaves(res)[-1]
             return res
 
-        def attention(jobs, out):
+        def attention(jobs, out, mask_away=None):
             samples, orders, z_parts, biases = zip(*jobs)
-            return ordered(attend, samples + orders, z_parts, biases, pair_mask, att_norms, w_all, w_out, out)
+            return ordered(attend, samples + orders, z_parts, biases, pair_mask, att_norms, w_all, w_out, out, mask_away)
 
         far = [(t, r) for t in range(n_own) for r in (2, 3)]
         a_far, b_far = ordered(l1_call, [n_own * (me ^ r) + t for t, r in far], zt, pair_mask, norms, w_ab)
@@ -584,25 +597,35 @@
         x_near = ordered(l2_call, [me], a_far, b_far, b_par, xgs)
 
         out = None
-        held, waiting = [], []
+        held = []
         for t in range(n_own):
-            z_own, z_par, bias, far2, far3 = ordered(u_call, [me, n_own * me + t], zt, arrived[t],
-                                                     [m[t] for m in masks], norms, xgs, w_ab, w_sq, w_bias8)
-            held.append({2: exchange(far2, 2), 3: exchange(far3, 3)})
+            last = t == n_own - 1
+            z_own, z_par, bias, far2, far3 = ordered(functools.partial(u_call, last), [me, n_own * me + t], zt,
+                                                     arrived[t], [m[t] for m in masks], norms, xgs, w_ab, w_sq, w_bias8)
             near = (n_own * (me ^ 1) + t, 0, exchange(z_par, 1), exchange(bias, 1))
-            out = attention(waiting + [(n_own * me + t, 0, z_own, bias)], out)
-            waiting = [near]
+            held.append({2: exchange(far2, 2)})
+            own = (n_own * me + t, 0, z_own, bias)
+            if last:
+                out, away = attention([own, (0, 0, far3, bias)], out, masks[3][t][None].astype(jnp.int32))
+                away = exchange(away, 3)
+            else:
+                held[t][3] = exchange(far3, 3)
+                out = attention([own, near], out)
         for t in range(n_own):
-            mine, z_two = {}, {}
-            for r in (2, 3):
+            last = t == n_own - 1
+            mine, z_two, biases = {}, {}, {}
+            for r in held[t]:
                 z_two[r], bias_own = ordered(r_call, [me, n_own * (me ^ r) + t, far.index((t, r))], zt, x_near,
                                              held[t][r], norms, w_sq, w_bias8)
-                mine[r] = (bias_own, held[t][r][FAR_BIAS:])
-            par = exchange(jnp.stack([*mine[3], *mine[2]]), 1)
-            out = attention(waiting + [
-                (n_own * (me ^ r) + t, me, z_two[r], jnp.stack([mine[r][0], par[2 * r - 4], mine[r][1], par[2 * r - 3]]))
-                for r in (2, 3)], out)
-            waiting = []
+                mine[r] = [bias_own, *jnp.split(held[t][r][FAR_BIAS:], 3 if last else 1)]
+            if last:
+                biases[2] = jnp.stack([mine[2][k] for k in (0, 3, 1, 2)])
+            else:
+                par = exchange(jnp.stack(mine[3] + mine[2]), 1)
+                biases = {r: jnp.stack([mine[r][0], par[2 * r - 4], mine[r][1], par[2 * r - 3]]) for r in (2, 3)}
+            out = attention(([] if t else [near]) + [
+                (n_own * (me ^ r) + t, me, z_two[r], biases[r]) for r in biases], out)
+        out = lax.dynamic_update_index_in_dim(out, away, n_own * (me ^ 3) + n_own - 1, 0)
         return jnp.transpose(out, (0, 1, 3, 2))
 
     pair_spec = P('data', 'dap')

time: 1190 us -> 1370 us (1.15)
  waiting for transfers between devices: 299 us -> 484 us
    ppermute x28 -> x27, waiting for transfers between devices: 299 us -> 484 us  [exchange(): return lax.ppermute(values, 'dap', [(i, i ^ r) for i in range(4)])]
    pallas_call x6 -> x5, Pallas kernels: 57.5 us -> 45.2 us  [r_call(): pl.pallas_call(r_kernel, out_shape=(ROW_WIDE, jax.ShapeDtypeStruct((4, RO...]
    unnamed x109 -> x101, local copies, waits for them, and re-layouts: 27.7 us -> 20.7 us
    squeeze x3 -> x5, local copies, waits for them, and re-layouts: 29.2 us -> 33.6 us  [local_block(): lax.dynamic_index_in_dim(lax.optimization_barrier((zt, *before))[0], n_ow...]
  transfers between devices with their start and end apart: 28 -> 27, of which waited for: 9 -> 12; matrix products, arithmetic and copies ran while one was open for 3% -> 3% of each run, Pallas kernels for 51% -> 48%
where the time goes in v2:
time: 1370 us; the launch traced here: 1360 us
  Pallas kernels  775 us (57%)
  waiting for transfers between devices  484 us (35%)
  local copies, waits for them, and re-layouts  68.8 us (5%)
  starting transfers between devices  21.3 us (2%)
    ppermute x27, waiting for transfers between devices, exchange(): return lax.ppermute(values, 'dap', [(i, i ^ r) for i in range(4)])  484 us
    pallas_call x6, Pallas kernels, attend(): pl.pallas_call(functools.partial(attention_kernel, n, fresh, away), out_s...  391 us
    pallas_call x3, Pallas kernels, u_call(): pl.pallas_call(functools.partial(u_kernel, last), out_shape=(ROW_WIDE, RO...  277 us
    pallas_call x5, Pallas kernels, r_call(): pl.pallas_call(r_kernel, out_shape=(ROW_WIDE, jax.ShapeDtypeStruct((4, RO...  45.2 us
    squeeze x5, local copies, waits for them, and re-layouts, local_block(): lax.dynamic_index_in_dim(lax.optimization_barrier((zt, *before))[0], n_ow...  33.6 us
    pallas_call x1, Pallas kernels, l2_call(): pl.pallas_call(l2_kernel, grid=(n // 2,), out_shape=jax.ShapeDtypeStruct(...  32.9 us
    pallas_call x1, Pallas kernels, l1_call(): pl.pallas_call(l1_kernel, out_shape=(ab, ab), grid_spec=pltpu.PrefetchSca...  28.7 us
  transfers between devices with their start and end apart: 27, of which 12 were waited for; matrix products, arithmetic and copies ran while one was open for 3% of the time, Pallas kernels for 48%

profile of v2, /device:TPU:0, one launch (start us, length us, event | category | flops | bytes accessed | tf_op | source)
XLA Modules:
  0.0 1356.2 jit_solution(11106717722514243360)
XLA Ops:
  0.0 1.2 convert_element_type.6
  1.4 4.9 dynamic-slice_bitcast_fusion.8
  7.7 28.7 %near_projections.1 = (bf16[6,64,64,256]{3,2,1,0:T(8,128)(2,1)S(1)}, bf16[6,64,64,256]{3,2,1,0:T(8,128)(2,1)}) custom-call(s32[6]{0:T(128)S(1)} %stack.230.ids, f32[12,64,64,256]{3,2,1,0:T(8,128)} %bitcast.143, s32[12,64,256]{2,1,0:T(8,128)S(1)} %copy-done.2, f32[6,64,256]{2,1,0:T(8,128)S(1)} %broadcast_dynamic-update-slice_fusion.norms, ...), custom_call_target="tpu_custom_call" | custom-call | tf_op jit(solution)/shard_map/near_projections/pallas_call | solution.py:271
  36.5 4.6 copy-done.6
  41.1 0.8 collective-permute-start
  41.9 4.8 dynamic-slice_bitcast_fusion.7
  46.8 4.7 dynamic-slice_bitcast_fusion.6
  51.4 2.6 collective-permute-start.3
  54.4 1.6 collective-permute-start.5
  57.7 0.6 dynamic-slice_bitcast_fusion.9
  59.0 0.7 pad_add_fusion.12.sc
  59.7 177.7 %collective-permute-done.5 = bf16[3,64,256]{2,1,0:T(8,128)(2,1)S(1)} collective-permute-done((bf16[3,64,256]{2,1,0:T(8,128)(2,1)S(1)}, bf16[3,64,256]{2,1,0:T(8,128)(2,1)S(1)}, u32[]{:S(2)}, u32[]{:S(2)}) %collective-permute-start.5) | collective-permute-done | bytes 98336 | tf_op jit(solution)/shard_map/ppermute | solution.py:534
  237.4 1.7 collective-permute-start.6
  239.0 0.6 slice_bitcast_fusion.7
  239.7 2.4 collective-permute-done.6
  243.4 0.6 slice_bitcast_fusion.8
  244.1 32.9 %near_product.1.x_near = bf16[6,64,64,128]{3,2,1,0:T(8,128)(2,1)S(1)} custom-call(s32[1]{0:T(128)} %bitcast.1.sc, bf16[6,64,64,256]{3,2,1,0:T(8,128)(2,1)} %copy-done.6, bf16[6,64,64,256]{3,2,1,0:T(8,128)(2,1)} %get-tuple-element.96.b_own, bf16[6,64,64,256]{3,2,1,0:T(8,128)(2,1)} %collective-permute-done.b_par, f32[4,64,8,128]{3,2,1,0:T(8,128)S(1)} %pad_maximum_fusion.xgs), custom_call_target="tpu_custom_call" | custom-call | tf_op jit(solution)/shard_map/near_product/pallas_call | solution.py:308
  276.9 2.6 copy-done
  279.5 92.5 %pair_updates.3 = (f32[64,64,256]{2,1,0:T(8,128)}, f32[64,64,256]{2,1,0:T(8,128)}, bf16[4,4,64,256]{3,2,1,0:T(8,128)(2,1)}, bf16[100,64,256]{2,1,0:T(8,128)(2,1)}, bf16[100,64,256]{2,1,0:T(8,128)(2,1)}) custom-call(s32[2]{0:T(128)} %pad_add_fusion.12.sc, f32[12,64,64,256]{3,2,1,0:T(8,128)} %bitcast.146, f32[64,64,256]{2,1,0:T(8,128)} %collective-permute-done.1.zr1, ...), custom_call_target="tpu_custom_call" | custom-call | tf_op jit(solution)/shard_map/pair_updates/pallas_call | solution.py:236
  372.3 9.6 dynamic-slice_bitcast_fusion.3
  381.9 1.9 collective-permute-start.10
  384.3 9.7 dynamic-slice_bitcast_fusion
  395.7 65.5 %triangle_attention.6.refs_8_ = f32[12,64,64,256]{3,2,1,0:T(8,128)} custom-call(s32[4]{0:T(128)S(1)} %get-tuple-element.113.sc, f32[64,64,256]{2,1,0:T(8,128)} %get-tuple-element.114.refs_0_, f32[64,64,256]{2,1,0:T(8,128)} %collective-permute-done.7.refs_1_, bf16[4,4,64,256]{3,2,1,0:T(8,128)(2,1)S(1)} %copy-done.14, ...), custom_call_target="tpu_custom_call" | custom-call | tf_op jit(solution)/shard_map/triangle_attention/pallas_call | solution.py:516
  461.2 14.5 %collective-permute-done.10.zr2 = f32[64,64,256]{2,1,0:T(8,128)} collective-permute-done((f32[64,64,256]{2,1,0:T(8,128)}, f32[64,64,256]{2,1,0:T(8,128)}, u32[]{:S(2)}, u32[]{:S(2)}) %collective-permute-start.10) | collective-permute-done | bytes 4194336 | tf_op jit(solution)/shard_map/ppermute | solution.py:534
  475.7 88.8 %collective-permute-done.11.zr3 = f32[64,64,256]{2,1,0:T(8,128)} collective-permute-done((f32[64,64,256]{2,1,0:T(8,128)}, f32[64,64,256]{2,1,0:T(8,128)}, u32[]{:S(2)}, u32[]{:S(2)}) %collective-permute-start.11) | collective-permute-done | bytes 4194336 | tf_op jit(solution)/shard_map/ppermute | solution.py:534
  564.4 92.5 %pair_updates.4 = (f32[64,64,256]{2,1,0:T(8,128)}, f32[64,64,256]{2,1,0:T(8,128)}, bf16[4,4,64,256]{3,2,1,0:T(8,128)(2,1)}, bf16[100,64,256]{2,1,0:T(8,128)(2,1)}, bf16[100,64,256]{2,1,0:T(8,128)(2,1)}) custom-call(s32[2]{0:T(128)} %pad_add_fusion.11.sc, f32[12,64,64,256]{3,2,1,0:T(8,128)} %bitcast.149, f32[64,64,256]{2,1,0:T(8,128)} %collective-permute-done.9.zr1, ...), custom_call_target="tpu_custom_call" | custom-call | tf_op jit(solution)/shard_map/pair_updates/pallas_call | solution.py:236
  657.3 1.2 collective-permute-start.15
  658.8 0.7 collective-permute-start.13
  659.5 1.2 collective-permute-start.17
  660.7 4.4 collective-permute-done.13.refs_3_
  665.1 1.2 collective-permute-start.18
  666.3 0.8 collective-permute-start.22
  667.1 1.0 pad_add_fusion.10.sc
  668.3 1.0 copy-done.15
  669.3 65.3 %triangle_attention.7.refs_9_ = f32[12,64,64,256]{3,2,1,0:T(8,128)} custom-call(s32[4]{0:T(128)S(1)} %get-tuple-element.125.sc, f32[64,64,256]{2,1,0:T(8,128)} %get-tuple-element.126.refs_0_, f32[64,64,256]{2,1,0:T(8,128)} %copy-done.17, bf16[4,4,64,256]{3,2,1,0:T(8,128)(2,1)S(1)} %copy-done.15, ...), custom_call_target="tpu_custom_call", output_to_operand_aliasing={{}: (9, {})} | custom-call | tf_op jit(solution)/shard_map/triangle_attention/pallas_call | solution.py:516
  734.6 16.5 %collective-permute-done.15.zr2 = f32[64,64,256]{2,1,0:T(8,128)} collective-permute-done((f32[64,64,256]{2,1,0:T(8,128)}, f32[64,64,256]{2,1,0:T(8,128)}, u32[]{:S(2)}, u32[]{:S(2)}) %collective-permute-start.15) | collective-permute-done | bytes 4194336 | tf_op jit(solution)/shard_map/ppermute | solution.py:534
  751.1 88.6 %collective-permute-done.16.zr3 = f32[64,64,256]{2,1,0:T(8,128)} collective-permute-done((f32[64,64,256]{2,1,0:T(8,128)}, f32[64,64,256]{2,1,0:T(8,128)}, u32[]{:S(2)}, u32[]{:S(2)}) %collective-permute-start.16) | collective-permute-done | bytes 4194336 | tf_op jit(solution)/shard_map/ppermute | solution.py:534
  839.7 92.0 %pair_updates.5 = (f32[64,64,256]{2,1,0:T(8,128)}, f32[64,64,256]{2,1,0:T(8,128)}, bf16[4,4,64,256]{3,2,1,0:T(8,128)(2,1)}, bf16[108,64,256]{2,1,0:T(8,128)(2,1)}, f32[64,64,256]{2,1,0:T(8,128)}) custom-call(s32[2]{0:T(128)} %pad_add_fusion.10.sc, f32[12,64,64,256]{3,2,1,0:T(8,128)} %bitcast.150, f32[64,64,256]{2,1,0:T(8,128)} %collective-permute-done.14.zr1, ...), custom_call_target="tpu_custom_call" | custom-call | tf_op jit(solution)/shard_map/pair_updates/pallas_call | solution.py:236
  931.7 1.6 collective-permute-start.19
  933.7 1.3 collective-permute-start.25
  935.0 1.0 copy-done.13
  936.1 65.3 %triangle_attention.8 = (f32[12,64,64,256]{3,2,1,0:T(8,128)}, f32[64,64,256]{2,1,0:T(8,128)}) custom-call(s32[4]{0:T(128)S(1)} %get-tuple-element.132.sc, f32[64,64,256]{2,1,0:T(8,128)} %get-tuple-element.133.refs_0_, f32[64,64,256]{2,1,0:T(8,128)} %get-tuple-element.131.refs_1_, ...), custom_call_target="tpu_custom_call", output_to_operand_aliasing={{0}: (10, {})} | custom-call | tf_op jit(solution)/shard_map/triangle_attention/pallas_call | solution.py:516
  1002.3 0.9 slice_bitcast_fusion.5
  1003.2 0.9 slice_bitcast_fusion.6
  1004.1 2.8 copy-done.1
  1006.9 8.9 row_updates.5
  1015.9 2.0 copy-done.8
  1017.9 9.2 row_updates.6
  1027.1 2.0 copy-done.9
  1029.2 22.5 %collective-permute-done.22.x_far.xi = bf16[100,64,256]{2,1,0:T(8,128)(2,1)} collective-permute-done((bf16[100,64,256]{2,1,0:T(8,128)(2,1)}, bf16[100,64,256]{2,1,0:T(8,128)(2,1)}, u32[]{:S(2)}, u32[]{:S(2)}) %collective-permute-start.22) | collective-permute-done | bytes 3276832 | tf_op jit(solution)/shard_map/ppermute | solution.py:534
  1051.7 0.9 slice_bitcast_fusion.3
  1052.7 67.9 %collective-permute-done.23.x_far.xi = bf16[100,64,256]{2,1,0:T(8,128)(2,1)} collective-permute-done((bf16[100,64,256]{2,1,0:T(8,128)(2,1)}, bf16[100,64,256]{2,1,0:T(8,128)(2,1)}, u32[]{:S(2)}, u32[]{:S(2)}) %collective-permute-start.23) | collective-permute-done | bytes 3276832 | tf_op jit(solution)/shard_map/ppermute | solution.py:534
  1120.6 1.1 collective-permute-start.20
  1121.7 0.9 slice_bitcast_fusion.4
  1123.2 95.9 %triangle_attention.9.refs_8_ = f32[12,64,64,256]{3,2,1,0:T(8,128)} custom-call(s32[6]{0:T(128)S(1)} %stack.215.sc, f32[64,64,256]{2,1,0:T(8,128)} %collective-permute-done.19.refs_0_, f32[64,64,256]{2,1,0:T(8,128)} %copy-done.8, f32[64,64,256]{2,1,0:T(8,128)} %copy-done.9, ...), custom_call_target="tpu_custom_call", output_to_operand_aliasing={{}: (11, {})} | custom-call | tf_op jit(solution)/shard_map/triangle_attention/pallas_call | solution.py:516
  1219.2 9.0 row_updates.7
  1228.2 2.0 copy-done.10
  1230.1 8.9 row_updates.8
  1239.1 2.0 copy-done.11
  1241.7 1.1 slice_bitcast_fusion.2
  1243.2 65.3 %triangle_attention.10.refs_6_ = f32[12,64,64,256]{3,2,1,0:T(8,128)} custom-call(s32[4]{0:T(128)S(1)} %pad_add_fusion.5.sc, f32[64,64,256]{2,1,0:T(8,128)} %copy-done.10, f32[64,64,256]{2,1,0:T(8,128)} %copy-done.11, bf16[4,4,64,256]{3,2,1,0:T(8,128)(2,1)S(1)} %pad_maximum_fusion.6.refs_2_, ...), custom_call_target="tpu_custom_call", output_to_operand_aliasing={{}: (9, {})} | custom-call | tf_op jit(solution)/shard_map/triangle_attention/pallas_call | solution.py:516
  1308.5 9.1 row_updates.9
  1317.7 33.6 %triangle_attention.11 = f32[12,64,64,256]{3,2,1,0:T(8,128)} custom-call(s32[2]{0:T(128)S(1)} %pad_add_fusion.3.sc, f32[64,64,256]{2,1,0:T(8,128)S(1)} %get-tuple-element.158.refs_0_, bf16[4,4,64,256]{3,2,1,0:T(8,128)(2,1)S(1)} %pad_maximum_fusion.7.refs_1_, s32[12,64,256]{2,1,0:T(8,128)S(1)} %copy-done.2, ...), custom_call_target="tpu_custom_call", output_to_operand_aliasing={{}: (7, {})} | custom-call | tf_op jit(solution)/shard_map/triangle_attention/pallas_call | solution.py:516
  1351.3 4.7 bitcast_dynamic-update-slice_fusion
  (182 shorter events, 11.8 us)
Async XLA Ops:
  1.2 5.1 copy-start.19
  1.2 5.2 copy-start.20
  1.2 5.3 copy-start.21
  1.3 5.4 copy-start.22
  1.3 5.5 copy-start.23
  1.3 5.6 copy-start.24
  1.3 5.7 copy-start.25
  1.3 5.8 copy-start.38
  1.3 5.9 copy-start.39
  1.3 6.0 copy-start.40
  1.3 6.1 copy-start.41
  1.4 6.1 copy-start.35
  1.4 6.2 copy-start.36
  1.4 6.4 copy-start.2
  7.3 29.2 %copy-start.12 = (bf16[2,256,64]{2,1,0:T(8,128)(2,1)}, bf16[2,256,64]{2,1,0:T(8,128)(2,1)S(1)}, u32[]{:S(2)}) copy-start(bf16[2,256,64]{2,1,0:T(8,128)(2,1)S(1)} %pad_maximum_fusion.8.w_ab) | copy-start | bytes 196612
  7.7 28.8 %copy-start.3 = (f32[6,64,256]{2,1,0:T(8,128)}, f32[6,64,256]{2,1,0:T(8,128)S(1)}, u32[]{:S(2)}) copy-start(f32[6,64,256]{2,1,0:T(8,128)S(1)} %broadcast_dynamic-update-slice_fusion.norms) | copy-start | bytes 1179652
  41.1 203.0 %collective-permute-start = (bf16[6,64,64,256]{3,2,1,0:T(8,128)(2,1)}, bf16[6,64,64,256]{3,2,1,0:T(8,128)(2,1)}, u32[]{:S(2)}, u32[]{:S(2)}) collective-permute-start(bf16[6,64,64,256]{3,2,1,0:T(8,128)(2,1)} %get-tuple-element.96.b_own), channel_id=1, source_target_pairs={{0,1},{1,0},{2,3},{3,2},{4,5},{5,4},{6,7},{7,6}} | collective-permute-start | bytes 37748744 | tf_op jit(solution)/shard_map/ppermute | solution.py:534
  46.7 9.4 copy-start.26
  46.7 9.5 copy-start.27
  46.7 9.6 copy-start.28
  46.7 9.7 copy-start.29
  46.7 9.8 copy-start.37
  46.7 11.6 copy-start.42
  46.7 11.8 copy-start.43
  46.7 11.9 copy-start.44
  46.7 12.0 copy-start.45
  51.4 228.1 %collective-permute-start.1 = (f32[64,64,256]{2,1,0:T(8,128)}, f32[64,64,256]{2,1,0:T(8,128)}, u32[]{:S(2)}, u32[]{:S(2)}) collective-permute-start(f32[64,64,256]{2,1,0:T(8,128)} %dynamic-slice_bitcast_fusion.6), channel_id=1, source_target_pairs={{0,1},{1,0},{2,3},{3,2},{4,5},{5,4},{6,7},{7,6}} | collective-permute-start | bytes 12582920 | tf_op jit(solution)/shard_map/ppermute | solution.py:534
  51.4 228.1 %collective-permute-start.3 = (f32[64,64,256]{2,1,0:T(8,128)}, f32[64,64,256]{2,1,0:T(8,128)}, u32[]{:S(2)}, u32[]{:S(2)}) collective-permute-start(f32[64,64,256]{2,1,0:T(8,128)} %dynamic-slice_bitcast_fusion.7), channel_id=1, source_target_pairs={{0,3},{1,2},{2,1},{3,0},{4,7},{5,6},{6,5},{7,4}} | collective-permute-start | bytes 12582920 | tf_op jit(solution)/shard_map/ppermute | solution.py:534
  54.0 225.5 %collective-permute-start.2 = (f32[64,64,256]{2,1,0:T(8,128)}, f32[64,64,256]{2,1,0:T(8,128)}, u32[]{:S(2)}, u32[]{:S(2)}) collective-permute-start(f32[64,64,256]{2,1,0:T(8,128)} %dynamic-slice_bitcast_fusion.8), channel_id=1, source_target_pairs={{0,2},{1,3},{2,0},{3,1},{4,6},{5,7},{6,4},{7,5}} | collective-permute-start | bytes 12582920 | tf_op jit(solution)/shard_map/ppermute | solution.py:534
  54.4 182.9 %collective-permute-start.5 = (bf16[3,64,256]{2,1,0:T(8,128)(2,1)S(1)}, bf16[3,64,256]{2,1,0:T(8,128)(2,1)S(1)}, u32[]{:S(2)}, u32[]{:S(2)}) collective-permute-start(bf16[3,64,256]{2,1,0:T(8,128)(2,1)S(1)} %get-tuple-element.180), channel_id=1, source_target_pairs={{0,2},{1,3},{2,0},{3,1},{4,6},{5,7},{6,4},{7,5}} | collective-permute-start | bytes 294920 | tf_op jit(solution)/shard_map/ppermute | solution.py:534
  59.0 217.9 %copy-start.5 = (f32[4,64,8,128]{3,2,1,0:T(8,128)}, f32[4,64,8,128]{3,2,1,0:T(8,128)S(1)}, u32[]{:S(2)}) copy-start(f32[4,64,8,128]{3,2,1,0:T(8,128)S(1)} %pad_maximum_fusion.xgs) | copy-start | bytes 3145732
  237.4 4.7 collective-permute-start.6
  242.1 1.3 collective-permute-start.4
  372.0 12.0 copy-start.14
  372.0 23.7 %collective-permute-start.7 = (f32[64,64,256]{2,1,0:T(8,128)}, f32[64,64,256]{2,1,0:T(8,128)}, u32[]{:S(2)}, u32[]{:S(2)}) collective-permute-start(f32[64,64,256]{2,1,0:T(8,128)} %get-tuple-element.115), channel_id=1, source_target_pairs={{0,1},{1,0},{2,3},{3,2},{4,5},{5,4},{6,7},{7,6}} | collective-permute-start | bytes 12582920 | tf_op jit(solution)/shard_map/ppermute | solution.py:534
  381.9 93.8 %collective-permute-start.10 = (f32[64,64,256]{2,1,0:T(8,128)}, f32[64,64,256]{2,1,0:T(8,128)}, u32[]{:S(2)}, u32[]{:S(2)}) collective-permute-start(f32[64,64,256]{2,1,0:T(8,128)} %get-tuple-element.163), channel_id=1, source_target_pairs={{0,2},{1,3},{2,0},{3,1},{4,6},{5,7},{6,4},{7,5}} | collective-permute-start | bytes 12582920 | tf_op jit(solution)/shard_map/ppermute | solution.py:534
  383.8 180.7 %collective-permute-start.11 = (f32[64,64,256]{2,1,0:T(8,128)}, f32[64,64,256]{2,1,0:T(8,128)}, u32[]{:S(2)}, u32[]{:S(2)}) collective-permute-start(f32[64,64,256]{2,1,0:T(8,128)} %get-tuple-element.162), channel_id=1, source_target_pairs={{0,3},{1,2},{2,1},{3,0},{4,7},{5,6},{6,5},{7,4}} | collective-permute-start | bytes 12582920 | tf_op jit(solution)/shard_map/ppermute | solution.py:534
  383.8 180.7 %collective-permute-start.9 = (f32[64,64,256]{2,1,0:T(8,128)}, f32[64,64,256]{2,1,0:T(8,128)}, u32[]{:S(2)}, u32[]{:S(2)}) collective-permute-start(f32[64,64,256]{2,1,0:T(8,128)} %get-tuple-element.164), channel_id=1, source_target_pairs={{0,1},{1,0},{2,3},{3,2},{4,5},{5,4},{6,7},{7,6}} | collective-permute-start | bytes 12582920 | tf_op jit(solution)/shard_map/ppermute | solution.py:534
  384.0 10.0 collective-permute-start.8
  384.3 10.0 copy-start.30
  384.3 10.1 copy-start.31
  384.3 10.2 copy-start.32
  384.3 10.3 copy-start.33
  384.3 10.4 copy-start.34
  394.0 265.5 %collective-permute-start.14 = (f32[64,64,256]{2,1,0:T(8,128)}, f32[64,64,256]{2,1,0:T(8,128)}, u32[]{:S(2)}, u32[]{:S(2)}) collective-permute-start(f32[64,64,256]{2,1,0:T(8,128)} %get-tuple-element.161), channel_id=1, source_target_pairs={{0,1},{1,0},{2,3},{3,2},{4,5},{5,4},{6,7},{7,6}} | collective-permute-start | bytes 12582920 | tf_op jit(solution)/shard_map/ppermute | solution.py:534
  656.9 9.4 collective-permute-start.12
  657.3 93.8 %collective-permute-start.15 = (f32[64,64,256]{2,1,0:T(8,128)}, f32[64,64,256]{2,1,0:T(8,128)}, u32[]{:S(2)}, u32[]{:S(2)}) collective-permute-start(f32[64,64,256]{2,1,0:T(8,128)} %get-tuple-element.160), channel_id=1, source_target_pairs={{0,2},{1,3},{2,0},{3,1},{4,6},{5,7},{6,4},{7,5}} | collective-permute-start | bytes 12582920 | tf_op jit(solution)/shard_map/ppermute | solution.py:534
  658.5 181.2 %collective-permute-start.16 = (f32[64,64,256]{2,1,0:T(8,128)}, f32[64,64,256]{2,1,0:T(8,128)}, u32[]{:S(2)}, u32[]{:S(2)}) collective-permute-start(f32[64,64,256]{2,1,0:T(8,128)} %get-tuple-element.159), channel_id=1, source_target_pairs={{0,3},{1,2},{2,1},{3,0},{4,7},{5,6},{6,5},{7,4}} | collective-permute-start | bytes 12582920 | tf_op jit(solution)/shard_map/ppermute | solution.py:534
  658.8 6.3 collective-permute-start.13
  659.5 274.2 %collective-permute-start.17 = (bf16[100,64,256]{2,1,0:T(8,128)(2,1)}, bf16[100,64,256]{2,1,0:T(8,128)(2,1)}, u32[]{:S(2)}, u32[]{:S(2)}) collective-permute-start(bf16[100,64,256]{2,1,0:T(8,128)(2,1)} %get-tuple-element.137), channel_id=1, source_target_pairs={{0,2},{1,3},{2,0},{3,1},{4,6},{5,7},{6,4},{7,5}} | collective-permute-start | bytes 9830408 | tf_op jit(solution)/shard_map/ppermute | solution.py:534
  665.1 336.3 %collective-permute-start.18 = (bf16[100,64,256]{2,1,0:T(8,128)(2,1)}, bf16[100,64,256]{2,1,0:T(8,128)(2,1)}, u32[]{:S(2)}, u32[]{:S(2)}) collective-permute-start(bf16[100,64,256]{2,1,0:T(8,128)(2,1)} %get-tuple-element.112), channel_id=1, source_target_pairs={{0,3},{1,2},{2,1},{3,0},{4,7},{5,6},{6,5},{7,4}} | collective-permute-start | bytes 9830408 | tf_op jit(solution)/shard_map/ppermute | solution.py:534
  666.3 385.4 %collective-permute-start.22 = (bf16[100,64,256]{2,1,0:T(8,128)(2,1)}, bf16[100,64,256]{2,1,0:T(8,128)(2,1)}, u32[]{:S(2)}, u32[]{:S(2)}) collective-permute-start(bf16[100,64,256]{2,1,0:T(8,128)(2,1)} %get-tuple-element.147), channel_id=1, source_target_pairs={{0,2},{1,3},{2,0},{3,1},{4,6},{5,7},{6,4},{7,5}} | collective-permute-start | bytes 9830408 | tf_op jit(solution)/shard_map/ppermute | solution.py:534
  931.7 191.5 %collective-permute-start.19 = (f32[64,64,256]{2,1,0:T(8,128)}, f32[64,64,256]{2,1,0:T(8,128)}, u32[]{:S(2)}, u32[]{:S(2)}) collective-permute-start(f32[64,64,256]{2,1,0:T(8,128)} %get-tuple-element.142), channel_id=1, source_target_pairs={{0,1},{1,0},{2,3},{3,2},{4,5},{5,4},{6,7},{7,6}} | collective-permute-start | bytes 12582920 | tf_op jit(solution)/shard_map/ppermute | solution.py:534
  933.4 187.2 %collective-permute-start.23 = (bf16[100,64,256]{2,1,0:T(8,128)(2,1)}, bf16[100,64,256]{2,1,0:T(8,128)(2,1)}, u32[]{:S(2)}, u32[]{:S(2)}) collective-permute-start(bf16[100,64,256]{2,1,0:T(8,128)(2,1)} %get-tuple-element.124), channel_id=1, source_target_pairs={{0,3},{1,2},{2,1},{3,0},{4,7},{5,6},{6,5},{7,4}} | collective-permute-start | bytes 9830408 | tf_op jit(solution)/shard_map/ppermute | solution.py:534
  933.7 308.0 %collective-permute-start.25 = (bf16[108,64,256]{2,1,0:T(8,128)(2,1)}, bf16[108,64,256]{2,1,0:T(8,128)(2,1)}, u32[]{:S(2)}, u32[]{:S(2)}) collective-permute-start(bf16[108,64,256]{2,1,0:T(8,128)(2,1)} %get-tuple-element.155), channel_id=1, source_target_pairs={{0,2},{1,3},{2,0},{3,1},{4,6},{5,7},{6,4},{7,5}} | collective-permute-start | bytes 10616840 | tf_op jit(solution)/shard_map/ppermute | solution.py:534
  936.1 68.0 %copy-start.4 = (f32[6,64,256]{2,1,0:T(8,128)S(1)}, f32[6,64,256]{2,1,0:T(8,128)}, u32[]{:S(2)}) copy-start(f32[6,64,256]{2,1,0:T(8,128)} %copy-done.3) | copy-start | bytes 1179652
  936.1 68.0 %copy-start.7 = (bf16[4,64,64]{2,1,0:T(8,128)(2,1)S(1)}, bf16[4,64,64]{2,1,0:T(8,128)(2,1)}, u32[]{:S(2)}) copy-start(bf16[4,64,64]{2,1,0:T(8,128)(2,1)} %pad_maximum_fusion.10.w_sq) | copy-start | bytes 98308
  936.1 68.0 %copy-start.16 = (bf16[8,64]{1,0:T(8,128)(2,1)S(1)}, bf16[8,64]{1,0:T(8,128)(2,1)}, u32[]{:S(2)}) copy-start(bf16[8,64]{1,0:T(8,128)(2,1)} %concatenate.53.w_bias) | copy-start | bytes 3076
  1001.4 349.9 %collective-permute-start.26 = (f32[64,64,256]{2,1,0:T(8,128)}, f32[64,64,256]{2,1,0:T(8,128)}, u32[]{:S(2)}, u32[]{:S(2)}) collective-permute-start(f32[64,64,256]{2,1,0:T(8,128)} %get-tuple-element.135), channel_id=1, source_target_pairs={{0,3},{1,2},{2,1},{3,0},{4,7},{5,6},{6,5},{7,4}} | collective-permute-start | bytes 12582920 | tf_op jit(solution)/shard_map/ppermute | solution.py:534
  1017.9 201.3 %slice-start = ((s8[6291456]{0:T(1024)(128)(4,1)}), s8[4194304]{0:T(1024)(128)(4,1)S(1)}, s32[]{:S(2)}) async-start(s8[6291456]{0:T(1024)(128)(4,1)} %bitcast.125), calls=%async_computation | async-start | bytes 8388608
  1051.7 71.0 %collective-permute-start.21 = (bf16[4,4,64,256]{3,2,1,0:T(8,128)(2,1)S(1)}, bf16[4,4,64,256]{3,2,1,0:T(8,128)(2,1)S(1)}, u32[]{:S(2)}, u32[]{:S(2)}) collective-permute-start(bf16[4,4,64,256]{3,2,1,0:T(8,128)(2,1)S(1)} %fusion.5), channel_id=1, source_target_pairs={{0,1},{1,0},{2,3},{3,2},{4,5},{5,4},{6,7},{7,6}} | collective-permute-start | bytes 1572872 | tf_op jit(solution)/shard_map/ppermute | solution.py:534
  1120.6 2.6 collective-permute-start.20
  1123.2 95.9 %slice-start.1 = ((s8[6291456]{0:T(1024)(128)(4,1)}), s8[2097152]{0:T(1024)(128)(4,1)S(1)}, s32[]{:S(2)}) async-start(s8[6291456]{0:T(1024)(128)(4,1)} %bitcast.125), calls=%async_computation.1 | async-start | bytes 4194304
  1241.1 1.9 collective-permute-start.24
  (11 other events, 27.0 us)

commit v3 on v2

--- a/solution.py
+++ b/solution.py
@@ -34,8 +34,9 @@
 
 
 def ab_row(proj, tile_a, tile_b, slot):
-    tile_a[slot] = ((jnp.tanh(proj[CH:2 * CH]) + 1.0) * proj[:CH]).astype(BF16)
-    tile_b[slot] = ((jnp.tanh(proj[3 * CH:]) + 1.0) * proj[2 * CH:3 * CH]).astype(BF16)
+    for n, tile in enumerate((tile_a, tile_b)):
+        linear, gate = jnp.split(proj[2 * CH * n:2 * CH * n + 2 * CH], 2, axis=0)
+        tile[slot] = ((jnp.tanh(gate) + 1.0) * linear).astype(BF16)
 
 
 def x_norm_tile(x_s, tile_x, base, xg, xb):
@@ -68,25 +69,23 @@
                 held[k][i] = stage(i, held[k - 1].pop(i) if k else None)
 
 
-def u_kernel(last, sc, zt, zr1, zr2, zr3, mask0, mask1, mask2, mask3, norms, xgs, w_ab, w_sq, w_bias,
-             z2_own, z2_par, bias_out, far2, far3,
-             z_s, a_s, b_s, x_s, mask, stats, tile_a, tile_b, tile_x, tile_c, tile_d, tile_z, in_sem, z_sem, x_sem):
+def u_kernel(last, layout, sc, *refs):
+    z_refs = refs[:len(layout)]
+    (mask0, mask1, mask2, mask3, norms, xgs, w_ab, w_sq, w_bias, z2_own, z2_par, bias_out, far2, far3,
+     z_s, a_s, b_s, x_s, mask, stats, tile_a, tile_b, tile_x, tile_c, tile_d, tile_z, in_sem, z_sem, x_sem) = refs[len(layout):]
     me, sample = sc[0], sc[1]
-    srcs = (zt.at[sample], zr1, zr2, zr3)
     lanes = pl.ds(pl.multiple_of(LANES * (me // 2), LANES), LANES)
     out_norm = (norms[0], norms[1])
     in_norm = (norms[2], norms[3])
     att_norm = (norms[4], norms[5])
     n_tiles = COLS // TILE
 
-    def z_copy(r):
-        start = pl.multiple_of(ROWS * (me ^ r), ROWS)
-        return pltpu.make_async_copy(srcs[r], z_s.at[pl.ds(start, ROWS)], in_sem.at[r])
-
-    for r in range(4):
-        z_copy(r).start()
+    for ref, (r, start) in zip(z_refs, layout):
+        src = ref if r else ref.at[sample]
+        rows = pl.ds(pl.multiple_of(ROWS * (me ^ r) + start, 8), src.shape[0])
+        pltpu.make_async_copy(src, z_s.at[rows], in_sem.at[r]).start()
     for r, part in enumerate((mask0, mask1, mask2, mask3)):
-        mask[pl.ds(pl.multiple_of(ROWS * (me ^ r), ROWS), ROWS), :] = part[...].astype(F32)
+        mask[pl.ds(pl.multiple_of(ROWS * (me ^ r), ROWS), ROWS), :] = part[:].astype(F32)
 
     def mask_row(base, i):
         return mask[pl.ds(base + i, 1), :]
@@ -101,8 +100,8 @@
         return [stats[first + n, pl.ds(base + i, 1), :] for n in range(2)]
 
     def flush(base):
-        a_s[:, pl.ds(base, TILE), :] = jnp.swapaxes(tile_a[...], 0, 1)
-        b_s[:, pl.ds(base, TILE), :] = jnp.swapaxes(tile_b[...], 0, 1)
+        a_s[:, pl.ds(base, TILE), :] = jnp.swapaxes(tile_a[:], 0, 1)
+        b_s[:, pl.ds(base, TILE), :] = jnp.swapaxes(tile_b[:], 0, 1)
 
     def export(t, start, outgoing, sem):
         r = (t * TILE // ROWS) ^ me
@@ -130,7 +129,7 @@
 
         @pl.when(v * TILE % ROWS == 0)
         def _():
-            pltpu.make_async_copy(zr1, z_s.at[pl.ds(0, ROWS)], in_sem.at[r]).wait()
+            pltpu.make_async_copy(z_refs[0].at[sample], z_s.at[pl.ds(0, ROWS)], in_sem.at[r]).wait()
 
         base = pl.multiple_of(ROWS * (me ^ r) + v * TILE % ROWS, TILE)
         staggered(
@@ -152,7 +151,7 @@
             export(t - 2, False, True, x_sem)
 
         x_norm_tile(x_s, tile_x, base, xgs.at[0], xgs.at[1])
-        tile_c[t % 2] = jnp.swapaxes(tile_x[...], 0, 1)
+        tile_c[t % 2] = jnp.swapaxes(tile_x[:], 0, 1)
 
         def gate_and_update(i, _):
             normed = channel_norm(z_s[base + i], out_norm, recall(base, i, 0)).astype(BF16)
@@ -185,7 +184,7 @@
             export(t - 2, False, False, z_sem)
 
         x_norm_tile(x_s, tile_x, base, xgs.at[2], xgs.at[3])
-        tile_c[t % 2] = jnp.swapaxes(tile_x[...], 0, 1)
+        tile_c[t % 2] = jnp.swapaxes(tile_x[:], 0, 1)
 
         def gate_and_update(i, _):
             normed = channel_norm(z_s[base + i], in_norm, recall(base, i, 2)).astype(BF16)
@@ -197,11 +196,11 @@
             return channel_norm(z_two, att_norm).astype(BF16)
 
         def bias_row(i, normed):
-            tile_d[i] = mm(w_bias[...], normed)
+            tile_d[i] = mm(w_bias[:], normed)
 
         staggered(TILE, gate_and_update, next_norm, bias_row)
         rows = pl.ds(pl.multiple_of(t * TILE % ROWS, TILE), TILE)
-        bias_out[t * TILE // ROWS, :, rows, :] = jnp.swapaxes(tile_d[...], 0, 1)[:4].astype(BF16)
+        bias_out[t * TILE // ROWS, :, rows, :] = jnp.swapaxes(tile_d[:], 0, 1)[:4].astype(BF16)
         export(t, True, False, z_sem)
 
     bias_to = ((far2, 0, 0), (far2, 1, 1), (far2, 3, 2)) if last else ((far2, 0, 0), (far3, 1, 0))
@@ -232,11 +231,11 @@
 SAMPLE_BF = pltpu.VMEM((CH, COLS, COLS), BF16)
 
 
-def u_call(last, sc, zt, zr, masks, norms, xgs, w_ab, w_sq, w_bias):
+def u_call(last, layout, sc, z_parts, masks, norms, xgs, w_ab, w_sq, w_bias):
     return pl.pallas_call(
-        functools.partial(u_kernel, last),
+        functools.partial(u_kernel, last, layout),
         out_shape=(ROW_WIDE, ROW_WIDE, jax.ShapeDtypeStruct((4, 4, ROWS, COLS), BF16), *((FAR_LAST, ROW_WIDE) if last else (FAR, FAR))),
-        in_specs=[SM] + [HB] * 4 + [VM] * 9,
+        in_specs=[SM] + [HB] * len(layout) + [VM] * 9,
         out_specs=(HB, HB, VM, HB, HB),
         scratch_shapes=[
             pltpu.VMEM((COLS, CH, COLS), F32), SAMPLE_BF, SAMPLE_BF,
@@ -246,12 +245,12 @@
         ],
         compiler_params=pltpu.CompilerParams(vmem_limit_bytes=62 << 20),
         name="pair_updates",
-    )(sc, zt, *zr, *masks, norms, xgs, w_ab, w_sq, w_bias)
+    )(sc, *z_parts, *masks, norms, xgs, w_ab, w_sq, w_bias)
 
 
 def l1_kernel(ids, z_in, mask_in, norms, w_ab, a_out, b_out, mask, tile_a, tile_b):
     out_norm = (norms[0], norms[1])
-    mask[...] = mask_in[0].astype(F32)
+    mask[:] = mask_in[0].astype(F32)
 
     @pl.loop(0, ROWS // TILE)
     def _(t):
@@ -260,8 +259,8 @@
             TILE,
             lambda i, _: mm(w_ab[0], (mask[pl.ds(base + i, 1), :] * channel_norm(z_in[0, base + i], out_norm)).astype(BF16)),
             lambda i, proj: ab_row(proj, tile_a, tile_b, i))
-        a_out[0, :, pl.ds(base, TILE), :] = jnp.swapaxes(tile_a[...], 0, 1)
-        b_out[0, :, pl.ds(base, TILE), :] = jnp.swapaxes(tile_b[...], 0, 1)
+        a_out[0, :, pl.ds(base, TILE), :] = jnp.swapaxes(tile_a[:], 0, 1)
+        b_out[0, :, pl.ds(base, TILE), :] = jnp.swapaxes(tile_b[:], 0, 1)
 
 
 def l1_call(ids, zt, mask, norms, w_ab):
@@ -297,7 +296,7 @@
     def _(t):
         base = pl.multiple_of(TILE * t, TILE)
         x_norm_tile(x_s, tile_x, base, xgs.at[0], xgs.at[1])
-        both = jnp.swapaxes(tile_x[...], 0, 1)
+        both = jnp.swapaxes(tile_x[:], 0, 1)
         for n in range(2):
             x_out[n, pl.ds(base, TILE)] = both[:, :, LANES * n:LANES * n + LANES]
 
@@ -343,10 +342,10 @@
         return channel_norm(z_two, att_norm).astype(BF16)
 
     def bias_row(i, normed):
-        tile_d[i] = mm(w_bias[...], normed)
+        tile_d[i] = mm(w_bias[:], normed)
 
     staggered(TILE, outgoing, norm_one, incoming, norm_two, bias_row)
-    bias_out[...] = jnp.swapaxes(tile_d[...], 0, 1)[:4].astype(BF16)
+    bias_out[:] = jnp.swapaxes(tile_d[:], 0, 1)[:4].astype(BF16)
 
 
 def r_call(sc, zt, x_near, far, norms, w_sq, w_bias):
@@ -372,15 +371,16 @@
 CHUNK = 32
 SLOTS = 2
 STEPS = 6
+AWAY_FIRST = 48
 
 
 def attention_kernel(n, fresh, away, sc, *refs):
     z_refs, bias_refs = refs[:n], refs[n:2 * n]
     mask_in, norms, w_all, w_proj = refs[2 * n:2 * n + 4]
     rest = refs[2 * n + 4 + away + (not fresh):]
-    mask_away, out_away = refs[2 * n + 4], rest[1]
+    mask_away, out_away = refs[2 * n + 4], rest[1:1 + 2 * away]
     (out, z_in, z_out, mask_i, mask, bias_rows, bias_t, q_s, k_s, v_s, g_s, vn_s, gn_s, keep_s, s_buf, e_buf, p_s,
-     top_s, inv_s, o_s, m_sem, z_sem, o_sem) = rest[:1] + rest[1 + away:]
+     top_s, inv_s, o_s, m_sem, z_sem, o_sem) = rest[:1] + rest[1 + 2 * away:]
     n_rows = n * ROWS
 
     def z_copy(j):
@@ -391,8 +391,13 @@
         return pltpu.make_async_copy(src, mask_i.at[pl.ds(ROWS * j, ROWS)], m_sem.at[j])
 
     def o_copy(j):
-        dst = out_away if away and j == n - 1 else out.at[sc[j]]
-        return pltpu.make_async_copy(z_out.at[pl.ds(ROWS * j, ROWS)], dst, o_sem.at[j])
+        return pltpu.make_async_copy(z_out.at[pl.ds(ROWS * j, ROWS)], out.at[sc[j]], o_sem.at[j])
+
+    def o_copies(j):
+        if not (away and j == n - 1):
+            return [o_copy(j)]
+        return [pltpu.make_async_copy(z_out.at[pl.ds(ROWS * j + start, ref.shape[0])], ref, o_sem.at[j])
+                for ref, start in zip(out_away, (0, AWAY_FIRST))]
 
     for j in range(n):
         m_copy(j).start()
@@ -403,8 +408,8 @@
     for j in range(n):
         m_copy(j).wait()
     z_copy(0).wait()
-    mask[...] = mask_i[...].astype(F32)
-    q_s[...] = jnp.zeros_like(q_s)
+    mask[:] = mask_i[:].astype(F32)
+    q_s[:] = jnp.zeros_like(q_s)
 
     @pl.loop(0, n * HEADS)
     def _(h):
@@ -413,7 +418,7 @@
     def project(row, slot):
         row = jnp.minimum(row, n_rows - 1)
         normed = channel_norm(z_in[row], (norms[0], norms[1])).astype(BF16)
-        proj = mm(w_all[...], normed)
+        proj = mm(w_all[:], normed)
         k_s[slot] = proj[CH:2 * CH].T.astype(BF16)
         q = proj[:CH].astype(BF16)
         for h in range(HEADS):
@@ -458,13 +463,13 @@
         top_s[buf] = jnp.broadcast_to(jnp.max(top, axis=0, keepdims=True), (8, COLS))
         inv_s[prev] = jnp.broadcast_to(1.0 / jnp.sum(total, axis=0, keepdims=True), (8, COLS))
         if defer:
-            p_s[...] = jnp.concatenate(probs, axis=0)
+            p_s[:] = jnp.concatenate(probs, axis=0)
         else:
             weigh(1 - slot if h < 2 else slot, (h - 2) % HEADS, jnp.concatenate(probs, axis=0))
 
     def finish(row, slot):
         gated = (g_s[slot] * o_s[slot]).astype(BF16)
-        z_out[jnp.maximum(row, 0)] = z_in[jnp.clip(row, 0, n_rows - 1)] + mm(w_proj[...], gated)
+        z_out[jnp.maximum(row, 0)] = z_in[jnp.clip(row, 0, n_rows - 1)] + mm(w_proj[:], gated)
 
     project(0, 0)
     keep_mask(0, 0)
@@ -474,7 +479,7 @@
     def _(it):
         first = STEPS * it - 1
         lg = scores(1, 0)
-        weigh(0, 1, p_s[...])
+        weigh(0, 1, p_s[:])
         for k in range(STEPS):
             row, slot, last = first + k, 1 - k % 2, k == STEPS - 1
             for h in range(HEADS):
@@ -497,15 +502,18 @@
             def _():
                 o_copy(j - 1).start()
 
-    o_copy(n - 1).start()
+    for copy in o_copies(n - 1):
+        copy.start()
     for j in range(n):
-        o_copy(j).wait()
+        for copy in o_copies(j):
+            copy.wait()
 
 
 def attend(sc, z_parts, biases, mask, norms, w_all, w_proj, out, mask_away=None):
     n, fresh, away = len(z_parts), out is None, mask_away is not None
     args = (sc, *z_parts, *biases, mask, norms, w_all, w_proj) + ((mask_away,) if away else ()) + (() if fresh else (out,))
     whole = jax.ShapeDtypeStruct((mask.shape[0], ROWS, CH, COLS), F32)
+    aways = [jax.ShapeDtypeStruct((k, CH, COLS), F32) for k in (AWAY_FIRST, ROWS - AWAY_FIRST)]
     rows = n * ROWS
     pair = pltpu.VMEM((SLOTS, CH, COLS), BF16)
     wide = pltpu.VMEM((SLOTS, CH, COLS), F32)
@@ -515,9 +523,9 @@
     sems = pltpu.SemaphoreType.DMA((n,))
     return pl.pallas_call(
         functools.partial(attention_kernel, n, fresh, away),
-        out_shape=(whole, ROW_WIDE) if away else whole,
+        out_shape=(whole, *aways) if away else whole,
         in_specs=[SM] + [HB] * n + [VM] * n + [HB] + [VM] * 3 + [HB] * (away + (not fresh)),
-        out_specs=(HB, HB) if away else HB,
+        out_specs=(HB, HB, HB) if away else HB,
         scratch_shapes=[
             pltpu.VMEM((rows, CH, COLS), F32), pltpu.VMEM((rows + STEPS, CH, COLS), F32), pltpu.VMEM((rows, COLS), jnp.int32),
             pltpu.VMEM((rows, COLS), F32), each, each, pltpu.VMEM((SLOTS, HEADS, CH, COLS), BF16),
@@ -530,6 +538,9 @@
     )(*args)
 
 
+FIRST = 8
+
+
 def exchange(values, r):
     return lax.ppermute(values, 'dap', [(i, i ^ r) for i in range(4)])
 
@@ -549,20 +560,24 @@
         zt = jnp.transpose(pair_z, (0, 1, 3, 2))
         n_own = zt.shape[0] // 4
         mask_bf = pair_mask.astype(BF16)
-        arrived, before = [], ()
+        arrived, layouts, before = [], [], ()
         for t in range(n_own):
-            got = {}
-            for r in (2, 3, 1):
-                send = lax.dynamic_index_in_dim(lax.optimization_barrier((zt, *before))[0], n_own * (me ^ r) + t, 0, keepdims=False)
+            pieces = [(2, 0, FIRST), (2, FIRST, ROWS)] if t == 0 else [(2, 0, ROWS)]
+            pieces += [(3, 0, ROWS), (1, 0, ROWS)]
+            got = []
+            for r, start, stop in pieces:
+                where = (n_own * (me ^ r) + t, start, 0, 0)
+                send = lax.dynamic_slice(lax.optimization_barrier((zt, *before))[0], where, (1, stop - start, CH, COLS))[0]
                 if t == 0 or r == 1:
                     before = (send,)
-                got[r] = exchange(send, r)
-                if t == 0 and r == 2:
+                got.append(exchange(send, r))
+                if t == 0 and stop == ROWS and r == 2:
                     mask_bf, weights = lax.optimization_barrier((mask_bf, weights, send))[:2]
                     masks = [lax.dynamic_slice_in_dim(mask_bf, n_own * (me ^ k), n_own, axis=0) for k in range(4)]
                     before = (*before, *masks)
                     masks = [exchange(m, k) if k else m for k, m in enumerate(masks)]
-            arrived.append((got[1], got[2], got[3]))
+            arrived.append([zt, *got])
+            layouts.append(((0, 0), *((r, start) for r, start, _ in pieces)))
 
         out_n, out_x, out_ab, out_sq = update_weights(weights[:10])
         in_n, in_x, in_ab, in_sq = update_weights(weights[10:20])
@@ -600,14 +615,14 @@
         held = []
         for t in range(n_own):
             last = t == n_own - 1
-            z_own, z_par, bias, far2, far3 = ordered(functools.partial(u_call, last), [me, n_own * me + t], zt,
+            z_own, z_par, bias, far2, far3 = ordered(functools.partial(u_call, last, layouts[t]), [me, n_own * me + t],
                                                      arrived[t], [m[t] for m in masks], norms, xgs, w_ab, w_sq, w_bias8)
             near = (n_own * (me ^ 1) + t, 0, exchange(z_par, 1), exchange(bias, 1))
             held.append({2: exchange(far2, 2)})
             own = (n_own * me + t, 0, z_own, bias)
             if last:
-                out, away = attention([own, (0, 0, far3, bias)], out, masks[3][t][None].astype(jnp.int32))
-                away = exchange(away, 3)
+                out, *away = attention([own, (0, 0, far3, bias)], out, masks[3][t][None].astype(jnp.int32))
+                away = [exchange(v, 3) for v in away]
             else:
                 held[t][3] = exchange(far3, 3)
                 out = attention([own, near], out)
@@ -625,7 +640,8 @@
                 biases = {r: jnp.stack([mine[r][0], par[2 * r - 4], mine[r][1], par[2 * r - 3]]) for r in (2, 3)}
             out = attention(([] if t else [near]) + [
                 (n_own * (me ^ r) + t, me, z_two[r], biases[r]) for r in biases], out)
-        out = lax.dynamic_update_index_in_dim(out, away, n_own * (me ^ 3) + n_own - 1, 0)
+        for v, start in zip(away, (0, AWAY_FIRST)):
+            out = lax.dynamic_update_slice(out, v[None], (n_own * (me ^ 3) + n_own - 1, start, 0, 0))
         return jnp.transpose(out, (0, 1, 3, 2))
 
     pair_spec = P('data', 'dap')

time: 1370 us -> 1270 us (0.927)
  waiting for transfers between devices: 484 us -> 389 us
    ppermute x27 -> x29, waiting for transfers between devices: 484 us -> 389 us  [exchange(): return lax.ppermute(values, 'dap', [(i, i ^ r) for i in range(4)])]
    squeeze x5 -> x6, local copies, waits for them, and re-layouts: 33.6 us -> 34.3 us  [local_block(): lax.dynamic_slice(lax.optimization_barrier((zt, *before))[0], where, (1,...]
  transfers between devices with their start and end apart: 27 -> 29, of which waited for: 12 -> 11; matrix products, arithmetic and copies ran while one was open for 3% -> 4% of each run, Pallas kernels for 48% -> 52%
where the time goes in v3:
time: 1270 us; the launch traced here: 1260 us
  Pallas kernels  775 us (61%)
  waiting for transfers between devices  389 us (31%)
  local copies, waits for them, and re-layouts  68.7 us (5%)
  starting transfers between devices  20.1 us (2%)
    pallas_call x6, Pallas kernels, attend(): pl.pallas_call(functools.partial(attention_kernel, n, fresh, away), out_s...  390 us
    ppermute x29, waiting for transfers between devices, exchange(): return lax.ppermute(values, 'dap', [(i, i ^ r) for i in range(4)])  389 us
    pallas_call x3, Pallas kernels, u_call(): pl.pallas_call(functools.partial(u_kernel, last, layout), out_shape=(ROW_...  277 us
    pallas_call x5, Pallas kernels, r_call(): pl.pallas_call(r_kernel, out_shape=(ROW_WIDE, jax.ShapeDtypeStruct((4, RO...  46.5 us
    squeeze x6, local copies, waits for them, and re-layouts, local_block(): lax.dynamic_slice(lax.optimization_barrier((zt, *before))[0], where, (1,...  34.3 us
    pallas_call x1, Pallas kernels, l2_call(): pl.pallas_call(l2_kernel, grid=(n // 2,), out_shape=jax.ShapeDtypeStruct(...  32.9 us
    pallas_call x1, Pallas kernels, l1_call(): pl.pallas_call(l1_kernel, out_shape=(ab, ab), grid_spec=pltpu.PrefetchSca...  28.7 us
  transfers between devices with their start and end apart: 29, of which 11 were waited for; matrix products, arithmetic and copies ran while one was open for 4% of the time, Pallas kernels for 52%

profile of v3, /device:TPU:0, one launch (start us, length us, event | category | flops | bytes accessed | tf_op | source)
XLA Modules:
  0.0 1259.3 jit_solution(902614571433815411)
XLA Ops:
  0.0 1.1 dynamic-slice_bitcast_fusion.9
  1.3 4.4 dynamic-slice_bitcast_fusion.8
  7.3 28.7 %near_projections.1 = (bf16[6,64,64,256]{3,2,1,0:T(8,128)(2,1)S(1)}, bf16[6,64,64,256]{3,2,1,0:T(8,128)(2,1)}) custom-call(s32[6]{0:T(128)S(1)} %stack.230.ids, f32[12,64,64,256]{3,2,1,0:T(8,128)} %bitcast.148, s32[12,64,256]{2,1,0:T(8,128)S(1)} %copy-done.1, f32[6,64,256]{2,1,0:T(8,128)S(1)} %broadcast_dynamic-update-slice_fusion.norms.refs_9_.refs_8_, ...), custom_call_target="tpu_custom_call" | custom-call | tf_op jit(solution)/shard_map/near_projections/pallas_call | solution.py:270
  36.0 4.6 copy-done.5
  40.6 0.8 collective-permute-start
  41.5 4.6 dynamic-slice_bitcast_fusion.7
  46.2 4.7 dynamic-slice_bitcast_fusion.6
  50.9 2.6 collective-permute-start.3
  53.9 1.5 collective-permute-start.7
  57.0 0.7 dynamic-slice_bitcast_fusion.10
  57.8 167.5 %collective-permute-done.7 = bf16[3,64,256]{2,1,0:T(8,128)(2,1)S(1)} collective-permute-done((bf16[3,64,256]{2,1,0:T(8,128)(2,1)S(1)}, bf16[3,64,256]{2,1,0:T(8,128)(2,1)S(1)}, u32[]{:S(2)}, u32[]{:S(2)}) %collective-permute-start.7) | collective-permute-done | bytes 98336 | tf_op jit(solution)/shard_map/ppermute | solution.py:545
  225.2 2.3 collective-permute-start.6
  227.5 0.6 pad_maximum_fusion.10.refs_12_.refs_11_.w_sq
  228.2 2.4 collective-permute-done.6
  230.6 0.7 pad_add_fusion.12.sc
  231.3 0.6 collective-permute-done.5
  231.9 1.7 collective-permute-start.1
  233.6 0.6 slice_convert_fusion
  234.3 0.6 slice_bitcast_fusion.7
  235.6 32.9 %near_product.1.x_near = bf16[6,64,64,128]{3,2,1,0:T(8,128)(2,1)S(1)} custom-call(s32[1]{0:T(128)} %bitcast.1.sc, bf16[6,64,64,256]{3,2,1,0:T(8,128)(2,1)} %copy-done.5, bf16[6,64,64,256]{3,2,1,0:T(8,128)(2,1)} %get-tuple-element.99.b_own, bf16[6,64,64,256]{3,2,1,0:T(8,128)(2,1)} %collective-permute-done.b_par, ...), custom_call_target="tpu_custom_call" | custom-call | tf_op jit(solution)/shard_map/near_product/pallas_call | solution.py:307
  268.4 2.6 copy-done
  271.0 0.8 copy-done.20
  271.9 92.5 %pair_updates.3 = (f32[64,64,256]{2,1,0:T(8,128)}, f32[64,64,256]{2,1,0:T(8,128)}, bf16[4,4,64,256]{3,2,1,0:T(8,128)(2,1)}, bf16[100,64,256]{2,1,0:T(8,128)(2,1)}, bf16[100,64,256]{2,1,0:T(8,128)(2,1)}) custom-call(s32[2]{0:T(128)} %pad_add_fusion.12.sc, f32[12,64,64,256]{3,2,1,0:T(8,128)} %bitcast.151, f32[8,64,256]{2,1,0:T(8,128)} %copy-done.20, ...), custom_call_target="tpu_custom_call" | custom-call | tf_op jit(solution)/shard_map/pair_updates/pallas_call | solution.py:235
  364.4 9.7 dynamic-slice_bitcast_fusion.3
  374.1 1.8 collective-permute-start.11
  376.5 9.7 dynamic-slice_bitcast_fusion
  387.9 65.5 %triangle_attention.6.refs_8_ = f32[12,64,64,256]{3,2,1,0:T(8,128)} custom-call(s32[4]{0:T(128)S(1)} %get-tuple-element.116.sc, f32[64,64,256]{2,1,0:T(8,128)} %get-tuple-element.117.refs_0_, f32[64,64,256]{2,1,0:T(8,128)} %collective-permute-done.8.refs_1_, bf16[4,4,64,256]{3,2,1,0:T(8,128)(2,1)S(1)} %copy-done.14, ...), custom_call_target="tpu_custom_call" | custom-call | tf_op jit(solution)/shard_map/triangle_attention/pallas_call | solution.py:524
  453.4 14.5 %collective-permute-done.10.refs_1_ = f32[64,64,256]{2,1,0:T(8,128)} collective-permute-done((f32[64,64,256]{2,1,0:T(8,128)}, f32[64,64,256]{2,1,0:T(8,128)}, u32[]{:S(2)}, u32[]{:S(2)}) %collective-permute-start.10) | collective-permute-done | bytes 4194336 | tf_op jit(solution)/shard_map/ppermute | solution.py:545
  467.9 88.8 %collective-permute-done.11.refs_2_ = f32[64,64,256]{2,1,0:T(8,128)} collective-permute-done((f32[64,64,256]{2,1,0:T(8,128)}, f32[64,64,256]{2,1,0:T(8,128)}, u32[]{:S(2)}, u32[]{:S(2)}) %collective-permute-start.11) | collective-permute-done | bytes 4194336 | tf_op jit(solution)/shard_map/ppermute | solution.py:545
  556.7 92.4 %pair_updates.4 = (f32[64,64,256]{2,1,0:T(8,128)}, f32[64,64,256]{2,1,0:T(8,128)}, bf16[4,4,64,256]{3,2,1,0:T(8,128)(2,1)}, bf16[100,64,256]{2,1,0:T(8,128)(2,1)}, bf16[100,64,256]{2,1,0:T(8,128)(2,1)}) custom-call(s32[2]{0:T(128)} %pad_add_fusion.11.sc, f32[12,64,64,256]{3,2,1,0:T(8,128)} %bitcast.154, f32[64,64,256]{2,1,0:T(8,128)} %collective-permute-done.10.refs_1_, ...), custom_call_target="tpu_custom_call" | custom-call | tf_op jit(solution)/shard_map/pair_updates/pallas_call | solution.py:235
  649.2 0.9 collective-permute-start.13
  650.2 2.1 collective-permute-start.18
  652.2 11.6 collective-permute-done.14.refs_3_
  663.8 2.0 collective-permute-start.23
  666.5 1.0 copy-done.15
  667.5 65.3 %triangle_attention.7.refs_9_ = f32[12,64,64,256]{3,2,1,0:T(8,128)} custom-call(s32[4]{0:T(128)S(1)} %get-tuple-element.128.sc, f32[64,64,256]{2,1,0:T(8,128)} %get-tuple-element.129.refs_0_, f32[64,64,256]{2,1,0:T(8,128)} %copy-done.19, bf16[4,4,64,256]{3,2,1,0:T(8,128)(2,1)S(1)} %copy-done.15, ...), custom_call_target="tpu_custom_call", output_to_operand_aliasing={{}: (9, {})} | custom-call | tf_op jit(solution)/shard_map/triangle_attention/pallas_call | solution.py:524
  732.8 10.3 collective-permute-done.16.refs_2_
  743.1 92.0 %pair_updates.5 = (f32[64,64,256]{2,1,0:T(8,128)}, f32[64,64,256]{2,1,0:T(8,128)}, bf16[4,4,64,256]{3,2,1,0:T(8,128)(2,1)}, bf16[108,64,256]{2,1,0:T(8,128)(2,1)}, f32[64,64,256]{2,1,0:T(8,128)}) custom-call(s32[2]{0:T(128)} %pad_add_fusion.10.sc, f32[12,64,64,256]{3,2,1,0:T(8,128)} %bitcast.155, f32[64,64,256]{2,1,0:T(8,128)} %collective-permute-done.15.refs_1_, ...), custom_call_target="tpu_custom_call" | custom-call | tf_op jit(solution)/shard_map/pair_updates/pallas_call | solution.py:235
  835.1 0.7 collective-permute-start.20
  835.8 1.7 collective-permute-start.26
  837.7 1.2 copy-done.12
  838.9 65.4 %triangle_attention.8 = (f32[12,64,64,256]{3,2,1,0:T(8,128)}, f32[48,64,256]{2,1,0:T(8,128)}, f32[16,64,256]{2,1,0:T(8,128)S(1)}) custom-call(s32[4]{0:T(128)S(1)} %get-tuple-element.135.sc, f32[64,64,256]{2,1,0:T(8,128)} %get-tuple-element.136.refs_0_, f32[64,64,256]{2,1,0:T(8,128)} %get-tuple-element.134.refs_1_, ...), custom_call_target="tpu_custom_call", output_to_operand_aliasing={{0}: (10, {})} | custom-call | tf_op jit(solution)/shard_map/triangle_attention/pallas_call | solution.py:524
  904.3 1.0 copy-done.17
  905.5 0.9 slice_bitcast_fusion.5
  906.4 0.9 slice_bitcast_fusion.6
  907.4 9.2 row_updates.5
  916.5 1.9 copy-done.7
  918.5 9.6 row_updates.6
  928.1 1.9 copy-done.8
  930.1 24.1 %collective-permute-done.23.x_far.xi = bf16[100,64,256]{2,1,0:T(8,128)(2,1)} collective-permute-done((bf16[100,64,256]{2,1,0:T(8,128)(2,1)}, bf16[100,64,256]{2,1,0:T(8,128)(2,1)}, u32[]{:S(2)}, u32[]{:S(2)}) %collective-permute-start.23) | collective-permute-done | bytes 3276832 | tf_op jit(solution)/shard_map/ppermute | solution.py:545
  954.2 0.9 slice_bitcast_fusion.3
  955.1 68.8 %collective-permute-done.24.x_far.xi = bf16[100,64,256]{2,1,0:T(8,128)(2,1)} collective-permute-done((bf16[100,64,256]{2,1,0:T(8,128)(2,1)}, bf16[100,64,256]{2,1,0:T(8,128)(2,1)}, u32[]{:S(2)}, u32[]{:S(2)}) %collective-permute-start.24) | collective-permute-done | bytes 3276832 | tf_op jit(solution)/shard_map/ppermute | solution.py:545
  1024.2 0.9 slice_bitcast_fusion.4
  1025.9 95.5 %triangle_attention.9.refs_8_ = f32[12,64,64,256]{3,2,1,0:T(8,128)} custom-call(s32[6]{0:T(128)S(1)} %stack.215.sc, f32[64,64,256]{2,1,0:T(8,128)} %collective-permute-done.20.refs_0_, f32[64,64,256]{2,1,0:T(8,128)} %copy-done.7, f32[64,64,256]{2,1,0:T(8,128)} %copy-done.8, ...), custom_call_target="tpu_custom_call", output_to_operand_aliasing={{}: (11, {})} | custom-call | tf_op jit(solution)/shard_map/triangle_attention/pallas_call | solution.py:524
  1121.4 9.2 row_updates.7
  1130.6 2.0 copy-done.9
  1132.6 9.1 row_updates.8
  1141.7 1.9 copy-done.10
  1144.3 1.1 slice_bitcast_fusion.2
  1145.9 65.3 %triangle_attention.10.refs_6_ = f32[12,64,64,256]{3,2,1,0:T(8,128)} custom-call(s32[4]{0:T(128)S(1)} %pad_add_fusion.5.sc, f32[64,64,256]{2,1,0:T(8,128)} %copy-done.9, f32[64,64,256]{2,1,0:T(8,128)} %copy-done.10, bf16[4,4,64,256]{3,2,1,0:T(8,128)(2,1)S(1)} %pad_maximum_fusion.6.refs_2_, ...), custom_call_target="tpu_custom_call", output_to_operand_aliasing={{}: (9, {})} | custom-call | tf_op jit(solution)/shard_map/triangle_attention/pallas_call | solution.py:524
  1211.2 9.4 row_updates.9
  1220.7 33.4 %triangle_attention.11 = f32[12,64,64,256]{3,2,1,0:T(8,128)} custom-call(s32[2]{0:T(128)S(1)} %pad_add_fusion.3.sc, f32[64,64,256]{2,1,0:T(8,128)S(1)} %get-tuple-element.161.refs_0_, bf16[4,4,64,256]{3,2,1,0:T(8,128)(2,1)S(1)} %pad_maximum_fusion.7.refs_1_, s32[12,64,256]{2,1,0:T(8,128)S(1)} %copy-done.1, ...), custom_call_target="tpu_custom_call", output_to_operand_aliasing={{}: (7, {})} | custom-call | tf_op jit(solution)/shard_map/triangle_attention/pallas_call | solution.py:524
  1254.1 3.9 bitcast_dynamic-update-slice_fusion
  1258.0 1.1 bitcast_dynamic-update-slice_fusion.1
  (194 shorter events, 9.8 us)
Async XLA Ops:
  0.0 5.7 copy-start.1
  1.2 5.1 copy-start.26
  1.2 5.2 copy-start.27
  1.2 5.3 copy-start.28
  1.3 5.4 copy-start.41
  1.3 5.6 copy-start.42
  1.3 5.6 copy-start.43
  1.3 5.7 copy-start.44
  1.3 5.8 copy-start.38
  1.3 5.8 copy-start.39
  6.8 29.2 %copy-start.11 = (bf16[2,256,64]{2,1,0:T(8,128)(2,1)}, bf16[2,256,64]{2,1,0:T(8,128)(2,1)S(1)}, u32[]{:S(2)}) copy-start(bf16[2,256,64]{2,1,0:T(8,128)(2,1)S(1)} %pad_maximum_fusion.8.w_ab.refs_11_.refs_10_) | copy-start | bytes 196612
  7.2 28.8 %copy-start.2 = (f32[6,64,256]{2,1,0:T(8,128)}, f32[6,64,256]{2,1,0:T(8,128)S(1)}, u32[]{:S(2)}) copy-start(f32[6,64,256]{2,1,0:T(8,128)S(1)} %broadcast_dynamic-update-slice_fusion.norms.refs_9_.refs_8_) | copy-start | bytes 1179652
  40.6 194.9 %collective-permute-start = (bf16[6,64,64,256]{3,2,1,0:T(8,128)(2,1)}, bf16[6,64,64,256]{3,2,1,0:T(8,128)(2,1)}, u32[]{:S(2)}, u32[]{:S(2)}) collective-permute-start(bf16[6,64,64,256]{3,2,1,0:T(8,128)(2,1)} %get-tuple-element.99.b_own), channel_id=1, source_target_pairs={{0,1},{1,0},{2,3},{3,2},{4,5},{5,4},{6,7},{7,6}} | collective-permute-start | bytes 37748744 | tf_op jit(solution)/shard_map/ppermute | solution.py:545
  46.1 9.2 copy-start.29
  46.1 9.3 copy-start.30
  46.1 9.4 copy-start.31
  46.1 9.5 copy-start.32
  46.1 9.7 copy-start.40
  46.1 10.3 copy-start.45
  46.1 10.4 copy-start.46
  46.1 10.5 copy-start.47
  46.2 10.6 copy-start.48
  50.9 220.1 %collective-permute-start.4 = (f32[64,64,256]{2,1,0:T(8,128)}, f32[64,64,256]{2,1,0:T(8,128)}, u32[]{:S(2)}, u32[]{:S(2)}) collective-permute-start(f32[64,64,256]{2,1,0:T(8,128)} %dynamic-slice_bitcast_fusion.6), channel_id=1, source_target_pairs={{0,1},{1,0},{2,3},{3,2},{4,5},{5,4},{6,7},{7,6}} | collective-permute-start | bytes 12582920 | tf_op jit(solution)/shard_map/ppermute | solution.py:545
  50.9 220.2 %collective-permute-start.3 = (f32[64,64,256]{2,1,0:T(8,128)}, f32[64,64,256]{2,1,0:T(8,128)}, u32[]{:S(2)}, u32[]{:S(2)}) collective-permute-start(f32[64,64,256]{2,1,0:T(8,128)} %dynamic-slice_bitcast_fusion.7), channel_id=1, source_target_pairs={{0,3},{1,2},{2,1},{3,0},{4,7},{5,6},{6,5},{7,4}} | collective-permute-start | bytes 12582920 | tf_op jit(solution)/shard_map/ppermute | solution.py:545
  53.5 217.5 %collective-permute-start.2 = (f32[56,64,256]{2,1,0:T(8,128)}, f32[56,64,256]{2,1,0:T(8,128)}, u32[]{:S(2)}, u32[]{:S(2)}) collective-permute-start(f32[56,64,256]{2,1,0:T(8,128)} %dynamic-slice_bitcast_fusion.8), channel_id=1, source_target_pairs={{0,2},{1,3},{2,0},{3,1},{4,6},{5,7},{6,4},{7,5}} | collective-permute-start | bytes 11010056 | tf_op jit(solution)/shard_map/ppermute | solution.py:545
  53.9 171.4 %collective-permute-start.7 = (bf16[3,64,256]{2,1,0:T(8,128)(2,1)S(1)}, bf16[3,64,256]{2,1,0:T(8,128)(2,1)S(1)}, u32[]{:S(2)}, u32[]{:S(2)}) collective-permute-start(bf16[3,64,256]{2,1,0:T(8,128)(2,1)S(1)} %get-tuple-element.183), channel_id=1, source_target_pairs={{0,3},{1,2},{2,1},{3,0},{4,7},{5,6},{6,5},{7,4}} | collective-permute-start | bytes 294920 | tf_op jit(solution)/shard_map/ppermute | solution.py:545
  57.0 211.4 %copy-start.4 = (f32[4,64,8,128]{3,2,1,0:T(8,128)}, f32[4,64,8,128]{3,2,1,0:T(8,128)S(1)}, u32[]{:S(2)}) copy-start(f32[4,64,8,128]{3,2,1,0:T(8,128)S(1)} %pad_maximum_fusion.xgs.refs_10_.refs_9_) | copy-start | bytes 3145732
  225.2 5.4 collective-permute-start.6
  230.6 1.3 collective-permute-start.5
  231.9 39.1 %collective-permute-start.1 = (f32[8,64,256]{2,1,0:T(8,128)S(1)}, f32[8,64,256]{2,1,0:T(8,128)S(1)}, u32[]{:S(2)}, u32[]{:S(2)}) collective-permute-start(f32[8,64,256]{2,1,0:T(8,128)S(1)} %dynamic-slice_bitcast_fusion.9), channel_id=1, source_target_pairs={{0,2},{1,3},{2,0},{3,1},{4,6},{5,7},{6,4},{7,5}} | collective-permute-start | bytes 1572872 | tf_op jit(solution)/shard_map/ppermute | solution.py:545
  364.4 11.9 copy-start.14
  364.4 23.5 %collective-permute-start.8 = (f32[64,64,256]{2,1,0:T(8,128)}, f32[64,64,256]{2,1,0:T(8,128)}, u32[]{:S(2)}, u32[]{:S(2)}) collective-permute-start(f32[64,64,256]{2,1,0:T(8,128)} %get-tuple-element.118), channel_id=1, source_target_pairs={{0,1},{1,0},{2,3},{3,2},{4,5},{5,4},{6,7},{7,6}} | collective-permute-start | bytes 12582920 | tf_op jit(solution)/shard_map/ppermute | solution.py:545
  374.1 93.8 %collective-permute-start.10 = (f32[64,64,256]{2,1,0:T(8,128)}, f32[64,64,256]{2,1,0:T(8,128)}, u32[]{:S(2)}, u32[]{:S(2)}) collective-permute-start(f32[64,64,256]{2,1,0:T(8,128)} %get-tuple-element.168), channel_id=1, source_target_pairs={{0,2},{1,3},{2,0},{3,1},{4,6},{5,7},{6,4},{7,5}} | collective-permute-start | bytes 12582920 | tf_op jit(solution)/shard_map/ppermute | solution.py:545
  374.1 182.6 %collective-permute-start.11 = (f32[64,64,256]{2,1,0:T(8,128)}, f32[64,64,256]{2,1,0:T(8,128)}, u32[]{:S(2)}, u32[]{:S(2)}) collective-permute-start(f32[64,64,256]{2,1,0:T(8,128)} %get-tuple-element.167), channel_id=1, source_target_pairs={{0,3},{1,2},{2,1},{3,0},{4,7},{5,6},{6,5},{7,4}} | collective-permute-start | bytes 12582920 | tf_op jit(solution)/shard_map/ppermute | solution.py:545
  375.9 180.8 %collective-permute-start.12 = (f32[64,64,256]{2,1,0:T(8,128)}, f32[64,64,256]{2,1,0:T(8,128)}, u32[]{:S(2)}, u32[]{:S(2)}) collective-permute-start(f32[64,64,256]{2,1,0:T(8,128)} %get-tuple-element.166), channel_id=1, source_target_pairs={{0,1},{1,0},{2,3},{3,2},{4,5},{5,4},{6,7},{7,6}} | collective-permute-start | bytes 12582920 | tf_op jit(solution)/shard_map/ppermute | solution.py:545
  376.3 9.9 collective-permute-start.9
  376.4 10.0 copy-start.33
  376.5 10.1 copy-start.34
  376.5 10.2 copy-start.35
  376.5 10.3 copy-start.36
  376.5 10.4 copy-start.37
  386.2 266.0 %collective-permute-start.15 = (f32[64,64,256]{2,1,0:T(8,128)}, f32[64,64,256]{2,1,0:T(8,128)}, u32[]{:S(2)}, u32[]{:S(2)}) collective-permute-start(f32[64,64,256]{2,1,0:T(8,128)} %get-tuple-element.165), channel_id=1, source_target_pairs={{0,2},{1,3},{2,0},{3,1},{4,6},{5,7},{6,4},{7,5}} | collective-permute-start | bytes 12582920 | tf_op jit(solution)/shard_map/ppermute | solution.py:545
  649.2 14.7 %collective-permute-start.13 = (f32[64,64,256]{2,1,0:T(8,128)}, f32[64,64,256]{2,1,0:T(8,128)S(1)}, u32[]{:S(2)}, u32[]{:S(2)}) collective-permute-start(f32[64,64,256]{2,1,0:T(8,128)} %get-tuple-element.130), channel_id=1, source_target_pairs={{0,1},{1,0},{2,3},{3,2},{4,5},{5,4},{6,7},{7,6}} | collective-permute-start | bytes 12582920 | tf_op jit(solution)/shard_map/ppermute | solution.py:545
  650.1 93.0 %collective-permute-start.16 = (f32[64,64,256]{2,1,0:T(8,128)}, f32[64,64,256]{2,1,0:T(8,128)}, u32[]{:S(2)}, u32[]{:S(2)}) collective-permute-start(f32[64,64,256]{2,1,0:T(8,128)} %get-tuple-element.164), channel_id=1, source_target_pairs={{0,3},{1,2},{2,1},{3,0},{4,7},{5,6},{6,5},{7,4}} | collective-permute-start | bytes 12582920 | tf_op jit(solution)/shard_map/ppermute | solution.py:545
  650.1 93.0 %collective-permute-start.17 = (f32[64,64,256]{2,1,0:T(8,128)}, f32[64,64,256]{2,1,0:T(8,128)}, u32[]{:S(2)}, u32[]{:S(2)}) collective-permute-start(f32[64,64,256]{2,1,0:T(8,128)} %get-tuple-element.163), channel_id=1, source_target_pairs={{0,1},{1,0},{2,3},{3,2},{4,5},{5,4},{6,7},{7,6}} | collective-permute-start | bytes 12582920 | tf_op jit(solution)/shard_map/ppermute | solution.py:545
  650.2 185.7 %collective-permute-start.18 = (bf16[100,64,256]{2,1,0:T(8,128)(2,1)}, bf16[100,64,256]{2,1,0:T(8,128)(2,1)}, u32[]{:S(2)}, u32[]{:S(2)}) collective-permute-start(bf16[100,64,256]{2,1,0:T(8,128)(2,1)} %get-tuple-element.140), channel_id=1, source_target_pairs={{0,2},{1,3},{2,0},{3,1},{4,6},{5,7},{6,4},{7,5}} | collective-permute-start | bytes 9830408 | tf_op jit(solution)/shard_map/ppermute | solution.py:545
  652.2 11.6 collective-permute-start.14
  663.8 241.4 %collective-permute-start.19 = (bf16[100,64,256]{2,1,0:T(8,128)(2,1)}, bf16[100,64,256]{2,1,0:T(8,128)(2,1)}, u32[]{:S(2)}, u32[]{:S(2)}) collective-permute-start(bf16[100,64,256]{2,1,0:T(8,128)(2,1)} %get-tuple-element.115), channel_id=1, source_target_pairs={{0,3},{1,2},{2,1},{3,0},{4,7},{5,6},{6,5},{7,4}} | collective-permute-start | bytes 9830408 | tf_op jit(solution)/shard_map/ppermute | solution.py:545
  663.8 290.3 %collective-permute-start.23 = (bf16[100,64,256]{2,1,0:T(8,128)(2,1)}, bf16[100,64,256]{2,1,0:T(8,128)(2,1)}, u32[]{:S(2)}, u32[]{:S(2)}) collective-permute-start(bf16[100,64,256]{2,1,0:T(8,128)(2,1)} %get-tuple-element.150), channel_id=1, source_target_pairs={{0,2},{1,3},{2,0},{3,1},{4,6},{5,7},{6,4},{7,5}} | collective-permute-start | bytes 9830408 | tf_op jit(solution)/shard_map/ppermute | solution.py:545
  835.1 190.8 %collective-permute-start.20 = (f32[64,64,256]{2,1,0:T(8,128)}, f32[64,64,256]{2,1,0:T(8,128)}, u32[]{:S(2)}, u32[]{:S(2)}) collective-permute-start(f32[64,64,256]{2,1,0:T(8,128)} %get-tuple-element.145), channel_id=1, source_target_pairs={{0,1},{1,0},{2,3},{3,2},{4,5},{5,4},{6,7},{7,6}} | collective-permute-start | bytes 12582920 | tf_op jit(solution)/shard_map/ppermute | solution.py:545
  835.8 188.1 %collective-permute-start.24 = (bf16[100,64,256]{2,1,0:T(8,128)(2,1)}, bf16[100,64,256]{2,1,0:T(8,128)(2,1)}, u32[]{:S(2)}, u32[]{:S(2)}) collective-permute-start(bf16[100,64,256]{2,1,0:T(8,128)(2,1)} %get-tuple-element.127), channel_id=1, source_target_pairs={{0,3},{1,2},{2,1},{3,0},{4,7},{5,6},{6,5},{7,4}} | collective-permute-start | bytes 9830408 | tf_op jit(solution)/shard_map/ppermute | solution.py:545
  835.8 308.5 %collective-permute-start.26 = (bf16[108,64,256]{2,1,0:T(8,128)(2,1)}, bf16[108,64,256]{2,1,0:T(8,128)(2,1)}, u32[]{:S(2)}, u32[]{:S(2)}) collective-permute-start(bf16[108,64,256]{2,1,0:T(8,128)(2,1)} %get-tuple-element.158), channel_id=1, source_target_pairs={{0,2},{1,3},{2,0},{3,1},{4,6},{5,7},{6,4},{7,5}} | collective-permute-start | bytes 10616840 | tf_op jit(solution)/shard_map/ppermute | solution.py:545
  837.7 69.6 %slice-start = ((s8[6291456]{0:T(1024)(128)(4,1)}), s8[4194304]{0:T(1024)(128)(4,1)S(1)}, s32[]{:S(2)}) async-start(s8[6291456]{0:T(1024)(128)(4,1)} %bitcast.129), calls=%async_computation | async-start | bytes 8388608
  838.9 68.5 %slice-start.1 = ((s8[6291456]{0:T(1024)(128)(4,1)}), s8[2097152]{0:T(1024)(128)(4,1)S(1)}, s32[]{:S(2)}) async-start(s8[6291456]{0:T(1024)(128)(4,1)} %bitcast.129), calls=%async_computation.1 | async-start | bytes 4194304
  838.9 68.5 %copy-start.3 = (f32[6,64,256]{2,1,0:T(8,128)S(1)}, f32[6,64,256]{2,1,0:T(8,128)}, u32[]{:S(2)}) copy-start(f32[6,64,256]{2,1,0:T(8,128)} %copy-done.2) | copy-start | bytes 1179652
  838.9 68.5 %copy-start.6 = (bf16[4,64,64]{2,1,0:T(8,128)(2,1)S(1)}, bf16[4,64,64]{2,1,0:T(8,128)(2,1)}, u32[]{:S(2)}) copy-start(bf16[4,64,64]{2,1,0:T(8,128)(2,1)} %pad_maximum_fusion.10.refs_12_.refs_11_.w_sq) | copy-start | bytes 98308
  838.9 68.5 %copy-start.16 = (bf16[8,64]{1,0:T(8,128)(2,1)S(1)}, bf16[8,64]{1,0:T(8,128)(2,1)}, u32[]{:S(2)}) copy-start(bf16[8,64]{1,0:T(8,128)(2,1)} %concatenate.53.refs_13_.refs_12_.w_bias) | copy-start | bytes 3076
  905.2 348.9 %collective-permute-start.27 = (f32[48,64,256]{2,1,0:T(8,128)}, f32[48,64,256]{2,1,0:T(8,128)}, u32[]{:S(2)}, u32[]{:S(2)}) collective-permute-start(f32[48,64,256]{2,1,0:T(8,128)} %get-tuple-element.162), channel_id=1, source_target_pairs={{0,3},{1,2},{2,1},{3,0},{4,7},{5,6},{6,5},{7,4}} | collective-permute-start | bytes 9437192 | tf_op jit(solution)/shard_map/ppermute | solution.py:545
  918.5 105.5 %copy-start.13 = (bf16[4,4,64,256]{3,2,1,0:T(8,128)(2,1)S(1)}, bf16[4,4,64,256]{3,2,1,0:T(8,128)(2,1)}, u32[]{:S(2)}) copy-start(bf16[4,4,64,256]{3,2,1,0:T(8,128)(2,1)} %get-tuple-element.137.refs_2_.refs_3_) | copy-start | bytes 1572868
  954.2 71.0 %collective-permute-start.22 = (bf16[4,4,64,256]{3,2,1,0:T(8,128)(2,1)S(1)}, bf16[4,4,64,256]{3,2,1,0:T(8,128)(2,1)S(1)}, u32[]{:S(2)}, u32[]{:S(2)}) collective-permute-start(bf16[4,4,64,256]{3,2,1,0:T(8,128)(2,1)S(1)} %fusion.5), channel_id=1, source_target_pairs={{0,1},{1,0},{2,3},{3,2},{4,5},{5,4},{6,7},{7,6}} | collective-permute-start | bytes 1572872 | tf_op jit(solution)/shard_map/ppermute | solution.py:545
  1024.0 1.9 collective-permute-start.21
  1132.5 11.7 copy-start.18
  1143.7 1.9 collective-permute-start.25
  1144.2 113.8 %collective-permute-start.28 = (f32[16,64,256]{2,1,0:T(8,128)S(1)}, f32[16,64,256]{2,1,0:T(8,128)S(1)}, u32[]{:S(2)}, u32[]{:S(2)}) collective-permute-start(f32[16,64,256]{2,1,0:T(8,128)S(1)} %copy-done.18), channel_id=1, source_target_pairs={{0,3},{1,2},{2,1},{3,0},{4,7},{5,6},{6,5},{7,4}} | collective-permute-start | bytes 3145736 | tf_op jit(solution)/shard_map/ppermute | solution.py:545
  (16 other events, 45.9 us)

commit v4 on v3

--- a/solution.py
+++ b/solution.py
@@ -29,13 +29,25 @@
     return 0.5 * jnp.tanh(0.5 * vals) + 0.5
 
 
+def swap_major(vals):
+    return jnp.swapaxes(vals, 0, 1)
+
+
+def norm_of(norms, place):
+    return norms[2 * place], norms[2 * place + 1]
+
+
+def contract(lhs, rhs, axis_id):
+    return lax.dot_general(lhs, rhs, (((axis_id,), (axis_id,)), ((), ())), preferred_element_type=F32)
+
+
 def mm(lhs, rhs):
     return jnp.dot(lhs, rhs, preferred_element_type=F32)
 
 
 def ab_row(proj, tile_a, tile_b, slot):
     for n, tile in enumerate((tile_a, tile_b)):
-        linear, gate = jnp.split(proj[2 * CH * n:2 * CH * n + 2 * CH], 2, axis=0)
+        linear, gate = jnp.split(proj[2 * CH * n:2 * CH * n + 2 * CH], 2)
         tile[slot] = ((jnp.tanh(gate) + 1.0) * linear).astype(BF16)
 
 
@@ -54,7 +66,7 @@
             rows.append(jnp.concatenate(
                 [(load(c, (sub, half)) - means[2 * sub + half]) * scales[2 * sub + half] * xg[c] + xb[c]
                  for half in range(2)], axis=1))
-        tile_x[c] = jnp.concatenate(rows, axis=0).astype(BF16)
+        tile_x[c] = jnp.concatenate(rows).astype(BF16)
 
 
 LAG = 3
@@ -71,13 +83,14 @@
 
 def u_kernel(last, layout, sc, *refs):
     z_refs = refs[:len(layout)]
-    (mask0, mask1, mask2, mask3, norms, xgs, w_ab, w_sq, w_bias, z2_own, z2_par, bias_out, far2, far3,
-     z_s, a_s, b_s, x_s, mask, stats, tile_a, tile_b, tile_x, tile_c, tile_d, tile_z, in_sem, z_sem, x_sem) = refs[len(layout):]
+    n_far = 3 if last else 1
+    (mask0, mask1, mask2, mask3, norms, xgs, w_ab, w_sq, w_bias, z2_own, z2_par, bias_out, far2, *far3) = refs[len(layout):][:13 + n_far]
+    (z_s, a_s, b_s, x_s, mask, stats, tile_a, tile_b, tile_x, tile_c, tile_d, tile_z, in_sem, z_sem, x_sem) = refs[len(layout) + 13 + n_far:]
     me, sample = sc[0], sc[1]
     lanes = pl.ds(pl.multiple_of(LANES * (me // 2), LANES), LANES)
-    out_norm = (norms[0], norms[1])
-    in_norm = (norms[2], norms[3])
-    att_norm = (norms[4], norms[5])
+    out_norm = norm_of(norms, 0)
+    in_norm = norm_of(norms, 1)
+    att_norm = norm_of(norms, 2)
     n_tiles = COLS // TILE
 
     for ref, (r, start) in zip(z_refs, layout):
@@ -100,8 +113,8 @@
         return [stats[first + n, pl.ds(base + i, 1), :] for n in range(2)]
 
     def flush(base):
-        a_s[:, pl.ds(base, TILE), :] = jnp.swapaxes(tile_a[:], 0, 1)
-        b_s[:, pl.ds(base, TILE), :] = jnp.swapaxes(tile_b[:], 0, 1)
+        a_s[:, pl.ds(base, TILE), :] = swap_major(tile_a[:])
+        b_s[:, pl.ds(base, TILE), :] = swap_major(tile_b[:])
 
     def export(t, start, outgoing, sem):
         r = (t * TILE // ROWS) ^ me
@@ -110,18 +123,21 @@
         half = pl.ds(pl.multiple_of(ROWS + TILE * (q % 2), TILE), TILE)
         side = pl.ds(pl.multiple_of(LANES * (q // 2), LANES), LANES)
         act = (lambda cp: cp.start()) if start else (lambda cp: cp.wait())
-        for k, dst in ((0, z2_own), (1, z2_par), (2, far2), (3, far3)):
-            plain = k < 2 or (last and k == 3)
-            if not (outgoing and plain):
-                @pl.when(r == k)
-                def _():
-                    if plain:
-                        src, to = tile_z.at[t % 2], dst.at[rows]
-                    elif outgoing:
-                        src, to = tile_c.at[t % 2, :, :, lanes], dst.at[half, :, side]
-                    else:
-                        src, to = tile_c.at[t % 2], dst.at[rows]
-                    act(pltpu.make_async_copy(src, to, sem.at[t % 2]))
+        wide, z_tile = tile_c.at[t % 2], tile_z.at[t % 2]
+        narrow = tile_c.at[t % 2, :, :, lanes]
+        jobs = [(r == 2, narrow, far2.at[half, :, side])] if outgoing else [
+            (r == 0, z_tile, z2_own.at[rows]), (r == 1, z_tile, z2_par.at[rows]), (r == 2, wide, far2.at[rows])]
+        if last:
+            jobs += [((r == 3) & (q == 0), narrow, far3[1]) if outgoing else ((r == 3) & (q == 0), wide, far3[0])]
+            if not outgoing:
+                rest = pl.ds(pl.multiple_of(jnp.maximum(q - 1, 0) * TILE, TILE), TILE)
+                jobs += [((r == 3) & (q > 0), z_tile, far3[2].at[rest])]
+        else:
+            jobs += [(r == 3, narrow, far3[0].at[half, :, side]) if outgoing else (r == 3, wide, far3[0].at[rows])]
+        for when, src, dst in jobs:
+            @pl.when(when)
+            def _():
+                act(pltpu.make_async_copy(src, dst, sem.at[t % 2]))
 
     @pl.loop(0, n_tiles)
     def _(v):
@@ -140,7 +156,7 @@
 
     @pl.loop(0, CH, unroll=4)
     def _(c):
-        x_s[c] = lax.dot_general(a_s[c], b_s[c], (((1,), (1,)), ((), ())), preferred_element_type=F32)
+        x_s[c] = contract(a_s[c], b_s[c], 1)
 
     @pl.loop(0, n_tiles)
     def _(t):
@@ -151,7 +167,7 @@
             export(t - 2, False, True, x_sem)
 
         x_norm_tile(x_s, tile_x, base, xgs.at[0], xgs.at[1])
-        tile_c[t % 2] = jnp.swapaxes(tile_x[:], 0, 1)
+        tile_c[t % 2] = swap_major(tile_x[:])
 
         def gate_and_update(i, _):
             normed = channel_norm(z_s[base + i], out_norm, recall(base, i, 0)).astype(BF16)
@@ -173,7 +189,7 @@
 
     @pl.loop(0, CH, unroll=4)
     def _(c):
-        x_s[c] = lax.dot_general(a_s[c], b_s[c], (((0,), (0,)), ((), ())), preferred_element_type=F32)
+        x_s[c] = contract(a_s[c], b_s[c], 0)
 
     @pl.loop(0, n_tiles)
     def _(t):
@@ -184,7 +200,7 @@
             export(t - 2, False, False, z_sem)
 
         x_norm_tile(x_s, tile_x, base, xgs.at[2], xgs.at[3])
-        tile_c[t % 2] = jnp.swapaxes(tile_x[:], 0, 1)
+        tile_c[t % 2] = swap_major(tile_x[:])
 
         def gate_and_update(i, _):
             normed = channel_norm(z_s[base + i], in_norm, recall(base, i, 2)).astype(BF16)
@@ -200,10 +216,10 @@
 
         staggered(TILE, gate_and_update, next_norm, bias_row)
         rows = pl.ds(pl.multiple_of(t * TILE % ROWS, TILE), TILE)
-        bias_out[t * TILE // ROWS, :, rows, :] = jnp.swapaxes(tile_d[:], 0, 1)[:4].astype(BF16)
+        bias_out[t * TILE // ROWS, :, rows, :] = swap_major(tile_d[:])[:4].astype(BF16)
         export(t, True, False, z_sem)
 
-    bias_to = ((far2, 0, 0), (far2, 1, 1), (far2, 3, 2)) if last else ((far2, 0, 0), (far3, 1, 0))
+    bias_to = ((far2, 0, 0), (far2, 1, 1), (far2, 3, 2)) if last else ((far2, 0, 0), (far3[0], 1, 0))
 
     def bias_copy(n):
         dst, block, place = bias_to[n]
@@ -220,23 +236,28 @@
 LANES = 128
 VM = pl.BlockSpec(memory_space=pltpu.VMEM)
 HB = pl.BlockSpec(memory_space=pl.ANY)
+SDS = jax.ShapeDtypeStruct
+AT_FIRST = lambda i, *_: (i, 0, 0, 0)
 SM = pl.BlockSpec(memory_space=pltpu.SMEM)
 PARAMS = pltpu.CompilerParams(vmem_limit_bytes=40 << 20, dimension_semantics=("arbitrary",))
 AB_TILE = pltpu.VMEM((TILE, CH, COLS), BF16)
 DMA2 = pltpu.SemaphoreType.DMA((2,))
 FAR_BIAS = ROWS + ROWS // 2
-FAR = jax.ShapeDtypeStruct((FAR_BIAS + 4, CH, COLS), BF16)
-FAR_LAST = jax.ShapeDtypeStruct((FAR_BIAS + 12, CH, COLS), BF16)
-ROW_WIDE = jax.ShapeDtypeStruct((ROWS, CH, COLS), F32)
+FAR = SDS((FAR_BIAS + 4, CH, COLS), BF16)
+TILE_FULL = SDS((TILE, CH, COLS), BF16)
+TILE_HALF = SDS((TILE, CH, LANES), BF16)
+AWAY = SDS((ROWS - TILE, CH, COLS), F32)
+FAR_LAST = SDS((FAR_BIAS + 12, CH, COLS), BF16)
+ROW_WIDE = SDS((ROWS, CH, COLS), F32)
 SAMPLE_BF = pltpu.VMEM((CH, COLS, COLS), BF16)
 
 
 def u_call(last, layout, sc, z_parts, masks, norms, xgs, w_ab, w_sq, w_bias):
     return pl.pallas_call(
         functools.partial(u_kernel, last, layout),
-        out_shape=(ROW_WIDE, ROW_WIDE, jax.ShapeDtypeStruct((4, 4, ROWS, COLS), BF16), *((FAR_LAST, ROW_WIDE) if last else (FAR, FAR))),
+        out_shape=(ROW_WIDE, ROW_WIDE, SDS((4, 4, ROWS, COLS), BF16), *((FAR_LAST, TILE_FULL, TILE_HALF, AWAY) if last else (FAR, FAR))),
         in_specs=[SM] + [HB] * len(layout) + [VM] * 9,
-        out_specs=(HB, HB, VM, HB, HB),
+        out_specs=(HB, HB, VM) + (HB,) * (4 if last else 2),
         scratch_shapes=[
             pltpu.VMEM((COLS, CH, COLS), F32), SAMPLE_BF, SAMPLE_BF,
             pltpu.VMEM((CH, COLS, COLS), F32), pltpu.VMEM((COLS, COLS), F32), pltpu.VMEM((4, COLS, COLS), F32), AB_TILE, AB_TILE, pltpu.VMEM((CH, TILE, COLS), BF16), pltpu.VMEM((2, TILE, CH, COLS), BF16),
@@ -249,7 +270,7 @@
 
 
 def l1_kernel(ids, z_in, mask_in, norms, w_ab, a_out, b_out, mask, tile_a, tile_b):
-    out_norm = (norms[0], norms[1])
+    out_norm = norm_of(norms, 0)
     mask[:] = mask_in[0].astype(F32)
 
     @pl.loop(0, ROWS // TILE)
@@ -259,14 +280,14 @@
             TILE,
             lambda i, _: mm(w_ab[0], (mask[pl.ds(base + i, 1), :] * channel_norm(z_in[0, base + i], out_norm)).astype(BF16)),
             lambda i, proj: ab_row(proj, tile_a, tile_b, i))
-        a_out[0, :, pl.ds(base, TILE), :] = jnp.swapaxes(tile_a[:], 0, 1)
-        b_out[0, :, pl.ds(base, TILE), :] = jnp.swapaxes(tile_b[:], 0, 1)
+        a_out[0, :, pl.ds(base, TILE), :] = swap_major(tile_a[:])
+        b_out[0, :, pl.ds(base, TILE), :] = swap_major(tile_b[:])
 
 
 def l1_call(ids, zt, mask, norms, w_ab):
     n = ids.shape[0]
-    ab = jax.ShapeDtypeStruct((n, CH, ROWS, COLS), BF16)
-    ab_spec = pl.BlockSpec((1, CH, ROWS, COLS), lambda i, ids: (i, 0, 0, 0))
+    ab = SDS((n, CH, ROWS, COLS), BF16)
+    ab_spec = pl.BlockSpec((1, CH, ROWS, COLS), AT_FIRST)
     return pl.pallas_call(
         l1_kernel,
         out_shape=(ab, ab),
@@ -288,28 +309,27 @@
     def _(c):
         for n in range(2):
             own, par = b_own[n, c].astype(F32), b_par[1 - n, c].astype(F32)
-            pair = jnp.concatenate([jnp.where(odd, par, own), jnp.where(odd, own, par)], axis=0).astype(BF16)
-            x_s[c, :, LANES * n:LANES * n + LANES] = lax.dot_general(
-                a_in[n, c], pair, (((1,), (1,)), ((), ())), preferred_element_type=F32)
+            pair = jnp.concatenate([jnp.where(odd, par, own), jnp.where(odd, own, par)]).astype(BF16)
+            x_s[c, :, LANES * n:LANES * n + LANES] = contract(a_in[n, c], pair, 1)
 
     @pl.loop(0, ROWS // TILE)
     def _(t):
         base = pl.multiple_of(TILE * t, TILE)
         x_norm_tile(x_s, tile_x, base, xgs.at[0], xgs.at[1])
-        both = jnp.swapaxes(tile_x[:], 0, 1)
+        both = swap_major(tile_x[:])
         for n in range(2):
             x_out[n, pl.ds(base, TILE)] = both[:, :, LANES * n:LANES * n + LANES]
 
 
 def l2_call(sc, a_all, b_own, b_par, xgs):
     n = a_all.shape[0]
-    ab_spec = pl.BlockSpec((2, CH, ROWS, COLS), lambda i: (i, 0, 0, 0))
+    ab_spec = pl.BlockSpec((2, CH, ROWS, COLS), AT_FIRST)
     return pl.pallas_call(
         l2_kernel,
         grid=(n // 2,),
-        out_shape=jax.ShapeDtypeStruct((n, ROWS, CH, LANES), BF16),
+        out_shape=SDS((n, ROWS, CH, LANES), BF16),
         in_specs=[SM, ab_spec, ab_spec, ab_spec, VM],
-        out_specs=pl.BlockSpec((2, ROWS, CH, LANES), lambda i: (i, 0, 0, 0)),
+        out_specs=pl.BlockSpec((2, ROWS, CH, LANES), AT_FIRST),
         scratch_shapes=[pltpu.VMEM((CH, ROWS, COLS), F32), pltpu.VMEM((CH, TILE, COLS), BF16)],
         compiler_params=PARAMS,
         name="near_product",
@@ -318,9 +338,9 @@
 
 def r_kernel(sc, z_in, x_near, x_far, xi, norms, w_sq, w_bias, z_out, bias_out, tile_d):
     first = sc[0] < 2
-    out_norm = (norms[0], norms[1])
-    in_norm = (norms[2], norms[3])
-    att_norm = (norms[4], norms[5])
+    out_norm = norm_of(norms, 0)
+    in_norm = norm_of(norms, 1)
+    att_norm = norm_of(norms, 2)
 
     def outgoing(i, _):
         near, far = x_near[0, i].astype(F32), x_far[i].astype(F32)
@@ -345,25 +365,26 @@
         tile_d[i] = mm(w_bias[:], normed)
 
     staggered(TILE, outgoing, norm_one, incoming, norm_two, bias_row)
-    bias_out[:] = jnp.swapaxes(tile_d[:], 0, 1)[:4].astype(BF16)
-
-
-def r_call(sc, zt, x_near, far, norms, w_sq, w_bias):
+    bias_out[:] = swap_major(tile_d[:])[:4].astype(BF16)
+
+
+def r_call(sc, zt, x_near, x_far, xi, norms, w_sq, w_bias):
+    steps = 1 if x_far.shape[0] == TILE else ROWS // TILE
+    far_map = (lambda i, sc: (i, 0, 0)) if steps == 1 else (lambda i, sc: (ROWS // TILE + i % 2, 0, i // 2))
+    row_map = lambda i, sc: (i, 0, 0)
     return pl.pallas_call(
         r_kernel,
-        out_shape=(ROW_WIDE, jax.ShapeDtypeStruct((4, ROWS, COLS), BF16)),
+        out_shape=(SDS((steps * TILE, CH, COLS), F32), SDS((4, steps * TILE, COLS), BF16)),
         grid_spec=pltpu.PrefetchScalarGridSpec(
-            num_scalar_prefetch=1, grid=(ROWS // TILE,),
+            num_scalar_prefetch=1, grid=(steps,),
             in_specs=[pl.BlockSpec((1, TILE, CH, COLS), lambda i, sc: (sc[1], i, 0, 0)),
                       pl.BlockSpec((1, TILE, CH, LANES), lambda i, sc: (sc[2], i, 0, 0)),
-                      pl.BlockSpec((TILE, CH, LANES), lambda i, sc: (ROWS // TILE + i % 2, 0, i // 2)),
-                      pl.BlockSpec((TILE, CH, COLS), lambda i, sc: (i, 0, 0)), VM, VM, VM],
-            out_specs=(pl.BlockSpec((TILE, CH, COLS), lambda i, sc: (i, 0, 0)),
-                       pl.BlockSpec((4, TILE, COLS), lambda i, sc: (0, i, 0))),
+                      pl.BlockSpec((TILE, CH, LANES), far_map), pl.BlockSpec((TILE, CH, COLS), row_map), VM, VM, VM],
+            out_specs=(pl.BlockSpec((TILE, CH, COLS), row_map), pl.BlockSpec((4, TILE, COLS), lambda i, sc: (0, i, 0))),
             scratch_shapes=[pltpu.VMEM((TILE, 8, COLS), F32)]),
         compiler_params=PARAMS,
         name="row_updates",
-    )(sc, zt, x_near, far, far, norms, w_sq, w_bias)
+    )(sc, zt, x_near, x_far, xi, norms, w_sq, w_bias)
 
 
 HEADS, HEAD = 4, 16
@@ -371,27 +392,28 @@
 CHUNK = 32
 SLOTS = 2
 STEPS = 6
-AWAY_FIRST = 48
-
-
-def attention_kernel(n, fresh, away, sc, *refs):
+AWAY_FIRST = 32
+
+
+def attention_kernel(sizes, fresh, away, sc, *refs):
+    n = len(sizes)
     z_refs, bias_refs = refs[:n], refs[n:2 * n]
     mask_in, norms, w_all, w_proj = refs[2 * n:2 * n + 4]
     rest = refs[2 * n + 4 + away + (not fresh):]
     mask_away, out_away = refs[2 * n + 4], rest[1:1 + 2 * away]
     (out, z_in, z_out, mask_i, mask, bias_rows, bias_t, q_s, k_s, v_s, g_s, vn_s, gn_s, keep_s, s_buf, e_buf, p_s,
      top_s, inv_s, o_s, m_sem, z_sem, o_sem) = rest[:1] + rest[1 + 2 * away:]
-    n_rows = n * ROWS
+    n_rows = sum(sizes)
 
     def z_copy(j):
-        return pltpu.make_async_copy(z_refs[j], z_in.at[pl.ds(ROWS * j, ROWS)], z_sem.at[j])
+        return pltpu.make_async_copy(z_refs[j], z_in.at[pl.ds(ROWS * j, sizes[j])], z_sem.at[j])
 
     def m_copy(j):
-        src = mask_away.at[0] if away and j == n - 1 else mask_in.at[sc[j]]
-        return pltpu.make_async_copy(src, mask_i.at[pl.ds(ROWS * j, ROWS)], m_sem.at[j])
+        src = mask_away.at[0] if away and j == n - 1 else mask_in.at[sc[j], pl.ds(0, sizes[j])]
+        return pltpu.make_async_copy(src, mask_i.at[pl.ds(ROWS * j, sizes[j])], m_sem.at[j])
 
     def o_copy(j):
-        return pltpu.make_async_copy(z_out.at[pl.ds(ROWS * j, ROWS)], out.at[sc[j]], o_sem.at[j])
+        return pltpu.make_async_copy(z_out.at[pl.ds(ROWS * j, sizes[j])], out.at[sc[j], pl.ds(0, sizes[j])], o_sem.at[j])
 
     def o_copies(j):
         if not (away and j == n - 1):
@@ -417,7 +439,7 @@
 
     def project(row, slot):
         row = jnp.minimum(row, n_rows - 1)
-        normed = channel_norm(z_in[row], (norms[0], norms[1])).astype(BF16)
+        normed = channel_norm(z_in[row], norm_of(norms, 0)).astype(BF16)
         proj = mm(w_all[:], normed)
         k_s[slot] = proj[CH:2 * CH].T.astype(BF16)
         q = proj[:CH].astype(BF16)
@@ -430,6 +452,9 @@
         row = jnp.minimum(row, n_rows - 1)
         keep_s[slot] = jnp.broadcast_to(mask[pl.ds(row, 1), :], (LANES, COLS)).T
 
+    def tall(line):
+        return jnp.concatenate([line] * (CHUNK // 8))
+
     def fold(part, op):
         out = part[:8]
         for n in range(1, part.shape[0] // 8):
@@ -449,8 +474,8 @@
         top, total, probs = None, None, []
         for c in range(COLS // CHUNK):
             rows = slice(CHUNK * c, CHUNK * c + CHUNK)
-            probs.append((e_buf[buf, rows] * jnp.concatenate([inv_s[buf]] * (CHUNK // 8), axis=0)).astype(BF16))
-            exps = jnp.exp(s_buf[prev, rows] - jnp.concatenate([top_s[prev]] * (CHUNK // 8), axis=0))
+            probs.append((e_buf[buf, rows] * tall(inv_s[buf])).astype(BF16))
+            exps = jnp.exp(s_buf[prev, rows] - tall(top_s[prev]))
             e_buf[prev, rows] = exps
             part = fold(exps, jnp.add)
             total = part if total is None else total + part
@@ -463,9 +488,9 @@
         top_s[buf] = jnp.broadcast_to(jnp.max(top, axis=0, keepdims=True), (8, COLS))
         inv_s[prev] = jnp.broadcast_to(1.0 / jnp.sum(total, axis=0, keepdims=True), (8, COLS))
         if defer:
-            p_s[:] = jnp.concatenate(probs, axis=0)
+            p_s[:] = jnp.concatenate(probs)
         else:
-            weigh(1 - slot if h < 2 else slot, (h - 2) % HEADS, jnp.concatenate(probs, axis=0))
+            weigh(1 - slot if h < 2 else slot, (h - 2) % HEADS, jnp.concatenate(probs))
 
     def finish(row, slot):
         gated = (g_s[slot] * o_s[slot]).astype(BF16)
@@ -511,10 +536,11 @@
 
 def attend(sc, z_parts, biases, mask, norms, w_all, w_proj, out, mask_away=None):
     n, fresh, away = len(z_parts), out is None, mask_away is not None
+    sizes = tuple(z.shape[0] for z in z_parts)
     args = (sc, *z_parts, *biases, mask, norms, w_all, w_proj) + ((mask_away,) if away else ()) + (() if fresh else (out,))
-    whole = jax.ShapeDtypeStruct((mask.shape[0], ROWS, CH, COLS), F32)
-    aways = [jax.ShapeDtypeStruct((k, CH, COLS), F32) for k in (AWAY_FIRST, ROWS - AWAY_FIRST)]
-    rows = n * ROWS
+    whole = SDS((mask.shape[0], ROWS, CH, COLS), F32)
+    aways = [SDS((k, CH, COLS), F32) for k in (AWAY_FIRST, AWAY.shape[0] - AWAY_FIRST)]
+    rows = sum(sizes)
     pair = pltpu.VMEM((SLOTS, CH, COLS), BF16)
     wide = pltpu.VMEM((SLOTS, CH, COLS), F32)
     square = pltpu.VMEM((SLOTS, COLS, COLS), F32)
@@ -522,7 +548,7 @@
     line = pltpu.VMEM((SLOTS, 8, COLS), F32)
     sems = pltpu.SemaphoreType.DMA((n,))
     return pl.pallas_call(
-        functools.partial(attention_kernel, n, fresh, away),
+        functools.partial(attention_kernel, sizes, fresh, away),
         out_shape=(whole, *aways) if away else whole,
         in_specs=[SM] + [HB] * n + [VM] * n + [HB] + [VM] * 3 + [HB] * (away + (not fresh)),
         out_specs=(HB, HB, HB) if away else HB,
@@ -551,7 +577,7 @@
     wide = lambda v: jnp.broadcast_to(v[:, None], (CH, COLS))
     deep = lambda v: jnp.broadcast_to(v[:, None, None], (CH, 8, 128))
     return ([wide(norm_gain), wide(norm_bias)], [deep(x_gain), deep(x_bias)],
-            half * jnp.concatenate([w_a.T, w_agate.T, w_b.T, w_bgate.T], axis=0), [half * w_gate.T, half * w_proj.T])
+            half * jnp.concatenate([w_a.T, w_agate.T, w_b.T, w_bgate.T]), [half * w_gate.T, half * w_proj.T])
 
 
 def solution(mesh):
@@ -573,7 +599,7 @@
                 got.append(exchange(send, r))
                 if t == 0 and stop == ROWS and r == 2:
                     mask_bf, weights = lax.optimization_barrier((mask_bf, weights, send))[:2]
-                    masks = [lax.dynamic_slice_in_dim(mask_bf, n_own * (me ^ k), n_own, axis=0) for k in range(4)]
+                    masks = [lax.dynamic_slice_in_dim(mask_bf, n_own * (me ^ k), n_own) for k in range(4)]
                     before = (*before, *masks)
                     masks = [exchange(m, k) if k else m for k, m in enumerate(masks)]
             arrived.append([zt, *got])
@@ -587,8 +613,8 @@
         xgs = jnp.stack(out_x + in_x)
         w_ab = jnp.stack([out_ab, in_ab])
         w_sq = jnp.stack(out_sq + in_sq)
-        w_bias8 = jnp.concatenate([w_bias.T, jnp.zeros((4, CH), BF16)], axis=0)
-        w_all = jnp.concatenate([w_q.T * jnp.bfloat16(HEAD ** -0.5), w_k.T, w_v.T, w_gate.T], axis=0)
+        w_bias8 = jnp.concatenate([w_bias.T, jnp.zeros((4, CH), BF16)])
+        w_all = jnp.concatenate([w_q.T * jnp.bfloat16(HEAD ** -0.5), w_k.T, w_v.T, w_gate.T])
         w_out = w_proj.T
         att_norms = norms[4:]
 
@@ -615,32 +641,33 @@
         held = []
         for t in range(n_own):
             last = t == n_own - 1
-            z_own, z_par, bias, far2, far3 = ordered(functools.partial(u_call, last, layouts[t]), [me, n_own * me + t],
-                                                     arrived[t], [m[t] for m in masks], norms, xgs, w_ab, w_sq, w_bias8)
+            z_own, z_par, bias, far2, *far3 = ordered(functools.partial(u_call, last, layouts[t]), [me, n_own * me + t],
+                                                      arrived[t], [m[t] for m in masks], norms, xgs, w_ab, w_sq, w_bias8)
             near = (n_own * (me ^ 1) + t, 0, exchange(z_par, 1), exchange(bias, 1))
-            held.append({2: exchange(far2, 2)})
             own = (n_own * me + t, 0, z_own, bias)
+            three = [exchange(v, 3) for v in (far3[:2] if last else far3)]
+            two = exchange(far2, 2)
+            held.append({2: (two, two), 3: (three[-1], three[0])})
             if last:
-                out, *away = attention([own, (0, 0, far3, bias)], out, masks[3][t][None].astype(jnp.int32))
+                out, *away = attention([own, (0, 0, far3[2], bias)], out, masks[3][t][None, TILE:].astype(jnp.int32))
                 away = [exchange(v, 3) for v in away]
             else:
-                held[t][3] = exchange(far3, 3)
                 out = attention([own, near], out)
         for t in range(n_own):
             last = t == n_own - 1
-            mine, z_two, biases = {}, {}, {}
-            for r in held[t]:
+            mine, z_two = {}, {}
+            for r in (2, 3):
                 z_two[r], bias_own = ordered(r_call, [me, n_own * (me ^ r) + t, far.index((t, r))], zt, x_near,
-                                             held[t][r], norms, w_sq, w_bias8)
-                mine[r] = [bias_own, *jnp.split(held[t][r][FAR_BIAS:], 3 if last else 1)]
+                                             *held[t][r], norms, w_sq, w_bias8)
+                mine[r] = [bias_own, *jnp.split(held[t][r][0][FAR_BIAS:], 3 if last else 1)]
+            par = exchange(jnp.stack(mine[2] + ([] if last else mine[3])), 1)
             if last:
-                biases[2] = jnp.stack([mine[2][k] for k in (0, 3, 1, 2)])
+                blocks = {2: [mine[2][k] for k in (0, 3, 1, 2)], 3: [par[k] for k in (3, 0, 2, 1)]}
             else:
-                par = exchange(jnp.stack(mine[3] + mine[2]), 1)
-                biases = {r: jnp.stack([mine[r][0], par[2 * r - 4], mine[r][1], par[2 * r - 3]]) for r in (2, 3)}
+                blocks = {2: [mine[2][0], par[2], mine[2][1], par[3]], 3: [mine[3][0], par[0], mine[3][1], par[1]]}
             out = attention(([] if t else [near]) + [
-                (n_own * (me ^ r) + t, me, z_two[r], biases[r]) for r in biases], out)
-        for v, start in zip(away, (0, AWAY_FIRST)):
+                (n_own * (me ^ r) + t, me, z_two[r], jnp.stack(blocks[r])) for r in (2, 3)], out)
+        for v, start in zip(away, (TILE, TILE + AWAY_FIRST)):
             out = lax.dynamic_update_slice(out, v[None], (n_own * (me ^ 3) + n_own - 1, start, 0, 0))
         return jnp.transpose(out, (0, 1, 3, 2))
 

time: 1270 us -> 1310 us (1.031)
  waiting for transfers between devices: 389 us -> 424 us
    ppermute x29 -> x32, waiting for transfers between devices: 389 us -> 424 us  [exchange(): return lax.ppermute(values, 'dap', [(i, i ^ r) for i in range(4)])]
    pallas_call x12 -> x13, Pallas kernels: 470 us -> 475 us  [the longest x6 391 us: attend(): pl.pallas_call(functools.partial(attention_kernel, sizes, fresh, away), o...]
  transfers between devices with their start and end apart: 29 -> 32, of which waited for: 11 -> 10; matrix products, arithmetic and copies ran while one was open for 4% -> 3% of each run, Pallas kernels for 52% -> 51%
where the time goes in v4:
time: 1310 us; the launch traced here: 1300 us
  Pallas kernels  781 us (60%)
  waiting for transfers between devices  424 us (32%)
  local copies, waits for them, and re-layouts  70.6 us (5%)
  starting transfers between devices  24.4 us (2%)
    ppermute x32, waiting for transfers between devices, exchange(): return lax.ppermute(values, 'dap', [(i, i ^ r) for i in range(4)])  424 us
    pallas_call x6, Pallas kernels, attend(): pl.pallas_call(functools.partial(attention_kernel, sizes, fresh, away), o...  391 us
    pallas_call x3, Pallas kernels, u_call(): pl.pallas_call(functools.partial(u_kernel, last, layout), out_shape=(ROW_...  277 us
    pallas_call x6, Pallas kernels, r_call(): pl.pallas_call(r_kernel, out_shape=(SDS((steps * TILE, CH, COLS), F32), S...  50.8 us
    squeeze x6, local copies, waits for them, and re-layouts, local_block(): lax.dynamic_slice(lax.optimization_barrier((zt, *before))[0], where, (1,...  34.3 us
    pallas_call x1, Pallas kernels, l2_call(): pl.pallas_call(l2_kernel, grid=(n // 2,), out_shape=SDS((n, ROWS, CH, LAN...  32.9 us
    pallas_call x1, Pallas kernels, l1_call(): pl.pallas_call(l1_kernel, out_shape=(ab, ab), grid_spec=pltpu.PrefetchSca...  28.7 us
  transfers between devices with their start and end apart: 32, of which 10 were waited for; matrix products, arithmetic and copies ran while one was open for 3% of the time, Pallas kernels for 51%

profile of v4, /device:TPU:0, one launch (start us, length us, event | category | flops | bytes accessed | tf_op | source)
XLA Modules:
  0.0 1304.8 jit_solution(10617638511968547661)
XLA Ops:
  0.0 1.1 dynamic-slice_bitcast_fusion.9
  1.3 4.4 dynamic-slice_bitcast_fusion.8
  7.3 28.7 %near_projections.1 = (bf16[6,64,64,256]{3,2,1,0:T(8,128)(2,1)S(1)}, bf16[6,64,64,256]{3,2,1,0:T(8,128)(2,1)}) custom-call(s32[6]{0:T(128)S(1)} %stack.247.ids, f32[12,64,64,256]{3,2,1,0:T(8,128)} %bitcast.150, s32[12,64,256]{2,1,0:T(8,128)S(1)} %copy-done.2, f32[6,64,256]{2,1,0:T(8,128)S(1)} %broadcast_dynamic-update-slice_fusion.norms.refs_9_.refs_8_, ...), custom_call_target="tpu_custom_call" | custom-call | tf_op jit(solution)/shard_map/near_projections/pallas_call | solution.py:291
  36.1 4.6 copy-done.6
  40.6 0.8 collective-permute-start
  41.5 4.6 dynamic-slice_bitcast_fusion.7
  46.2 4.7 dynamic-slice_bitcast_fusion.6
  50.9 2.6 collective-permute-start.3
  53.9 1.5 collective-permute-start.7
  57.1 0.7 dynamic-slice_bitcast_fusion.10
  57.8 167.5 %collective-permute-done.7 = bf16[3,64,256]{2,1,0:T(8,128)(2,1)S(1)} collective-permute-done((bf16[3,64,256]{2,1,0:T(8,128)(2,1)S(1)}, bf16[3,64,256]{2,1,0:T(8,128)(2,1)S(1)}, u32[]{:S(2)}, u32[]{:S(2)}) %collective-permute-start.7) | collective-permute-done | bytes 98336 | tf_op jit(solution)/shard_map/ppermute | solution.py:571
  225.3 2.3 collective-permute-start.6
  228.2 2.4 collective-permute-done.6
  231.2 0.7 collective-permute-done.5
  231.9 1.7 collective-permute-start.1
  235.6 32.9 %near_product.1.x_near = bf16[6,64,64,128]{3,2,1,0:T(8,128)(2,1)S(1)} custom-call(s32[1]{0:T(128)} %bitcast.2.sc, bf16[6,64,64,256]{3,2,1,0:T(8,128)(2,1)} %copy-done.6, bf16[6,64,64,256]{3,2,1,0:T(8,128)(2,1)} %get-tuple-element.102.b_own, bf16[6,64,64,256]{3,2,1,0:T(8,128)(2,1)} %collective-permute-done.b_par, ...), custom_call_target="tpu_custom_call" | custom-call | tf_op jit(solution)/shard_map/near_product/pallas_call | solution.py:327
  268.5 2.6 copy-done
  271.1 0.8 copy-done.22
  271.9 92.5 %pair_updates.3 = (f32[64,64,256]{2,1,0:T(8,128)}, f32[64,64,256]{2,1,0:T(8,128)}, bf16[4,4,64,256]{3,2,1,0:T(8,128)(2,1)}, bf16[100,64,256]{2,1,0:T(8,128)(2,1)}, bf16[100,64,256]{2,1,0:T(8,128)(2,1)}) custom-call(s32[2]{0:T(128)} %pad_add_fusion.10.sc, f32[12,64,64,256]{3,2,1,0:T(8,128)} %bitcast.153, f32[8,64,256]{2,1,0:T(8,128)} %copy-done.22, ...), custom_call_target="tpu_custom_call" | custom-call | tf_op jit(solution)/shard_map/pair_updates/pallas_call | solution.py:256
  364.4 9.7 dynamic-slice_bitcast_fusion.3
  374.1 1.8 collective-permute-start.11
  376.4 9.7 dynamic-slice_bitcast_fusion
  387.8 65.5 %triangle_attention.6.refs_8_ = f32[12,64,64,256]{3,2,1,0:T(8,128)} custom-call(s32[4]{0:T(128)S(1)} %get-tuple-element.119.sc, f32[64,64,256]{2,1,0:T(8,128)} %get-tuple-element.120.refs_0_, f32[64,64,256]{2,1,0:T(8,128)} %collective-permute-done.8.refs_1_, bf16[4,4,64,256]{3,2,1,0:T(8,128)(2,1)S(1)} %copy-done.16, ...), custom_call_target="tpu_custom_call" | custom-call | tf_op jit(solution)/shard_map/triangle_attention/pallas_call | solution.py:550
  453.2 14.6 %collective-permute-done.10.refs_1_ = f32[64,64,256]{2,1,0:T(8,128)} collective-permute-done((f32[64,64,256]{2,1,0:T(8,128)}, f32[64,64,256]{2,1,0:T(8,128)}, u32[]{:S(2)}, u32[]{:S(2)}) %collective-permute-start.10) | collective-permute-done | bytes 4194336 | tf_op jit(solution)/shard_map/ppermute | solution.py:571
  467.8 88.8 %collective-permute-done.11.refs_2_ = f32[64,64,256]{2,1,0:T(8,128)} collective-permute-done((f32[64,64,256]{2,1,0:T(8,128)}, f32[64,64,256]{2,1,0:T(8,128)}, u32[]{:S(2)}, u32[]{:S(2)}) %collective-permute-start.11) | collective-permute-done | bytes 4194336 | tf_op jit(solution)/shard_map/ppermute | solution.py:571
  556.7 92.5 %pair_updates.4 = (f32[64,64,256]{2,1,0:T(8,128)}, f32[64,64,256]{2,1,0:T(8,128)}, bf16[4,4,64,256]{3,2,1,0:T(8,128)(2,1)}, bf16[100,64,256]{2,1,0:T(8,128)(2,1)}, bf16[100,64,256]{2,1,0:T(8,128)(2,1)}) custom-call(s32[2]{0:T(128)} %pad_add_fusion.9.sc, f32[12,64,64,256]{3,2,1,0:T(8,128)} %bitcast.156, f32[64,64,256]{2,1,0:T(8,128)} %collective-permute-done.10.refs_1_, ...), custom_call_target="tpu_custom_call" | custom-call | tf_op jit(solution)/shard_map/pair_updates/pallas_call | solution.py:256
  649.2 0.8 collective-permute-start.13
  650.1 1.7 collective-permute-start.19
  652.3 11.5 collective-permute-done.14.refs_3_
  663.8 1.7 collective-permute-start.24
  666.2 1.0 copy-done.17
  667.2 65.3 %triangle_attention.7.refs_9_ = f32[12,64,64,256]{3,2,1,0:T(8,128)} custom-call(s32[4]{0:T(128)S(1)} %get-tuple-element.131.sc, f32[64,64,256]{2,1,0:T(8,128)} %get-tuple-element.132.refs_0_, f32[64,64,256]{2,1,0:T(8,128)} %copy-done.21, bf16[4,4,64,256]{3,2,1,0:T(8,128)(2,1)S(1)} %copy-done.17, ...), custom_call_target="tpu_custom_call", output_to_operand_aliasing={{}: (9, {})} | custom-call | tf_op jit(solution)/shard_map/triangle_attention/pallas_call | solution.py:550
  732.5 10.5 collective-permute-done.16.refs_2_
  743.0 92.2 %pair_updates.5 = (f32[64,64,256]{2,1,0:T(8,128)}, f32[64,64,256]{2,1,0:T(8,128)}, bf16[4,4,64,256]{3,2,1,0:T(8,128)(2,1)}, bf16[108,64,256]{2,1,0:T(8,128)(2,1)...) custom-call(s32[2]{0:T(128)} %pad_add_fusion.8.sc, ...), custom_call_target="tpu_custom_call" | custom-call | tf_op jit(solution)/shard_map/pair_updates/pallas_call | solution.py:256
  835.2 1.0 collective-permute-start.20
  836.3 2.0 collective-permute-start.26
  838.6 0.9 slice_bitcast_fusion.5
  839.5 44.3 %collective-permute-done.18.x_far.xi = bf16[100,64,256]{2,1,0:T(8,128)(2,1)} collective-permute-done((bf16[100,64,256]{2,1,0:T(8,128)(2,1)}, bf16[100,64,256]{2,1,0:T(8,128)(2,1)}, u32[]{:S(2)}, u32[]{:S(2)}) %collective-permute-start.18) | collective-permute-done | bytes 3276832 | tf_op jit(solution)/shard_map/ppermute | solution.py:571
  883.9 0.9 slice_bitcast_fusion.6
  884.8 1.0 copy-done.14
  885.8 56.6 %triangle_attention.8 = (f32[12,64,64,256]{3,2,1,0:T(8,128)}, f32[32,64,256]{2,1,0:T(8,128)}, f32[16,64,256]{2,1,0:T(8,128)S(1)}) custom-call(s32[4]{0:T(128)S(1)} %get-tuple-element.138.sc, f32[64,64,256]{2,1,0:T(8,128)} %get-tuple-element.139.refs_0_, f32[48,64,256]{2,1,0:T(8,128)} %get-tuple-element.137.refs_1_, ...), custom_call_target="tpu_custom_call", output_to_operand_aliasing={{0}: (10, {})} | custom-call | tf_op jit(solution)/shard_map/triangle_attention/pallas_call | solution.py:550
  942.5 3.1 copy-done.1
  945.7 9.1 row_updates.6
  954.8 1.9 copy-done.9
  956.7 9.8 row_updates.7
  966.6 1.9 copy-done.10
  968.7 0.9 slice_bitcast_fusion.3
  970.1 54.2 %collective-permute-done.23.x_far.xi = bf16[100,64,256]{2,1,0:T(8,128)(2,1)} collective-permute-done((bf16[100,64,256]{2,1,0:T(8,128)(2,1)}, bf16[100,64,256]{2,1,0:T(8,128)(2,1)}, u32[]{:S(2)}, u32[]{:S(2)}) %collective-permute-start.23) | collective-permute-done | bytes 3276832 | tf_op jit(solution)/shard_map/ppermute | solution.py:571
  1024.3 0.9 slice_bitcast_fusion.4
  1025.5 95.5 %triangle_attention.9.refs_8_ = f32[12,64,64,256]{3,2,1,0:T(8,128)} custom-call(s32[6]{0:T(128)S(1)} %stack.233.sc, f32[64,64,256]{2,1,0:T(8,128)} %collective-permute-done.20.refs_0_, f32[64,64,256]{2,1,0:T(8,128)} %copy-done.9, f32[64,64,256]{2,1,0:T(8,128)} %copy-done.10, ...), custom_call_target="tpu_custom_call", output_to_operand_aliasing={{}: (11, {})} | custom-call | tf_op jit(solution)/shard_map/triangle_attention/pallas_call | solution.py:550
  1121.1 9.2 row_updates.8
  1130.2 2.0 copy-done.11
  1132.2 9.1 row_updates.9
  1142.1 1.3 collective-permute-start.28
  1143.4 1.1 slice_bitcast_fusion.2
  1144.7 65.6 %triangle_attention.10.refs_8_ = f32[12,64,64,256]{3,2,1,0:T(8,128)} custom-call(s32[4]{0:T(128)S(1)} %add_add_fusion.1.sc, f32[64,64,256]{2,1,0:T(8,128)} %copy-done.11, f32[64,64,256]{2,1,0:T(8,128)} %copy-done.12, bf16[4,4,64,256]{3,2,1,0:T(8,128)(2,1)S(1)} %fusion.5.refs_2_, ...), custom_call_target="tpu_custom_call", output_to_operand_aliasing={{}: (9, {})} | custom-call | tf_op jit(solution)/shard_map/triangle_attention/pallas_call | solution.py:550
  1210.3 9.4 row_updates.10
  1219.8 2.0 copy-done.8
  1222.9 1.3 collective-permute-start.27
  1224.3 28.9 %collective-permute-done.27.x_far = bf16[16,64,128]{2,1,0:T(8,128)(2,1)S(1)} collective-permute-done((bf16[16,64,128]{2,1,0:T(8,128)(2,1)S(1)}, bf16[16,64,128]{2,1,0:T(8,128)(2,1)S(1)}, u32[]{:S(2)}, u32[]{:S(2)}) %collective-permute-start.27) | collective-permute-done | bytes 262176 | tf_op jit(solution)/shard_map/ppermute | solution.py:571
  1253.3 4.2 row_updates.11
  1257.6 42.9 %triangle_attention.11 = f32[12,64,64,256]{3,2,1,0:T(8,128)} custom-call(s32[4]{0:T(128)S(1)} %add_add_fusion.sc, f32[64,64,256]{2,1,0:T(8,128)} %copy-done.8, f32[16,64,256]{2,1,0:T(8,128)S(1)} %get-tuple-element.167.refs_1_, bf16[4,4,64,256]{3,2,1,0:T(8,128)(2,1)S(1)} %get-tuple-element.183.refs_2_, ...), custom_call_target="tpu_custom_call", output_to_operand_aliasing={{}: (9, {})} | custom-call | tf_op jit(solution)/shard_map/triangle_attention/pallas_call | solution.py:550
  1300.4 3.1 bitcast_dynamic-update-slice_fusion
  1303.6 1.0 bitcast_dynamic-update-slice_fusion.1
  (218 shorter events, 13.6 us)
Async XLA Ops:
  1.3 5.8 copy-start.40
  1.3 5.9 copy-start.41
  6.8 29.2 %copy-start.13 = (bf16[2,256,64]{2,1,0:T(8,128)(2,1)}, bf16[2,256,64]{2,1,0:T(8,128)(2,1)S(1)}, u32[]{:S(2)}) copy-start(bf16[2,256,64]{2,1,0:T(8,128)(2,1)S(1)} %pad_maximum_fusion.10.w_ab.refs_11_.refs_10_) | copy-start | bytes 196612
  7.2 28.8 %copy-start.3 = (f32[6,64,256]{2,1,0:T(8,128)}, f32[6,64,256]{2,1,0:T(8,128)S(1)}, u32[]{:S(2)}) copy-start(f32[6,64,256]{2,1,0:T(8,128)S(1)} %broadcast_dynamic-update-slice_fusion.norms.refs_9_.refs_8_) | copy-start | bytes 1179652
  40.6 195.0 %collective-permute-start = (bf16[6,64,64,256]{3,2,1,0:T(8,128)(2,1)}, bf16[6,64,64,256]{3,2,1,0:T(8,128)(2,1)}, u32[]{:S(2)}, u32[]{:S(2)}) collective-permute-start(bf16[6,64,64,256]{3,2,1,0:T(8,128)(2,1)} %get-tuple-element.102.b_own), channel_id=1, source_target_pairs={{0,1},{1,0},{2,3},{3,2},{4,5},{5,4},{6,7},{7,6}} | collective-permute-start | bytes 37748744 | tf_op jit(solution)/shard_map/ppermute | solution.py:571
  46.1 9.3 copy-start.31
  46.1 9.3 copy-start.32
  46.1 9.4 copy-start.33
  46.1 9.6 copy-start.34
  46.1 9.7 copy-start.42
  46.2 10.3 copy-start.47
  46.2 10.4 copy-start.48
  46.2 10.5 copy-start.49
  46.2 10.6 copy-start.50
  50.9 220.1 %collective-permute-start.4 = (f32[64,64,256]{2,1,0:T(8,128)}, f32[64,64,256]{2,1,0:T(8,128)}, u32[]{:S(2)}, u32[]{:S(2)}) collective-permute-start(f32[64,64,256]{2,1,0:T(8,128)} %dynamic-slice_bitcast_fusion.6), channel_id=1, source_target_pairs={{0,1},{1,0},{2,3},{3,2},{4,5},{5,4},{6,7},{7,6}} | collective-permute-start | bytes 12582920 | tf_op jit(solution)/shard_map/ppermute | solution.py:571
  50.9 220.1 %collective-permute-start.3 = (f32[64,64,256]{2,1,0:T(8,128)}, f32[64,64,256]{2,1,0:T(8,128)}, u32[]{:S(2)}, u32[]{:S(2)}) collective-permute-start(f32[64,64,256]{2,1,0:T(8,128)} %dynamic-slice_bitcast_fusion.7), channel_id=1, source_target_pairs={{0,3},{1,2},{2,1},{3,0},{4,7},{5,6},{6,5},{7,4}} | collective-permute-start | bytes 12582920 | tf_op jit(solution)/shard_map/ppermute | solution.py:571
  53.5 217.5 %collective-permute-start.2 = (f32[56,64,256]{2,1,0:T(8,128)}, f32[56,64,256]{2,1,0:T(8,128)}, u32[]{:S(2)}, u32[]{:S(2)}) collective-permute-start(f32[56,64,256]{2,1,0:T(8,128)} %dynamic-slice_bitcast_fusion.8), channel_id=1, source_target_pairs={{0,2},{1,3},{2,0},{3,1},{4,6},{5,7},{6,4},{7,5}} | collective-permute-start | bytes 11010056 | tf_op jit(solution)/shard_map/ppermute | solution.py:571
  53.9 171.4 %collective-permute-start.7 = (bf16[3,64,256]{2,1,0:T(8,128)(2,1)S(1)}, bf16[3,64,256]{2,1,0:T(8,128)(2,1)S(1)}, u32[]{:S(2)}, u32[]{:S(2)}) collective-permute-start(bf16[3,64,256]{2,1,0:T(8,128)(2,1)S(1)} %get-tuple-element.195), channel_id=1, source_target_pairs={{0,3},{1,2},{2,1},{3,0},{4,7},{5,6},{6,5},{7,4}} | collective-permute-start | bytes 294920 | tf_op jit(solution)/shard_map/ppermute | solution.py:571
  57.0 211.4 %copy-start.5 = (f32[4,64,8,128]{3,2,1,0:T(8,128)}, f32[4,64,8,128]{3,2,1,0:T(8,128)S(1)}, u32[]{:S(2)}) copy-start(f32[4,64,8,128]{3,2,1,0:T(8,128)S(1)} %pad_maximum_fusion.xgs.refs_10_.refs_9_) | copy-start | bytes 3145732
  225.3 5.4 collective-permute-start.6
  230.6 1.3 collective-permute-start.5
  231.9 39.1 %collective-permute-start.1 = (f32[8,64,256]{2,1,0:T(8,128)S(1)}, f32[8,64,256]{2,1,0:T(8,128)S(1)}, u32[]{:S(2)}, u32[]{:S(2)}) collective-permute-start(f32[8,64,256]{2,1,0:T(8,128)S(1)} %dynamic-slice_bitcast_fusion.9), channel_id=1, source_target_pairs={{0,2},{1,3},{2,0},{3,1},{4,6},{5,7},{6,4},{7,5}} | collective-permute-start | bytes 1572872 | tf_op jit(solution)/shard_map/ppermute | solution.py:571
  364.3 11.9 copy-start.16
  364.3 23.4 %collective-permute-start.8 = (f32[64,64,256]{2,1,0:T(8,128)}, f32[64,64,256]{2,1,0:T(8,128)}, u32[]{:S(2)}, u32[]{:S(2)}) collective-permute-start(f32[64,64,256]{2,1,0:T(8,128)} %get-tuple-element.121), channel_id=1, source_target_pairs={{0,1},{1,0},{2,3},{3,2},{4,5},{5,4},{6,7},{7,6}} | collective-permute-start | bytes 12582920 | tf_op jit(solution)/shard_map/ppermute | solution.py:571
  374.1 93.8 %collective-permute-start.10 = (f32[64,64,256]{2,1,0:T(8,128)}, f32[64,64,256]{2,1,0:T(8,128)}, u32[]{:S(2)}, u32[]{:S(2)}) collective-permute-start(f32[64,64,256]{2,1,0:T(8,128)} %get-tuple-element.174), channel_id=1, source_target_pairs={{0,2},{1,3},{2,0},{3,1},{4,6},{5,7},{6,4},{7,5}} | collective-permute-start | bytes 12582920 | tf_op jit(solution)/shard_map/ppermute | solution.py:571
  374.1 182.6 %collective-permute-start.11 = (f32[64,64,256]{2,1,0:T(8,128)}, f32[64,64,256]{2,1,0:T(8,128)}, u32[]{:S(2)}, u32[]{:S(2)}) collective-permute-start(f32[64,64,256]{2,1,0:T(8,128)} %get-tuple-element.173), channel_id=1, source_target_pairs={{0,3},{1,2},{2,1},{3,0},{4,7},{5,6},{6,5},{7,4}} | collective-permute-start | bytes 12582920 | tf_op jit(solution)/shard_map/ppermute | solution.py:571
  375.9 180.8 %collective-permute-start.12 = (f32[64,64,256]{2,1,0:T(8,128)}, f32[64,64,256]{2,1,0:T(8,128)}, u32[]{:S(2)}, u32[]{:S(2)}) collective-permute-start(f32[64,64,256]{2,1,0:T(8,128)} %get-tuple-element.172), channel_id=1, source_target_pairs={{0,1},{1,0},{2,3},{3,2},{4,5},{5,4},{6,7},{7,6}} | collective-permute-start | bytes 12582920 | tf_op jit(solution)/shard_map/ppermute | solution.py:571
  376.2 9.9 collective-permute-start.9
  376.4 10.0 copy-start.35
  376.4 10.1 copy-start.36
  376.4 10.2 copy-start.37
  376.4 10.3 copy-start.38
  376.4 10.4 copy-start.39
  386.1 265.7 %collective-permute-start.15 = (f32[64,64,256]{2,1,0:T(8,128)}, f32[64,64,256]{2,1,0:T(8,128)}, u32[]{:S(2)}, u32[]{:S(2)}) collective-permute-start(f32[64,64,256]{2,1,0:T(8,128)} %get-tuple-element.171), channel_id=1, source_target_pairs={{0,2},{1,3},{2,0},{3,1},{4,6},{5,7},{6,4},{7,5}} | collective-permute-start | bytes 12582920 | tf_op jit(solution)/shard_map/ppermute | solution.py:571
  649.2 14.6 %collective-permute-start.13 = (f32[64,64,256]{2,1,0:T(8,128)}, f32[64,64,256]{2,1,0:T(8,128)S(1)}, u32[]{:S(2)}, u32[]{:S(2)}) collective-permute-start(f32[64,64,256]{2,1,0:T(8,128)} %get-tuple-element.133), channel_id=1, source_target_pairs={{0,1},{1,0},{2,3},{3,2},{4,5},{5,4},{6,7},{7,6}} | collective-permute-start | bytes 12582920 | tf_op jit(solution)/shard_map/ppermute | solution.py:571
  650.0 93.0 %collective-permute-start.16 = (f32[64,64,256]{2,1,0:T(8,128)}, f32[64,64,256]{2,1,0:T(8,128)}, u32[]{:S(2)}, u32[]{:S(2)}) collective-permute-start(f32[64,64,256]{2,1,0:T(8,128)} %get-tuple-element.170), channel_id=1, source_target_pairs={{0,3},{1,2},{2,1},{3,0},{4,7},{5,6},{6,5},{7,4}} | collective-permute-start | bytes 12582920 | tf_op jit(solution)/shard_map/ppermute | solution.py:571
  650.0 93.0 %collective-permute-start.17 = (f32[64,64,256]{2,1,0:T(8,128)}, f32[64,64,256]{2,1,0:T(8,128)}, u32[]{:S(2)}, u32[]{:S(2)}) collective-permute-start(f32[64,64,256]{2,1,0:T(8,128)} %get-tuple-element.169), channel_id=1, source_target_pairs={{0,1},{1,0},{2,3},{3,2},{4,5},{5,4},{6,7},{7,6}} | collective-permute-start | bytes 12582920 | tf_op jit(solution)/shard_map/ppermute | solution.py:571
  650.1 186.1 %collective-permute-start.19 = (bf16[100,64,256]{2,1,0:T(8,128)(2,1)}, bf16[100,64,256]{2,1,0:T(8,128)(2,1)}, u32[]{:S(2)}, u32[]{:S(2)}) collective-permute-start(bf16[100,64,256]{2,1,0:T(8,128)(2,1)} %get-tuple-element.118), channel_id=1, source_target_pairs={{0,3},{1,2},{2,1},{3,0},{4,7},{5,6},{6,5},{7,4}} | collective-permute-start | bytes 9830408 | tf_op jit(solution)/shard_map/ppermute | solution.py:571
  651.8 12.0 collective-permute-start.14
  663.8 220.1 %collective-permute-start.18 = (bf16[100,64,256]{2,1,0:T(8,128)(2,1)}, bf16[100,64,256]{2,1,0:T(8,128)(2,1)}, u32[]{:S(2)}, u32[]{:S(2)}) collective-permute-start(bf16[100,64,256]{2,1,0:T(8,128)(2,1)} %get-tuple-element.143), channel_id=1, source_target_pairs={{0,2},{1,3},{2,0},{3,1},{4,6},{5,7},{6,4},{7,5}} | collective-permute-start | bytes 9830408 | tf_op jit(solution)/shard_map/ppermute | solution.py:571
  663.8 304.9 %collective-permute-start.24 = (bf16[100,64,256]{2,1,0:T(8,128)(2,1)}, bf16[100,64,256]{2,1,0:T(8,128)(2,1)}, u32[]{:S(2)}, u32[]{:S(2)}) collective-permute-start(bf16[100,64,256]{2,1,0:T(8,128)(2,1)} %get-tuple-element.130), channel_id=1, source_target_pairs={{0,3},{1,2},{2,1},{3,0},{4,7},{5,6},{6,5},{7,4}} | collective-permute-start | bytes 9830408 | tf_op jit(solution)/shard_map/ppermute | solution.py:571
  835.2 190.3 %collective-permute-start.20 = (f32[64,64,256]{2,1,0:T(8,128)}, f32[64,64,256]{2,1,0:T(8,128)}, u32[]{:S(2)}, u32[]{:S(2)}) collective-permute-start(f32[64,64,256]{2,1,0:T(8,128)} %get-tuple-element.148), channel_id=1, source_target_pairs={{0,1},{1,0},{2,3},{3,2},{4,5},{5,4},{6,7},{7,6}} | collective-permute-start | bytes 12582920 | tf_op jit(solution)/shard_map/ppermute | solution.py:571
  836.2 188.1 %collective-permute-start.23 = (bf16[100,64,256]{2,1,0:T(8,128)(2,1)}, bf16[100,64,256]{2,1,0:T(8,128)(2,1)}, u32[]{:S(2)}, u32[]{:S(2)}) collective-permute-start(bf16[100,64,256]{2,1,0:T(8,128)(2,1)} %get-tuple-element.153), channel_id=1, source_target_pairs={{0,2},{1,3},{2,0},{3,1},{4,6},{5,7},{6,4},{7,5}} | collective-permute-start | bytes 9830408 | tf_op jit(solution)/shard_map/ppermute | solution.py:571
  836.3 307.1 %collective-permute-start.26 = (bf16[108,64,256]{2,1,0:T(8,128)(2,1)}, bf16[108,64,256]{2,1,0:T(8,128)(2,1)}, u32[]{:S(2)}, u32[]{:S(2)}) collective-permute-start(bf16[108,64,256]{2,1,0:T(8,128)(2,1)} %get-tuple-element.161), channel_id=1, source_target_pairs={{0,2},{1,3},{2,0},{3,1},{4,6},{5,7},{6,4},{7,5}} | collective-permute-start | bytes 10616840 | tf_op jit(solution)/shard_map/ppermute | solution.py:571
  885.8 56.6 %copy-start.4 = (f32[6,64,256]{2,1,0:T(8,128)S(1)}, f32[6,64,256]{2,1,0:T(8,128)}, u32[]{:S(2)}) copy-start(f32[6,64,256]{2,1,0:T(8,128)} %copy-done.3) | copy-start | bytes 1179652
  885.8 56.7 %copy-start.7 = (bf16[4,64,64]{2,1,0:T(8,128)(2,1)S(1)}, bf16[4,64,64]{2,1,0:T(8,128)(2,1)}, u32[]{:S(2)}) copy-start(bf16[4,64,64]{2,1,0:T(8,128)(2,1)} %pad_maximum_fusion.12.refs_12_.refs_11_.w_sq) | copy-start | bytes 98308
  885.8 56.7 %copy-start.18 = (bf16[8,64]{1,0:T(8,128)(2,1)S(1)}, bf16[8,64]{1,0:T(8,128)(2,1)}, u32[]{:S(2)}) copy-start(bf16[8,64]{1,0:T(8,128)(2,1)} %concatenate.53.refs_13_.refs_12_.w_bias) | copy-start | bytes 3076
  942.5 12.3 copy-start.19
  956.7 12.9 copy-start.15
  956.7 164.3 %slice-start = ((s8[6291456]{0:T(1024)(128)(4,1)}), s8[4194304]{0:T(1024)(128)(4,1)S(1)}, s32[]{:S(2)}) async-start(s8[6291456]{0:T(1024)(128)(4,1)} %bitcast.129), calls=%async_computation | async-start | bytes 8388608
  968.6 56.7 %collective-permute-start.22 = (bf16[4,4,64,256]{3,2,1,0:T(8,128)(2,1)S(1)}, bf16[4,4,64,256]{3,2,1,0:T(8,128)(2,1)S(1)}, u32[]{:S(2)}, u32[]{:S(2)}) collective-permute-start(bf16[4,4,64,256]{3,2,1,0:T(8,128)(2,1)S(1)} %fusion.11), channel_id=1, source_target_pairs={{0,1},{1,0},{2,3},{3,2},{4,5},{5,4},{6,7},{7,6}} | collective-permute-start | bytes 1572872 | tf_op jit(solution)/shard_map/ppermute | solution.py:571
  969.6 55.9 %collective-permute-start.21 = (bf16[4,4,64,256]{3,2,1,0:T(8,128)(2,1)S(1)}, bf16[4,4,64,256]{3,2,1,0:T(8,128)(2,1)S(1)}, u32[]{:S(2)}, u32[]{:S(2)}) collective-permute-start(bf16[4,4,64,256]{3,2,1,0:T(8,128)(2,1)S(1)} %copy-done.15), channel_id=1, source_target_pairs={{0,1},{1,0},{2,3},{3,2},{4,5},{5,4},{6,7},{7,6}} | collective-permute-start | bytes 1572872 | tf_op jit(solution)/shard_map/ppermute | solution.py:571
  1025.2 275.2 %collective-permute-start.30 = (f32[32,64,256]{2,1,0:T(8,128)}, f32[32,64,256]{2,1,0:T(8,128)}, u32[]{:S(2)}, u32[]{:S(2)}) collective-permute-start(f32[32,64,256]{2,1,0:T(8,128)} %get-tuple-element.168), channel_id=1, source_target_pairs={{0,3},{1,2},{2,1},{3,0},{4,7},{5,6},{6,5},{7,4}} | collective-permute-start | bytes 6291464 | tf_op jit(solution)/shard_map/ppermute | solution.py:571
  1025.5 95.5 %slice-start.1 = ((s8[6291456]{0:T(1024)(128)(4,1)}), s8[2097152]{0:T(1024)(128)(4,1)S(1)}, s32[]{:S(2)}) async-start(s8[6291456]{0:T(1024)(128)(4,1)} %bitcast.129), calls=%async_computation.1 | async-start | bytes 4194304
  1132.2 9.9 copy-start.51
  1141.5 3.0 collective-permute-start.25
  1142.1 111.2 %collective-permute-start.28 = (bf16[16,64,256]{2,1,0:T(8,128)(2,1)S(1)}, bf16[16,64,256]{2,1,0:T(8,128)(2,1)S(1)}, u32[]{:S(2)}, u32[]{:S(2)}) collective-permute-start(bf16[16,64,256]{2,1,0:T(8,128)(2,1)S(1)} %copy-done.51), channel_id=1, source_target_pairs={{0,3},{1,2},{2,1},{3,0},{4,7},{5,6},{6,5},{7,4}} | collective-permute-start | bytes 1572872 | tf_op jit(solution)/shard_map/ppermute | solution.py:571
  1144.7 108.6 %slice-start.2 = ((s8[6291456]{0:T(1024)(128)(4,1)}), s8[4194304]{0:T(1024)(128)(4,1)S(1)}, s32[]{:S(2)}) async-start(s8[6291456]{0:T(1024)(128)(4,1)} %bitcast.131), calls=%async_computation.2 | async-start | bytes 8388608
  1144.7 108.6 %slice-start.3 = ((s8[6291456]{0:T(1024)(128)(4,1)}), s8[2097152]{0:T(1024)(128)(4,1)S(1)}, s32[]{:S(2)}) async-start(s8[6291456]{0:T(1024)(128)(4,1)} %bitcast.131), calls=%async_computation.3 | async-start | bytes 4194304
  1210.3 12.1 copy-start.20
  1210.3 12.6 copy-start.52
  1221.9 35.6 %collective-permute-start.29 = (bf16[4,4,64,256]{3,2,1,0:T(8,128)(2,1)S(1)}, bf16[4,4,64,256]{3,2,1,0:T(8,128)(2,1)S(1)}, u32[]{:S(2)}, u32[]{:S(2)}) collective-permute-start(bf16[4,4,64,256]{3,2,1,0:T(8,128)(2,1)S(1)} %get-tuple-element.182), channel_id=1, source_target_pairs={{0,1},{1,0},{2,3},{3,2},{4,5},{5,4},{6,7},{7,6}} | collective-permute-start | bytes 1572872 | tf_op jit(solution)/shard_map/ppermute | solution.py:571
  1222.4 81.2 %collective-permute-start.31 = (f32[16,64,256]{2,1,0:T(8,128)S(1)}, f32[16,64,256]{2,1,0:T(8,128)S(1)}, u32[]{:S(2)}, u32[]{:S(2)}) collective-permute-start(f32[16,64,256]{2,1,0:T(8,128)S(1)} %copy-done.20), channel_id=1, source_target_pairs={{0,3},{1,2},{2,1},{3,0},{4,7},{5,6},{6,5},{7,4}} | collective-permute-start | bytes 3145736 | tf_op jit(solution)/shard_map/ppermute | solution.py:571
  1222.9 30.4 %collective-permute-start.27 = (bf16[16,64,128]{2,1,0:T(8,128)(2,1)S(1)}, bf16[16,64,128]{2,1,0:T(8,128)(2,1)S(1)}, u32[]{:S(2)}, u32[]{:S(2)}) collective-permute-start(bf16[16,64,128]{2,1,0:T(8,128)(2,1)S(1)} %copy-done.52), channel_id=1, source_target_pairs={{0,3},{1,2},{2,1},{3,0},{4,7},{5,6},{6,5},{7,4}} | collective-permute-start | bytes 786440 | tf_op jit(solution)/shard_map/ppermute | solution.py:571
  (25 other events, 94.9 us)
